TPU v7x, 32 devices: a whole 2x2x4 slice. The times are simulated.
32 devices in a mesh: seq: 4 (over z), shard: 8 (over y, x, core).
Axes of the slice: x: 2, y: 2, z: 4, core: 2. Of those that a mesh axis runs over, the one named last changes fastest.
Arguments:
- inputs: bfloat16 [4096, 1024], P(('seq', 'shard')), may hold values from -16 to 16
- positions: int32 [4096], P(('seq', 'shard')), may hold values from 0 to 8191
- segments: int32 [4096], replicated, may hold values from 0 to 7, never falling along the last dimension, each value on 1 to 1024 neighbouring positions
- pos_table: bfloat16 [8192, 1024], P('shard'), may hold values from -3 to 3
- w_qkv: bfloat16 [1024, 3072], P('shard'), may hold values from -0.1875 to 0.1875
- b_query: bfloat16 [1024], P('shard'), may hold values from -3 to 3
- b_value: bfloat16 [1024], P('shard'), may hold values from -3 to 3
- w_out: bfloat16 [1024, 1024], P('shard'), may hold values from -3 to 3
- b_out: bfloat16 [1024], P('shard'), may hold values from -3 to 3
- ln1_gain: bfloat16 [1024], P('shard'), may hold values from 0.5 to 1.5
- ln1_bias: bfloat16 [1024], P('shard'), may hold values from -2 to 2
- w_up: bfloat16 [1024, 4096], P('shard'), may hold values from -0.1875 to 0.1875
- b_up: bfloat16 [4096], P('shard'), may hold values from -3 to 3
- w_down: bfloat16 [4096, 1024], P('shard'), may hold values from -0.09375 to 0.09375
- b_down: bfloat16 [1024], P('shard'), may hold values from -3 to 3
- ln2_gain: bfloat16 [1024], P('shard'), may hold values from 0.5 to 1.5
- ln2_bias: bfloat16 [1024], P('shard'), may hold values from -2 to 2
- cotangent: bfloat16 [4096, 1024], P(('seq', 'shard')), may hold values from -6 to 6
Outputs:
- result: bfloat16 [4096, 1024], P(('seq', 'shard'))
- grad_inputs: bfloat16 [4096, 1024], P(('seq', 'shard'))
- grad_pos_table: float32 [8192, 1024], P('shard')
- grad_w_qkv: float32 [1024, 3072], P('shard')
- grad_b_query: float32 [1024], P('shard')
- grad_b_value: float32 [1024], P('shard')
- grad_w_out: float32 [1024, 1024], P('shard')
- grad_b_out: float32 [1024], P('shard')
- grad_ln1_gain: float32 [1024], P('shard')
- grad_ln1_bias: float32 [1024], P('shard')
- grad_w_up: float32 [1024, 4096], P('shard')
- grad_b_up: float32 [4096], P('shard')
- grad_w_down: float32 [4096, 1024], P('shard')
- grad_b_down: float32 [1024], P('shard')
- grad_ln2_gain: float32 [1024], P('shard')
- grad_ln2_bias: float32 [1024], P('shard')
Inputs may be any that keep to these rules, and one draw needn't show every extreme that they name: `segments`: never falls along the tokens; every id from 0 to 7 holds 1 to 1024 consecutive tokens, one id exactly 1024.
All inputs are finite; a program needn't handle non-finite values.
Results may differ from a plain program's by a relative error of at most 0.017.
Values may be sent and summed in bfloat16 or wider, within the bound.
A program may use at most 384 MiB of HBM per device.

v0:
```python
import math

import jax
import jax.numpy as jnp
from jax import lax
from jax.sharding import PartitionSpec as P

HEADS = 16
HEAD_DIM = 64


score_scale = 0.125
neg_large = -1e30
epsilon = 1e-06
root_half = 0.7071067811865476
inv_root_two_pi = 0.3989422804014327


def layer_normalize(summed):
    center = summed - jnp.mean(summed, axis=-1, keepdims=True)
    inverse = lax.rsqrt(jnp.mean(center * center, axis=-1, keepdims=True) + epsilon)
    return (center * inverse, inverse)


def normalize_back(grad_normed, normed, inverse):
    first_mean = jnp.mean(grad_normed, axis=-1, keepdims=True)
    second_mean = jnp.mean(grad_normed * normed, axis=-1, keepdims=True)
    return inverse * (grad_normed - first_mean - normed * second_mean)


def gelu_value(pre_act):
    return 0.5 * pre_act * (1.0 + jax.scipy.special.erf(pre_act * root_half))


def gelu_slope(pre_act):
    return (
        0.5 * (1.0 + jax.scipy.special.erf(pre_act * root_half))
        + pre_act * jnp.exp(-0.5 * pre_act * pre_act) * inv_root_two_pi
    )


def contract_rows(left_side, right_side):
    return lax.dot_general(
        left_side, right_side, (((0,), (0,)), ((), ())), preferred_element_type=jnp.float32
    )


def local(
    inputs,
    positions,
    segments,
    pos_table,
    w_qkv,
    b_query,
    b_value,
    w_out,
    b_out,
    ln1_gain,
    ln1_bias,
    w_up,
    b_up,
    w_down,
    b_down,
    ln2_gain,
    ln2_bias,
    cotangent,
):
    seq_count = lax.axis_size("seq")
    shard_count = lax.axis_size("shard")
    shard_index = lax.axis_index("shard")
    local_tokens = inputs.shape[0]
    width = inputs.shape[1]
    heads_here = HEADS // seq_count
    head_cols = heads_here * HEAD_DIM
    query_count = seq_count * local_tokens
    key_count = shard_count * query_count
    gathered = (
        lax.all_gather(pos_table, "shard", axis=0, tiled=True),
        lax.all_gather(w_qkv, "shard", axis=0, tiled=True),
        lax.all_gather(w_out, "shard", axis=0, tiled=True),
        lax.all_gather(w_up, "shard", axis=0, tiled=True),
        lax.all_gather(w_down, "shard", axis=0, tiled=True),
        lax.all_gather(b_query, "shard", axis=0, tiled=True),
        lax.all_gather(b_value, "shard", axis=0, tiled=True),
        lax.all_gather(b_out, "shard", axis=0, tiled=True),
        lax.all_gather(ln1_gain, "shard", axis=0, tiled=True),
        lax.all_gather(ln1_bias, "shard", axis=0, tiled=True),
        lax.all_gather(b_up, "shard", axis=0, tiled=True),
        lax.all_gather(b_down, "shard", axis=0, tiled=True),
        lax.all_gather(ln2_gain, "shard", axis=0, tiled=True),
        lax.all_gather(ln2_bias, "shard", axis=0, tiled=True),
    )
    (
        table_all,
        w_qkv_all,
        w_out_all,
        w_up_all,
        w_down_all,
        bias_query,
        bias_value,
        bias_out,
        gain_one,
        shift_one,
        bias_up,
        bias_down,
        gain_two,
        shift_two,
    ) = gathered
    hidden = inputs.astype(jnp.float32) + jnp.take(table_all, positions, axis=0).astype(jnp.float32)
    hidden_bf = hidden.astype(jnp.bfloat16)
    projected = jnp.dot(hidden_bf, w_qkv_all, preferred_element_type=jnp.float32)
    query_rows = (projected[:, :width] + bias_query.astype(jnp.float32)).astype(jnp.bfloat16)
    key_rows = projected[:, width : 2 * width].astype(jnp.bfloat16)
    value_rows = (projected[:, 2 * width :] + bias_value.astype(jnp.float32)).astype(jnp.bfloat16)
    query_heads, key_heads, value_heads = (
        lax.all_to_all(query_rows, "seq", split_axis=1, concat_axis=0, tiled=True),
        lax.all_to_all(key_rows, "seq", split_axis=1, concat_axis=0, tiled=True),
        lax.all_to_all(value_rows, "seq", split_axis=1, concat_axis=0, tiled=True),
    )
    seg_keys = (
        segments.reshape(seq_count, shard_count, local_tokens).transpose(1, 0, 2).reshape(key_count)
    )
    seg_query = lax.dynamic_slice_in_dim(seg_keys, shard_index * query_count, query_count)
    query_three = query_heads.reshape(query_count, heads_here, HEAD_DIM)

    def split_blocks(piece):
        key_piece, value_piece = piece
        piece_rows = key_piece.shape[0]
        block_rows = math.gcd(piece_rows, query_count)
        block_count = piece_rows // block_rows
        seg_piece = seg_keys.reshape(block_count, block_rows)
        offsets = jnp.arange(block_count, dtype=jnp.int32) * block_rows
        key_blocks = key_piece.reshape(block_count, block_rows, heads_here, HEAD_DIM)
        value_blocks = value_piece.reshape(block_count, block_rows, heads_here, HEAD_DIM)
        return (key_blocks, value_blocks, seg_piece, offsets)

    def block_scores(key_block, seg_block):
        scores = (
            jnp.einsum("qhd,khd->hqk", query_three, key_block, preferred_element_type=jnp.float32)
            * score_scale
        )
        same_seq = (seg_query[:, None] == seg_block[None, :])[None]
        return (scores, same_seq)

    init_state = (
        jnp.full((heads_here, query_count), neg_large, jnp.float32),
        jnp.zeros((heads_here, query_count), jnp.float32),
        jnp.zeros((query_count, heads_here, HEAD_DIM), jnp.float32),
    )
    fold_state = init_state

    def forward_one_block(inner_state, block_item):
        run_max, run_total, run_acc = inner_state
        key_block, value_block, seg_block, offset = block_item
        scores, same_seq = block_scores(key_block, seg_block)
        scores = jnp.where(same_seq, scores, neg_large)
        new_max = jnp.maximum(run_max, jnp.max(scores, axis=2))
        rescale = jnp.exp(run_max - new_max)
        exp_scores = jnp.where(same_seq, jnp.exp(scores - new_max[:, :, None]), 0.0)
        run_total = run_total * rescale + jnp.sum(exp_scores, axis=2)
        update = jnp.einsum(
            "hqk,khd->qhd",
            exp_scores.astype(jnp.bfloat16),
            value_block,
            preferred_element_type=jnp.float32,
        )
        run_acc = run_acc * jnp.transpose(rescale)[:, :, None] + update
        return ((new_max, run_total, run_acc), None)

    fold_state, unused = lax.scan(
        forward_one_block,
        fold_state,
        split_blocks(
            (
                lax.all_gather(key_heads, "shard", axis=0, tiled=True),
                lax.all_gather(value_heads, "shard", axis=0, tiled=True),
            )
        ),
    )
    run_max, run_total, run_acc = fold_state
    attended_heads = (
        (run_acc / jnp.transpose(run_total)[:, :, None])
        .reshape(query_count, head_cols)
        .astype(jnp.bfloat16)
    )
    log_total = run_max + jnp.log(run_total)
    attended = lax.all_to_all(attended_heads, "seq", split_axis=0, concat_axis=1, tiled=True)
    first_sum = (
        hidden
        + jnp.dot(attended, w_out_all, preferred_element_type=jnp.float32)
        + bias_out.astype(jnp.float32)
    )
    normed_one, inverse_one = layer_normalize(first_sum)
    first_norm = normed_one * gain_one.astype(jnp.float32) + shift_one.astype(jnp.float32)
    first_bf = first_norm.astype(jnp.bfloat16)
    up_pre = jnp.dot(first_bf, w_up_all, preferred_element_type=jnp.float32) + bias_up.astype(
        jnp.float32
    )
    activated = gelu_value(up_pre).astype(jnp.bfloat16)
    second_sum = (
        first_norm
        + jnp.dot(activated, w_down_all, preferred_element_type=jnp.float32)
        + bias_down.astype(jnp.float32)
    )
    normed_two, inverse_two = layer_normalize(second_sum)
    result = (normed_two * gain_two.astype(jnp.float32) + shift_two.astype(jnp.float32)).astype(
        jnp.bfloat16
    )
    back_qkv, back_out, back_up, back_down, back_gain_one, back_gain_two = (
        lax.all_gather(w_qkv, "shard", axis=0, tiled=True),
        lax.all_gather(w_out, "shard", axis=0, tiled=True),
        lax.all_gather(w_up, "shard", axis=0, tiled=True),
        lax.all_gather(w_down, "shard", axis=0, tiled=True),
        lax.all_gather(ln1_gain, "shard", axis=0, tiled=True),
        lax.all_gather(ln2_gain, "shard", axis=0, tiled=True),
    )
    grad_rows = cotangent.astype(jnp.float32)
    grad_ln2_gain = jnp.sum(grad_rows * normed_two, axis=0)
    grad_ln2_bias = jnp.sum(grad_rows, axis=0)
    d_second = normalize_back(
        grad_rows * back_gain_two.astype(jnp.float32), normed_two, inverse_two
    )
    grad_b_down = jnp.sum(d_second, axis=0)
    d_second_bf = d_second.astype(jnp.bfloat16)
    d_up = jnp.dot(d_second_bf, back_down.T, preferred_element_type=jnp.float32) * gelu_slope(
        up_pre
    )
    grad_b_up = jnp.sum(d_up, axis=0)
    d_up_bf = d_up.astype(jnp.bfloat16)
    d_first_norm = d_second + jnp.dot(d_up_bf, back_up.T, preferred_element_type=jnp.float32)
    grad_ln1_gain = jnp.sum(d_first_norm * normed_one, axis=0)
    grad_ln1_bias = jnp.sum(d_first_norm, axis=0)
    d_first = normalize_back(
        d_first_norm * back_gain_one.astype(jnp.float32), normed_one, inverse_one
    )
    grad_b_out = jnp.sum(d_first, axis=0)
    d_first_bf = d_first.astype(jnp.bfloat16)
    d_attended = jnp.dot(d_first_bf, back_out.T, preferred_element_type=jnp.float32).astype(
        jnp.bfloat16
    )
    grad_heads = lax.all_to_all(d_attended, "seq", split_axis=1, concat_axis=0, tiled=True)
    grad_three = grad_heads.reshape(query_count, heads_here, HEAD_DIM)
    attended_three = attended_heads.reshape(query_count, heads_here, HEAD_DIM)
    delta = jnp.transpose(
        jnp.sum(grad_three.astype(jnp.float32) * attended_three.astype(jnp.float32), axis=2)
    )
    back_init = (
        jnp.zeros((query_count, heads_here, HEAD_DIM), jnp.float32),
        jnp.zeros((key_count, head_cols), jnp.float32),
        jnp.zeros((key_count, head_cols), jnp.float32),
    )
    fold_state = back_init

    def backward_one_block(inner_state, block_item):
        grad_query, grad_key_all, grad_value_all = inner_state
        key_block, value_block, seg_block, offset = block_item
        scores, same_seq = block_scores(key_block, seg_block)
        probs = jnp.where(same_seq, jnp.exp(scores - log_total[:, :, None]), 0.0)
        grad_probs = jnp.einsum(
            "qhd,khd->hqk", grad_three, value_block, preferred_element_type=jnp.float32
        )
        grad_scores = (probs * (grad_probs - delta[:, :, None]) * score_scale).astype(jnp.bfloat16)
        grad_query = grad_query + jnp.einsum(
            "hqk,khd->qhd", grad_scores, key_block, preferred_element_type=jnp.float32
        )
        key_part = jnp.einsum(
            "hqk,qhd->khd", grad_scores, query_three, preferred_element_type=jnp.float32
        ).reshape(-1, head_cols)
        value_part = jnp.einsum(
            "hqk,qhd->khd",
            probs.astype(jnp.bfloat16),
            grad_three,
            preferred_element_type=jnp.float32,
        ).reshape(-1, head_cols)
        grad_key_all = lax.dynamic_update_slice_in_dim(grad_key_all, key_part, offset, 0)
        grad_value_all = lax.dynamic_update_slice_in_dim(grad_value_all, value_part, offset, 0)
        return ((grad_query, grad_key_all, grad_value_all), None)

    fold_state, unused = lax.scan(
        backward_one_block,
        fold_state,
        split_blocks(
            (
                lax.all_gather(key_heads, "shard", axis=0, tiled=True),
                lax.all_gather(value_heads, "shard", axis=0, tiled=True),
            )
        ),
    )
    grad_query, grad_key_all, grad_value_all = fold_state
    grad_key_own, grad_value_own = (
        lax.psum_scatter(grad_key_all, "shard", scatter_dimension=0, tiled=True),
        lax.psum_scatter(grad_value_all, "shard", scatter_dimension=0, tiled=True),
    )
    query_grad_bf = grad_query.reshape(query_count, head_cols).astype(jnp.bfloat16)
    d_query, d_key, d_value = (
        lax.all_to_all(query_grad_bf, "seq", split_axis=0, concat_axis=1, tiled=True),
        lax.all_to_all(
            grad_key_own.astype(jnp.bfloat16), "seq", split_axis=0, concat_axis=1, tiled=True
        ),
        lax.all_to_all(
            grad_value_own.astype(jnp.bfloat16), "seq", split_axis=0, concat_axis=1, tiled=True
        ),
    )
    d_project = jnp.concatenate([d_query, d_key, d_value], axis=1)
    grad_b_query = jnp.sum(d_query.astype(jnp.float32), axis=0)
    grad_b_value = jnp.sum(d_value.astype(jnp.float32), axis=0)
    d_hidden = d_first + jnp.dot(d_project, back_qkv.T, preferred_element_type=jnp.float32)
    grad_inputs = d_hidden.astype(jnp.bfloat16)
    width_rows = width // shard_count
    ff_rows = w_down.shape[0]
    table_rows = pos_table.shape[0]
    ff_total = w_up.shape[1]
    wide = lax.psum_scatter(
        jnp.concatenate(
            [
                contract_rows(hidden_bf, d_project),
                contract_rows(attended, d_first_bf),
                contract_rows(first_bf, d_up_bf),
            ],
            axis=1,
        ),
        "shard",
        scatter_dimension=0,
        tiled=True,
    )
    owner_rows = ff_rows + table_rows

    def one_owner(owner):
        act_cols = lax.dynamic_slice_in_dim(activated, owner * ff_rows, ff_rows, 1)
        down_part = contract_rows(act_cols, d_second_bf)
        local_ids = positions - owner * table_rows
        local_ids = jnp.where((local_ids >= 0) & (local_ids < table_rows), local_ids, table_rows)
        table_part = jax.ops.segment_sum(d_hidden, local_ids, num_segments=table_rows + 1)[
            :table_rows
        ]
        return jnp.concatenate([down_part, table_part], axis=0)

    owners = jnp.arange(lax.axis_size("shard") * owner_rows // owner_rows, dtype=jnp.int32)
    narrow = lax.psum_scatter(
        lax.map(one_owner, owners).reshape(lax.axis_size("shard") * owner_rows, width),
        "shard",
        scatter_dimension=0,
        tiled=True,
    )
    down_share = narrow[:ff_rows]
    table_share = narrow[ff_rows:]
    wide, down_share, table_share = lax.psum((wide, down_share, table_share), "seq")
    stacked = jnp.stack(
        [
            grad_b_query,
            grad_b_value,
            grad_b_out,
            grad_ln1_gain,
            grad_ln1_bias,
            grad_b_down,
            grad_ln2_gain,
            grad_ln2_bias,
        ]
    )
    stacked, grad_b_up = lax.psum((stacked, grad_b_up), ("seq", "shard"))
    stacked = lax.dynamic_slice_in_dim(stacked, shard_index * width_rows, width_rows, 1)
    grad_b_up = lax.dynamic_slice_in_dim(grad_b_up, shard_index * ff_rows, ff_rows, 0)
    grad_w_qkv = wide[:, : 3 * width]
    grad_w_out = wide[:, 3 * width : 4 * width]
    grad_w_up = wide[:, 4 * width : 4 * width + ff_total]
    return (
        result,
        grad_inputs,
        table_share,
        grad_w_qkv,
        stacked[0],
        stacked[1],
        grad_w_out,
        stacked[2],
        stacked[3],
        stacked[4],
        grad_w_up,
        grad_b_up,
        down_share,
        stacked[5],
        stacked[6],
        stacked[7],
    )


def solution(mesh):
    in_specs = (
        P(("seq", "shard"), None),
        P(("seq", "shard")),
        P(),
        P("shard", None),
        P("shard", None),
        P("shard"),
        P("shard"),
        P("shard", None),
        P("shard"),
        P("shard"),
        P("shard"),
        P("shard", None),
        P("shard"),
        P("shard", None),
        P("shard"),
        P("shard"),
        P("shard"),
        P(("seq", "shard"), None),
    )
    out_specs = (
        P(("seq", "shard"), None),
        P(("seq", "shard"), None),
        P("shard", None),
        P("shard", None),
        P("shard"),
        P("shard"),
        P("shard", None),
        P("shard"),
        P("shard"),
        P("shard"),
        P("shard", None),
        P("shard"),
        P("shard", None),
        P("shard"),
        P("shard"),
        P("shard"),
    )
    return jax.shard_map(local, mesh=mesh, in_specs=in_specs, out_specs=out_specs, check_vma=False)
```

profile of v0, /device:TPU:0, one launch (start us, length us, event | category | flops | bytes accessed | tf_op | source)
XLA Modules:
  0.0 1744.3 jit_solution(11462981221949819266)
XLA Ops:
  10.1 92.3 %all-gather.17.cloned.1.call-done = bf16[8192,1024]{1,0:T(8,128)(2,1)} async-done(((bf16[1024,1024]{1,0:T(8,128)(2,1)}), bf16[8192,1024]{1,0:T(8,128)(2,1)}) %all-gather.17.cloned.1.call-update) | async-done | bytes 16777232 | tf_op jit(solution)/shard_map/all_gather | solution.py:78
  102.4 9.0 gather_fusion
  111.4 38.3 %all-gather.19.cloned.1.call-done = bf16[1024,3072]{1,0:T(8,128)(2,1)} async-done(((bf16[128,3072]{1,0:T(8,128)(2,1)}), bf16[1024,3072]{1,0:T(8,128)(2,1)}) %all-gather.19.cloned.1.call-update) | async-done | bytes 6291472 | tf_op jit(solution)/shard_map/all_gather | solution.py:79
  153.6 13.8 all_to_all.140
  167.5 8.7 all-gather.1
  184.2 12.7 all_to_all.141
  239.0 80.4 %while.41 = (s32[]{:T(128)}, f32[4,512]{1,0:T(4,128)S(1)}, f32[4,512]{1,0:T(4,128)S(1)}, f32[512,4,64]{0,2,1:T(8,128)S(1)}, s32[512]{0:T(512)S(1)}, /*index=5*/s...) while((s32[]{:T(128)}, f32[4,512]{1,0:T(4,128)S(1)}, ...), condition=%wide.region_3.4_spmd.clone, body=%wide.region_0.3_spmd.clone.sunk | while | flops 282734592 | bytes 32383144 | solution.py:170
  324.2 9.0 all-gather.6
  341.2 9.0 all-gather.2
  350.2 8.2 all-gather.4
  358.3 8.7 all-gather.3
  374.9 8.8 all-gather.8
  415.7 9.1 all-to-all-done.4
  429.9 161.1 %while.42 = (s32[]{:T(128)}, f32[512,4,64]{0,2,1:T(8,128)S(1)}, f32[4096,256]{1,0:T(8,128)}, f32[4096,256]{1,0:T(8,128)}, bf16[8,512,4,64]{1,3,2,0:T(8,128)(2,1)...) while((s32[]{:T(128)}, f32[512,4,64]{0,2,1:T(8,128)S(1)}, ...), condition=%wide.region_14.15_spmd.clone, body=%wide.region_13.14_spmd.clone.sunk | while | flops 683147264 | bytes 51937684 | solution.py:279
  591.8 48.7 %reduce-scatter.7.cloned.1.call-done = f32[512,256]{1,0:T(8,128)} async-done(((f32[4096,256]{1,0:T(8,128)}), f32[512,256]{1,0:T(8,128)}) %reduce-scatter.7.cloned.1.call-update) | async-done | bytes 524304 | tf_op jit(solution)/shard_map/reduce_scatter | solution.py:292
  646.9 48.8 %reduce-scatter.5.cloned.1.call-done = f32[512,256]{1,0:T(8,128)} async-done(((f32[4096,256]{1,0:T(8,128)}), f32[512,256]{1,0:T(8,128)}) %reduce-scatter.5.cloned.1.call-update) | async-done | bytes 524304 | tf_op jit(solution)/shard_map/reduce_scatter | solution.py:291
  727.0 143.4 %while.40 = (s32[]{:T(128)}, f32[8,1536,1024]{2,1,0:T(8,128)}, s32[8]{0:T(128)S(1)}, bf16[128,4096]{1,0:T(8,128)(2,1)}, bf16[128,1024]{1,0:T(8,128)(2,1)S(1)}, /...) while((s32[]{:T(128)}, f32[8,1536,1024]{2,1,0:T(8,128)}, ...), condition=%wide.region_19.20_spmd, body=%wide.region_17.19_spmd.sunk | while | flops 135922304 | bytes 27661532 | solution.py:340
  872.4 11.4 fusion.65
  883.8 9.7 fusion.70
  893.6 28.9 %pad_maximum_fusion = f32[1024,8192]{1,0:T(8,128)} fusion(f32[1024,4096]{1,0:T(8,128)} %fusion.65, f32[1024,1024]{1,0:T(8,128)S(1)} %fusion.71, f32[1024,3072]{1,0:T(8,128)} %fusion.70), kind=kLoop, calls=%fused_computation.61 | loop fusion | flops 16777216 | bytes 67108864 | tf_op jit(solution)/shard_map/concatenate | solution.py:314
  922.5 230.9 %reduce-scatter.9.cloned.1.call-done = f32[1536,1024]{1,0:T(8,128)} async-done(((f32[12288,1024]{1,0:T(8,128)}), f32[1536,1024]{1,0:T(8,128)}) %reduce-scatter.9.cloned.1.call-update) | async-done | bytes 6291472 | tf_op jit(solution)/shard_map/reduce_scatter | solution.py:339
  1161.4 201.1 %reduce-scatter.11.cloned.1.call-done = f32[128,8192]{1,0:T(8,128)} async-done(((f32[1024,8192]{1,0:T(8,128)}), f32[128,8192]{1,0:T(8,128)}) %reduce-scatter.11.cloned.1.call-update) | async-done | bytes 4194320 | tf_op jit(solution)/shard_map/reduce_scatter | solution.py:313
  1363.7 45.4 %all-reduce = (f32[8,1024]{1,0:T(8,128)S(1)}, f32[4096]{0:T(1024)S(1)}) all-reduce(f32[8,1024]{1,0:T(8,128)S(1)} %stack.35, f32[4096]{0:T(1024)S(1)} %copy-done.39), channel_id=1, replica_groups=mesh['seq'=4,'shard'=8] {'seq','shard'}, use_global_device_ids=true, to_apply=%region_32.33 | all-reduce | flops 12288 | bytes 98304 | tf_op jit(solution)/shard_map/psum | solution.py:360
  1410.3 315.6 %all-reduce.4.cloned.1.call-done = (f32[1024,1024]{1,0:T(8,128)}, f32[128,8192]{1,0:T(8,128)}, f32[512,1024]{1,0:T(8,128)}) async-done(((f32[1024,1024]{1,0:T(8,128)}, f32[128,8192]{1,0:T(8,128)}, f32[512,1024]{1,0:T(8,128)}), (f32[1024,1024]{1,0:T(8,128)}, f32[128,8192]{1,0:T(8,128)}, f32[512,1024]{1,0:T(8,128)})) %all-reduce.4.cloned.1.call-update) | async-done | bytes 10485776 | tf_op jit(solution)/shard_map/psum | solution.py:347
  (541 shorter events, 533.5 us)
Async XLA Ops:
  7.2 142.5 %copy-start.18 = (bf16[128,1024]{1,0:T(8,128)(2,1)S(1)}, bf16[128,1024]{1,0:T(8,128)(2,1)}, u32[]{:S(2)}) copy-start(bf16[128,1024]{1,0:T(8,128)(2,1)} %param.24) | copy-start | bytes 786436
  7.2 95.2 %all-gather.17.cloned.1.call-start = ((), (), s32[]{:S(2)}) async-start(), calls=%async_computation.12 | async-start | bytes 18874368 | tf_op jit(solution)/shard_map/all_gather | solution.py:78
  7.9 141.8 %all-gather.19.cloned.1.call-start = ((), (), s32[]{:S(2)}) async-start(), calls=%async_computation.13 | async-start | bytes 7077888 | tf_op jit(solution)/shard_map/all_gather | solution.py:79
  8.7 202.2 %all-gather.21.cloned.1.call-start = ((), (), s32[]{:S(2)}) async-start(), calls=%async_computation.14 | async-start | bytes 2359296 | tf_op jit(solution)/shard_map/all_gather | solution.py:175
  111.3 272.4 %copy-start.12 = (bf16[128,1024]{1,0:T(8,128)(2,1)}, bf16[128,1024]{1,0:T(8,128)(2,1)S(1)}, u32[]{:S(2)}) copy-start(bf16[128,1024]{1,0:T(8,128)(2,1)S(1)} %gather_fusion) | copy-start | bytes 786436
  167.4 57.5 %all-gather.23.cloned.1.call-start = ((), (), s32[]{:S(2)}) async-start(), calls=%async_computation.15 | async-start | bytes 2359296 | tf_op jit(solution)/shard_map/all_gather | solution.py:176
  197.0 186.8 %all-gather.25.cloned.1.call-start = ((), (), s32[]{:S(2)}) async-start(), calls=%async_computation.16 | async-start | bytes 2359296 | tf_op jit(solution)/shard_map/all_gather | solution.py:80
  197.6 188.7 %all-gather.27.cloned.1.call-start = ((), (), s32[]{:S(2)}) async-start(), calls=%async_computation.17 | async-start | bytes 9437184 | tf_op jit(solution)/shard_map/all_gather | solution.py:81
  198.9 11.7 all-to-all-start.1
  202.3 190.4 %all-gather.29.cloned.1.call-start = ((), (), s32[]{:S(2)}) async-start(), calls=%async_computation.18 | async-start | bytes 9437184 | tf_op jit(solution)/shard_map/all_gather | solution.py:82
  239.0 119.3 %copy-start.46 = (bf16[128]{0:T(256)(128)(2,1)S(1)}, bf16[128]{0:T(256)(128)(2,1)}, u32[]{:S(2)}) copy-start(bf16[128]{0:T(256)(128)(2,1)} %param.33) | copy-start | bytes 772
  239.0 128.0 %copy-start.47 = (bf16[128]{0:T(256)(128)(2,1)S(1)}, bf16[128]{0:T(256)(128)(2,1)}, u32[]{:S(2)}) copy-start(bf16[128]{0:T(256)(128)(2,1)} %param.39) | copy-start | bytes 772
  239.0 135.9 %copy-start.48 = (bf16[128]{0:T(256)(128)(2,1)S(1)}, bf16[128]{0:T(256)(128)(2,1)}, u32[]{:S(2)}) copy-start(bf16[128]{0:T(256)(128)(2,1)} %param.40) | copy-start | bytes 772
  320.3 63.5 %all-to-all-start.3 = ((bf16[4,128,256]{1,2,0:T(8,128)(2,1)}), bf16[4,128,256]{1,2,0:T(8,128)(2,1)S(1)}, u32[]{:S(2)}, u32[]{:S(2)}) async-start(bf16[4,128,256]{1,2,0:T(8,128)(2,1)} %copy.123), calls=%async_computation.3 | async-start | bytes 524288 | tf_op jit(solution)/shard_map/all_to_all | solution.py:187
  410.4 14.5 all-to-all-start.4
  415.5 225.0 %reduce-scatter.7.cloned.1.call-start = ((), (), s32[]{:S(2)}) async-start(), calls=%async_computation.20 | async-start | bytes 4718592 | tf_op jit(solution)/shard_map/reduce_scatter | solution.py:292
  591.0 104.6 %reduce-scatter.5.cloned.1.call-start = ((), (), s32[]{:S(2)}) async-start(), calls=%async_computation.19 | async-start | bytes 4718592 | tf_op jit(solution)/shard_map/reduce_scatter | solution.py:291
  591.1 130.1 %copy-start.9 = (f32[128,1024]{1,0:T(8,128)S(1)}, f32[128,1024]{1,0:T(8,128)}, u32[]{:S(2)}) copy-start(f32[128,1024]{1,0:T(8,128)} %copy-done.8) | copy-start | bytes 1572868
  642.2 55.1 %all-to-all-start.7 = ((bf16[4,128,256]{2,1,0:T(8,128)(2,1)}), bf16[4,128,256]{2,1,0:T(8,128)(2,1)S(1)}, u32[]{:S(2)}, u32[]{:S(2)}) async-start(bf16[4,128,256]{2,1,0:T(8,128)(2,1)} %bitcast.43), calls=%async_computation.9 | async-start | bytes 524288 | tf_op jit(solution)/shard_map/all_to_all | solution.py:300
  697.4 13.4 all-to-all-start.6
  710.7 10.4 all-to-all-start.5
  714.2 439.3 %reduce-scatter.9.cloned.1.call-start = ((), (), s32[]{:S(2)}) async-start(), calls=%async_computation.21 | async-start | bytes 56623104 | tf_op jit(solution)/shard_map/reduce_scatter | solution.py:339
  870.4 492.2 %reduce-scatter.11.cloned.1.call-start = ((), (), s32[]{:S(2)}) async-start(), calls=%async_computation.22 | async-start | bytes 37748736 | tf_op jit(solution)/shard_map/reduce_scatter | solution.py:313
  922.5 803.4 %all-reduce.4.cloned.1.call-start = ((), (), s32[]{:S(2)}) async-start(), calls=%async_computation.23 | async-start | bytes 20971520 | tf_op jit(solution)/shard_map/psum | solution.py:347
  (95 other events, 955.1 us)
Sparse Core Ops, SparseCore 0:
  9.9 92.4 all-gather.16
  104.3 45.3 all-gather.18
  167.6 25.9 all-gather.20
  197.1 25.9 all-gather.22
  224.8 27.7 all-gather.24
  254.4 54.2 all-gather.26
  310.5 54.2 all-gather.28
  591.2 49.2 reduce-scatter.6
  644.4 51.1 reduce-scatter.4
  870.5 282.9 reduce-scatter.8
  1157.0 205.4 reduce-scatter.10
  1366.3 359.5 all-reduce.3
where the time goes:
time: 1750 us; the launch traced here: 1740 us
  waiting for transfers between devices  1010 us (58%)
  matrix products  198 us (11%)
  local copies, waits for them, and re-layouts  171 us (10%)
  other arithmetic  148 us (8%)
  blocking collectives  148 us (8%)
  loops' own time  27.4 us (2%)
  starting transfers between devices  26.4 us (2%)
    psum x1, waiting for transfers between devices, local(): lax.psum((wide, down_share, table_share), 'seq')  316 us
    reduce_scatter x1, waiting for transfers between devices, local(): lax.psum_scatter(lax.map(one_owner, owners).reshape(lax.axis_size('shard'...  231 us
    reduce_scatter x1, waiting for transfers between devices, local(): lax.psum_scatter(jnp.concatenate([contract_rows(hidden_bf, d_project), co...  201 us
    all_gather x1, waiting for transfers between devices, local(): lax.all_gather(pos_table, 'shard', axis=0, tiled=True)  92.3 us
    reduce_scatter x1, waiting for transfers between devices, local(): lax.psum_scatter(grad_key_all, 'shard', scatter_dimension=0, tiled=True)  48.8 us
    reduce_scatter x1, waiting for transfers between devices, local(): lax.psum_scatter(grad_value_all, 'shard', scatter_dimension=0, tiled=True)  48.7 us
    dynamic_update_slice x8, other arithmetic, local(): lax.map(one_owner, owners)  47.8 us
    dot_general x16, matrix products, block_scores(): jnp.einsum('qhd,khd->hqk', query_three, key_block, preferred_element_type...  45.7 us
  transfers between devices with their start and end apart: 18, of which 11 were waited for; matrix products, arithmetic and copies ran while one was open for 11% of the time, Pallas kernels for 0%

commit v1 on v0

v1 whole, which is shorter than its diff:
```python
import functools
import math

import jax
import jax.numpy as jnp
from jax import lax
from jax.experimental import pallas as pl
from jax.experimental.pallas import tpu as pltpu
from jax.sharding import PartitionSpec as P

HEADS = 16
HEAD_DIM = 64
score_scale = 0.125
neg_large = -1e30
epsilon = 1e-06
root_half = 0.7071067811865476
inv_root_two_pi = 0.3989422804014327
MESH = pl.DeviceIdType.MESH
F32 = jnp.float32
BF16 = jnp.bfloat16
VMEM_LIMIT = 60 * 1024 * 1024


def flip(value, mask, width):
    total, bit = 0, 1
    while bit < width:
        a = lax.rem(value // bit, 2)
        b = (mask // bit) % 2 if isinstance(mask, int) else lax.rem(mask // bit, 2)
        total = total + lax.rem(a + b, 2) * bit
        bit *= 2
    return total


def remote(src, dst, send_sem, recv_sem, device):
    return pltpu.make_async_remote_copy(
        src_ref=src,
        dst_ref=dst,
        send_sem=send_sem,
        recv_sem=recv_sem,
        device_id=device,
        device_id_type=MESH,
    )


def await_recv(dst, sem, device):
    remote(dst, dst, sem, sem, device).wait_recv()


def await_send(src, sem, device):
    remote(src, src, sem, sem, device).wait_send()


def rows_dot(a, b):
    return lax.dot_general(a, b, (((1,), (0,)), ((), ())), preferred_element_type=F32)


def rows_dot_t(a, b):
    return lax.dot_general(a, b, (((1,), (1,)), ((), ())), preferred_element_type=F32)


def cols_dot(a, b):
    return lax.dot_general(a, b, (((0,), (0,)), ((), ())), preferred_element_type=F32)


def entry_kernel(
    dims,
    pos_ref,
    inp_ref,
    table_ref,
    wqkv_ref,
    wup_ref,
    wdn_ref,
    wout_ref,
    par_ref,
    bup_ref,
    q_ref,
    kv_ref,
    hid_half_ref,
    hidden_ref,
    wq_ref,
    wup2_ref,
    wdn_o_ref,
    wout_o_ref,
    par_all_ref,
    bup_o_ref,
    pos_glob_ref,
    table_v,
    pstage,
    precv,
    cstage,
    crecv,
    qst,
    kvst,
    wup_own,
    wq_tmp,
    pos_ss,
    pos_rs,
    par_ss,
    par_rs,
    posz_ss,
    posz_rs,
    wq_ss,
    wq_rs,
    wqf_ss,
    wqf_rs,
    wup_ss,
    wup_rs,
    wupf_ss,
    wupf_rs,
    misc_ss,
    misc_rs,
    rsp_ss,
    rsp_rs,
    rsc_ss,
    rsc_rs,
    ag_ss,
    ag_rs,
    qx_ss,
    qx_rs,
    zx_ss,
    zx_rs,
    loc,
):
    S, n, C, L, D, hc, R, F2 = dims
    z = lax.axis_index("seq")
    s = lax.axis_index("shard")
    core = lax.rem(s, 2)
    chip = s // 2
    other = 1 - core
    partner = 2 * chip + other
    h2 = 2 * hc
    Dn = D // n

    table_copy = pltpu.make_async_copy(table_ref, table_v, loc.at[0])
    table_copy.start()
    own_wq = []
    for part in range(3):
        own_wq.append(
            pltpu.make_async_copy(
                wqkv_ref.at[:, pl.ds(pl.multiple_of(part * D + chip * h2, 128), h2)],
                wq_ref.at[s, :, part * h2 : (part + 1) * h2],
                loc.at[1 + part],
            )
        )
        own_wq[-1].start()
    own_wup_in = pltpu.make_async_copy(
        wup_ref.at[:, pl.ds(pl.multiple_of(chip * F2, 128), F2)], wup_own, loc.at[4]
    )
    own_wup_in.start()

    barrier = pltpu.get_barrier_semaphore()
    for d in range(1, n):
        pl.semaphore_signal(barrier, inc=1, device_id=(z, flip(s, d, n)), device_id_type=MESH)
    for d in range(1, S):
        pl.semaphore_signal(barrier, inc=1, device_id=(lax.rem(z + d, S), s), device_id_type=MESH)

    for d in (1, S - 1):
        pl.semaphore_signal(
            barrier, inc=1, device_id=(lax.rem(z + d, S), partner), device_id_type=MESH
        )
    pl.semaphore_wait(barrier, n - 1 + S - 1 + 2)

    pos_glob_ref[z, s] = pos_ref[...]
    par_all_ref[s] = par_ref[...]
    for d in range(1, n):
        peer = (z, flip(s, d, n))
        remote(pos_ref, pos_glob_ref.at[z, s], pos_ss.at[d], pos_rs.at[d], peer).start()
        remote(par_ref, par_all_ref.at[s], par_ss.at[d], par_rs.at[d], peer).start()

    for own in own_wq:
        own.wait()

    def wq_src(peer_chip, part):
        return wqkv_ref.at[:, pl.ds(pl.multiple_of(part * D + peer_chip * h2, 128), h2)]

    for j in range(C - 1, 0, -1):
        pc = flip(chip, j, C)
        for part in range(3):
            remote(
                wq_src(pc, part),
                wq_ref.at[s, :, part * h2 : (part + 1) * h2],
                wq_ss.at[j, part],
                wq_rs.at[j, part],
                (z, 2 * pc + core),
            ).start()
    remote(wq_ref.at[s], wq_ref.at[s], wqf_ss.at[0], wqf_rs.at[0], (z, partner)).start()

    for d in range(1, n):
        src = flip(s, d, n)
        await_recv(pos_glob_ref.at[z, src], pos_rs.at[d], (z, src))
    for d in range(1, S):
        remote(
            pos_glob_ref.at[z],
            pos_glob_ref.at[z],
            posz_ss.at[d],
            posz_rs.at[d],
            (lax.rem(z + d, S), s),
        ).start()

    table_copy.wait()
    lane_ids = lax.broadcasted_iota(jnp.int32, (L, R), 1) + s * R

    def picked(block):
        ids = jnp.broadcast_to(pos_glob_ref[z, block], (L, L)).T
        ids = jnp.concatenate([ids] * (R // L), axis=1)
        hot = jnp.where(ids == lane_ids, 1.0, 0.0).astype(BF16)
        return rows_dot(hot, table_v[...])

    def send_partner(j):
        pstage[j] = picked(2 * flip(chip, j, C) + other).astype(BF16)
        remote(pstage.at[j], precv.at[j], rsp_ss.at[j], rsp_rs.at[j], (z, partner)).start()

    def combined(j):
        mine = picked(2 * flip(chip, j, C) + core)
        await_recv(precv.at[j], rsp_rs.at[j], (z, partner))
        return mine + precv[j].astype(F32)

    send_partner(C - 1)

    def scatter_step(k, carry):
        j = C - 1 - k
        send_partner(j - 1)
        cstage[j] = combined(j).astype(BF16)
        remote(
            cstage.at[j], crecv.at[j], rsc_ss.at[j], rsc_rs.at[j], (z, 2 * flip(chip, j, C) + core)
        ).start()
        return carry

    lax.fori_loop(0, C - 1, scatter_step, 0)
    hidden = combined(0) + inp_ref[...].astype(F32)

    for j in range(1, C):
        src = 2 * flip(chip, j, C) + core
        for part in range(3):
            await_recv(
                wq_ref.at[src, :, part * h2 : (part + 1) * h2], wq_rs.at[j, part], (z, src)
            )
        remote(wq_ref.at[src], wq_ref.at[src], wqf_ss.at[j], wqf_rs.at[j], (z, partner)).start()

    for j in range(1, C):
        await_recv(crecv.at[j], rsc_rs.at[j], (z, 2 * flip(chip, j, C) + core))
        hidden = hidden + crecv[j].astype(F32)
    hidden_ref[...] = hidden
    hid_half_ref[chip] = hidden.astype(BF16)
    for j in range(C - 1, 0, -1):
        remote(
            hid_half_ref.at[chip],
            hid_half_ref.at[chip],
            ag_ss.at[j],
            ag_rs.at[j],
            (z, 2 * flip(chip, j, C) + core),
        ).start()

    own_wup_in.wait()
    own_wup_out = pltpu.make_async_copy(wup_own, wup2_ref.at[s], loc.at[5])
    own_wup_out.start()
    for j in range(C - 1, 0, -1):
        pc = flip(chip, j, C)
        remote(
            wup_ref.at[:, pl.ds(pl.multiple_of(pc * F2, 128), F2)],
            wup2_ref.at[s],
            wup_ss.at[j],
            wup_rs.at[j],
            (z, 2 * pc + core),
        ).start()
    remote(wup_own, wup2_ref.at[s], wupf_ss.at[0], wupf_rs.at[0], (z, partner)).start()
    remote(wdn_ref, wdn_o_ref, misc_ss.at[0], misc_rs.at[0], (z, partner)).start()
    remote(wout_ref, wout_o_ref, misc_ss.at[1], misc_rs.at[1], (z, partner)).start()
    remote(bup_ref, bup_o_ref, misc_ss.at[2], misc_rs.at[2], (z, partner)).start()

    for j in range(C):
        src = 2 * flip(chip, j, C) + other
        await_recv(wq_ref.at[src], wqf_rs.at[j], (z, partner))
    for d in range(1, n):
        src = flip(s, d, n)
        await_recv(par_all_ref.at[src], par_rs.at[d], (z, src))
    bias = jnp.concatenate([par_all_ref[2 * chip], par_all_ref[2 * chip + 1]], axis=1)
    bias_q, bias_v = bias[6:7], bias[7:8]
    first_core = core == 0

    def project(j, carry):
        c = flip(chip, j, C)

        @pl.when(j > 0)
        def _():
            await_recv(hid_half_ref.at[c], ag_rs.at[j], (z, 2 * c + core))

        res = rows_dot(hid_half_ref[c], wq_ref[...].reshape(D, 3 * h2))
        query = (res[:, :h2] + bias_q).astype(BF16) * score_scale
        key = res[:, h2 : 2 * h2].astype(BF16)
        value = (res[:, 2 * h2 :] + bias_v).astype(BF16)
        q_ref[c, core] = jnp.where(first_core, query[:, :hc], query[:, hc:])
        kv_ref[1, c, core, :, :hc] = jnp.where(first_core, key[:, :hc], key[:, hc:])
        kv_ref[1, c, core, :, hc:] = jnp.where(first_core, value[:, :hc], value[:, hc:])
        qst[j] = jnp.where(first_core, query[:, hc:], query[:, :hc])
        kvst[j, :, :hc] = jnp.where(first_core, key[:, hc:], key[:, :hc])
        kvst[j, :, hc:] = jnp.where(first_core, value[:, hc:], value[:, :hc])
        own_kv = kv_ref.at[1, c, core]

        @pl.when(z < S - 1)
        def _():
            remote(
                own_kv, kv_ref.at[0, c, core], zx_ss.at[j, 0], zx_rs.at[j, 0], (z + 1, s)
            ).start()
            remote(
                kvst.at[j], kv_ref.at[0, c, core], zx_ss.at[j, 1], zx_rs.at[j, 1], (z + 1, partner)
            ).start()

        @pl.when(z > 0)
        def _():
            remote(
                own_kv, kv_ref.at[2, c, core], zx_ss.at[j, 2], zx_rs.at[j, 2], (z - 1, s)
            ).start()
            remote(
                kvst.at[j], kv_ref.at[2, c, core], zx_ss.at[j, 3], zx_rs.at[j, 3], (z - 1, partner)
            ).start()

        remote(qst.at[j], q_ref.at[c, core], qx_ss.at[j, 0], qx_rs.at[j, 0], (z, partner)).start()
        remote(
            kvst.at[j], kv_ref.at[1, c, core], qx_ss.at[j, 1], qx_rs.at[j, 1], (z, partner)
        ).start()
        return carry

    lax.fori_loop(0, C, project, 0)

    for j in range(1, C):
        src = 2 * flip(chip, j, C) + core
        await_recv(wup2_ref.at[src], wup_rs.at[j], (z, src))
        remote(
            wup2_ref.at[src], wup2_ref.at[src], wupf_ss.at[j], wupf_rs.at[j], (z, partner)
        ).start()

    def settle(j, carry):
        c = flip(chip, j, C)
        await_recv(q_ref.at[c, other], qx_rs.at[j, 0], (z, partner))
        await_recv(kv_ref.at[1, c, other], qx_rs.at[j, 1], (z, partner))
        await_send(qst.at[j], qx_ss.at[j, 0], (z, partner))
        await_send(kvst.at[j], qx_ss.at[j, 1], (z, partner))

        @pl.when(z > 0)
        def _():
            await_recv(kv_ref.at[0, c, core], zx_rs.at[j, 0], (z - 1, s))
            await_recv(kv_ref.at[0, c, other], zx_rs.at[j, 1], (z - 1, partner))
            await_send(kvst.at[j], zx_ss.at[j, 2], (z - 1, s))
            await_send(kvst.at[j], zx_ss.at[j, 3], (z - 1, partner))

        @pl.when(z < S - 1)
        def _():
            await_recv(kv_ref.at[2, c, core], zx_rs.at[j, 2], (z + 1, s))
            await_recv(kv_ref.at[2, c, other], zx_rs.at[j, 3], (z + 1, partner))
            await_send(kvst.at[j], zx_ss.at[j, 0], (z + 1, s))
            await_send(kvst.at[j], zx_ss.at[j, 1], (z + 1, partner))

        await_send(pstage.at[j], rsp_ss.at[j], (z, partner))
        await_send(wq_ref.at[s], wqf_ss.at[j], (z, partner))
        await_recv(wup2_ref.at[2 * c + other], wupf_rs.at[j], (z, partner))
        await_send(wup2_ref.at[s], wupf_ss.at[j], (z, partner))
        return carry

    lax.fori_loop(0, C, settle, 0)
    for j in range(1, C):
        peer = (z, 2 * flip(chip, j, C) + core)
        await_send(cstage.at[j], rsc_ss.at[j], peer)
        await_send(hid_half_ref.at[chip], ag_ss.at[j], peer)
        await_send(wup_own, wup_ss.at[j], peer)
        for part in range(3):
            await_send(
                wq_ref.at[s, :, part * h2 : (part + 1) * h2], wq_ss.at[j, part], peer
            )
    for d in range(1, n):
        peer = (z, flip(s, d, n))
        await_send(pos_ref, pos_ss.at[d], peer)
        await_send(par_ref, par_ss.at[d], peer)
    for d in range(1, S):
        src = lax.rem(z + S - d, S)
        await_recv(pos_glob_ref.at[src], posz_rs.at[d], (src, s))
        await_send(pos_glob_ref.at[z], posz_ss.at[d], (lax.rem(z + d, S), s))
    for i, (mine, got) in enumerate(
        ((wdn_ref, wdn_o_ref), (wout_ref, wout_o_ref), (bup_ref, bup_o_ref))
    ):
        await_recv(got, misc_rs.at[i], (z, partner))
        await_send(mine, misc_ss.at[i], (z, partner))
    own_wup_out.wait()


def entry_call(S, n, pos, inp, table, wqkv, wup, wdn, wout, par, bup):
    C = n // 2
    L, D = inp.shape
    hc = D // n
    R = table.shape[0]
    F = wup.shape[1]
    F1, F2 = F // n, 2 * F // n
    dims = (S, n, C, L, D, hc, R, F2)
    dma = pltpu.SemaphoreType.DMA
    vm = pl.BlockSpec(memory_space=pltpu.VMEM)
    anyw = pl.BlockSpec(memory_space=pl.ANY)
    sds = jax.ShapeDtypeStruct
    return pl.pallas_call(
        functools.partial(entry_kernel, dims),
        out_shape=(
            sds((C, 2, L, hc), BF16),
            sds((3, C, 2, L, 2 * hc), BF16),
            sds((C, L, D), BF16),
            sds((L, D), F32),
            sds((n, D // n, 6 * hc), BF16),
            sds((n, D // n, F2), BF16),
            sds((F1, D), BF16),
            sds((D // n, D), BF16),
            sds((n, 8, hc), F32),
            sds((1, F1), F32),
            sds((S, n, 1, L), jnp.int32),
        ),
        in_specs=[vm, vm, anyw, anyw, anyw, anyw, anyw, vm, vm],
        out_specs=(vm, vm, vm, vm, vm, anyw, anyw, anyw, vm, vm, vm),
        scratch_shapes=[
            pltpu.VMEM((R, D), BF16),
            pltpu.VMEM((C, L, D), BF16),
            pltpu.VMEM((C, L, D), BF16),
            pltpu.VMEM((C, L, D), BF16),
            pltpu.VMEM((C, L, D), BF16),
            pltpu.VMEM((C, L, hc), BF16),
            pltpu.VMEM((C, L, 2 * hc), BF16),
            pltpu.VMEM((D // n, F2), BF16),
            pltpu.VMEM((8, 128), BF16),
            dma((n,)),
            dma((n,)),
            dma((n,)),
            dma((n,)),
            dma((S,)),
            dma((S,)),
            dma((C, 3)),
            dma((C, 3)),
            dma((C,)),
            dma((C,)),
            dma((C,)),
            dma((C,)),
            dma((C,)),
            dma((C,)),
            dma((3,)),
            dma((3,)),
            dma((C,)),
            dma((C,)),
            dma((C,)),
            dma((C,)),
            dma((C,)),
            dma((C,)),
            dma((C, 2)),
            dma((C, 2)),
            dma((C, 4)),
            dma((C, 4)),
            dma((6,)),
        ],
        compiler_params=pltpu.CompilerParams(
            collective_id=0, has_side_effects=True, vmem_limit_bytes=VMEM_LIMIT
        ),
        name="entry_stage",
    )(pos, inp, table, wqkv, wup, wdn, wout, par, bup)


def attend_kernel(dims, bounds_ref, q_ref, kv_ref, lohi_ref, att_ref, lse_ref, vt_ref):
    P_, hc, hh, bq, bk = dims
    lanes = lax.broadcasted_iota(jnp.int32, (bq, hc), 1) // HEAD_DIM
    nq = P_ // bq

    def flip_value(kb, carry):
        at = pl.multiple_of(kb * bk, bk)
        vt_ref[kb] = kv_ref[pl.ds(at, bk), hc:].T
        return carry

    lax.fori_loop(bounds_ref[0, 0], bounds_ref[1, nq - 1], flip_value, 0)

    def one_query_block(qi, carry):
        rows = pl.ds(pl.multiple_of(qi * bq, bq), bq)
        query = q_ref[rows, :]
        heads_q = [jnp.where(lanes == h, query, jnp.zeros_like(query)) for h in range(hh)]
        low, high = lohi_ref[0:1, rows], lohi_ref[1:2, rows]

        def one_key_block(kb, state):
            at = pl.multiple_of(kb * bk, bk)
            keys = kv_ref[pl.ds(at, bk), :hc]
            ids = lax.broadcasted_iota(jnp.int32, (bk, bq), 0) + kb * bk
            keep = (ids >= low) & (ids < high)
            fresh = []
            for h in range(hh):
                top, total, acc = state[h]
                scores = jnp.where(keep, rows_dot_t(keys, heads_q[h]), neg_large)
                new_top = jnp.maximum(top, jnp.max(scores, axis=0, keepdims=True))
                weights = jnp.exp(scores - new_top)
                shrink = jnp.exp(top - new_top)
                total = total * shrink + jnp.sum(weights, axis=0, keepdims=True)
                values = vt_ref[kb, h * HEAD_DIM : (h + 1) * HEAD_DIM, :]
                acc = acc * shrink + rows_dot(values, weights.astype(BF16))
                fresh.append((new_top, total, acc))
            return tuple(fresh)

        start = tuple(
            (
                jnp.full((1, bq), neg_large, F32),
                jnp.zeros((1, bq), F32),
                jnp.zeros((HEAD_DIM, bq), F32),
            )
            for _ in range(hh)
        )
        state = lax.fori_loop(bounds_ref[0, qi], bounds_ref[1, qi], one_key_block, start)
        mixed = jnp.concatenate([acc / total for _, total, acc in state], axis=0)
        att_ref[rows, :] = mixed.T.astype(BF16)
        for h in range(hh):
            lse_ref[h : h + 1, rows] = state[h][0] + jnp.log(state[h][1])
        return carry

    lax.fori_loop(0, nq, one_query_block, 0)


def attend_call(q, kv, bounds, lohi, bq, bk):
    P_, hc = q.shape
    hh = hc // HEAD_DIM
    vm = pl.BlockSpec(memory_space=pltpu.VMEM)
    sm = pl.BlockSpec(memory_space=pltpu.SMEM)
    return pl.pallas_call(
        functools.partial(attend_kernel, (P_, hc, hh, bq, bk)),
        out_shape=(
            jax.ShapeDtypeStruct((P_, hc), BF16),
            jax.ShapeDtypeStruct((hh, P_), F32),
        ),
        in_specs=[sm, vm, vm, vm],
        out_specs=(vm, vm),
        scratch_shapes=[pltpu.VMEM((3 * P_ // bk, hc, bk), BF16)],
        compiler_params=pltpu.CompilerParams(vmem_limit_bytes=VMEM_LIMIT),
        name="attend_stage",
    )(bounds, q, kv, lohi)


def attend_back_kernel(
    dims, bounds_ref, q_ref, kv_ref, lohi_ref, att_ref, datt_ref, lse_ref, dq_ref, dkv_ref, kt_ref, acc_ref
):
    P_, hc, hh, bq, bk = dims
    lanes = lax.broadcasted_iota(jnp.int32, (bq, hc), 1) // HEAD_DIM
    nq = P_ // bq
    acc_ref[...] = jnp.zeros_like(acc_ref)

    def flip_key(kb, carry):
        at = pl.multiple_of(kb * bk, bk)
        kt_ref[kb] = kv_ref[pl.ds(at, bk), :hc].T
        return carry

    lax.fori_loop(bounds_ref[0, 0], bounds_ref[1, nq - 1], flip_key, 0)

    def one_query_block(qi, carry):
        rows = pl.ds(pl.multiple_of(qi * bq, bq), bq)
        query, grad = q_ref[rows, :], datt_ref[rows, :]
        zero = jnp.zeros_like(query)
        heads_q = [jnp.where(lanes == h, query, zero) for h in range(hh)]
        heads_g = [jnp.where(lanes == h, grad, zero) for h in range(hh)]
        stack_q = jnp.concatenate(heads_q, axis=0)
        stack_g = jnp.concatenate(heads_g, axis=0)
        product = (grad.astype(F32) * att_ref[rows, :].astype(F32)).T
        delta = [
            jnp.sum(product[h * HEAD_DIM : (h + 1) * HEAD_DIM], axis=0, keepdims=True)
            for h in range(hh)
        ]
        logs = [lse_ref[h : h + 1, rows] for h in range(hh)]
        low, high = lohi_ref[0:1, rows], lohi_ref[1:2, rows]

        def one_key_block(kb, state):
            at = pl.multiple_of(kb * bk, bk)
            keys = kv_ref[pl.ds(at, bk), :hc]
            values = kv_ref[pl.ds(at, bk), hc:]
            ids = lax.broadcasted_iota(jnp.int32, (bk, bq), 0) + kb * bk
            keep = (ids >= low) & (ids < high)
            fresh, all_p, all_s = [], [], []
            for h in range(hh):
                scores = rows_dot_t(keys, heads_q[h])
                probs = jnp.where(keep, jnp.exp(scores - logs[h]), 0.0)
                grad_probs = rows_dot_t(values, heads_g[h])
                grad_scores = (probs * (grad_probs - delta[h])).astype(BF16)
                all_p.append(probs.astype(BF16))
                all_s.append(grad_scores)
                key_cols = kt_ref[kb, h * HEAD_DIM : (h + 1) * HEAD_DIM, :]
                fresh.append(state[h] + rows_dot(key_cols, grad_scores))
            acc_ref[pl.ds(at, bk), :hc] += rows_dot(jnp.concatenate(all_s, axis=1), stack_q)
            acc_ref[pl.ds(at, bk), hc:] += rows_dot(jnp.concatenate(all_p, axis=1), stack_g)
            return tuple(fresh)

        start = tuple(jnp.zeros((HEAD_DIM, bq), F32) for _ in range(hh))
        state = lax.fori_loop(bounds_ref[0, qi], bounds_ref[1, qi], one_key_block, start)
        dq_ref[rows, :] = (jnp.concatenate(state, axis=0).T * score_scale).astype(BF16)
        return carry

    lax.fori_loop(0, nq, one_query_block, 0)
    dkv_ref[...] = acc_ref[...].astype(BF16)


def attend_back_call(q, kv, bounds, lohi, att, datt, lse, bq, bk):
    P_, hc = q.shape
    hh = hc // HEAD_DIM
    vm = pl.BlockSpec(memory_space=pltpu.VMEM)
    sm = pl.BlockSpec(memory_space=pltpu.SMEM)
    return pl.pallas_call(
        functools.partial(attend_back_kernel, (P_, hc, hh, bq, bk)),
        out_shape=(
            jax.ShapeDtypeStruct((P_, hc), BF16),
            jax.ShapeDtypeStruct((3 * P_, 2 * hc), BF16),
        ),
        in_specs=[sm, vm, vm, vm, vm, vm, vm],
        out_specs=(vm, vm),
        scratch_shapes=[
            pltpu.VMEM((3 * P_ // bk, hc, bk), BF16),
            pltpu.VMEM((3 * P_, 2 * hc), F32),
        ],
        compiler_params=pltpu.CompilerParams(vmem_limit_bytes=VMEM_LIMIT),
        name="attend_back_stage",
    )(bounds, q, kv, lohi, att, datt, lse)


def ranges(segments, P_, bq, bk):
    z = lax.axis_index("seq")
    own = lax.dynamic_slice_in_dim(segments, z * P_, P_)
    low = jnp.sum((segments[:, None] < own[None, :]).astype(jnp.int32), axis=0) - (z - 1) * P_
    high = jnp.sum((segments[:, None] <= own[None, :]).astype(jnp.int32), axis=0) - (z - 1) * P_
    lohi = jnp.stack([low, high])
    bounds = jnp.stack([low[::bq] // bk, (high[bq - 1 :: bq] + bk - 1) // bk])
    return bounds, lohi


def layer_stats(summed):
    center = summed - jnp.mean(summed, axis=1, keepdims=True)
    inverse = lax.rsqrt(jnp.mean(center * center, axis=1, keepdims=True) + epsilon)
    return center * inverse, inverse


def layer_back(grad, normed, inverse):
    first = jnp.mean(grad, axis=1, keepdims=True)
    second = jnp.mean(grad * normed, axis=1, keepdims=True)
    return inverse * (grad - first - normed * second)


def col_sum(x):
    return jnp.sum(x, axis=0, keepdims=True)


def middle_kernel(
    dims,
    att_ref,
    hidden_ref,
    cot_ref,
    par_ref,
    wout_ref,
    wout_o_ref,
    wup_ref,
    wdn_ref,
    wdn_o_ref,
    bup_ref,
    bup_o_ref,
    result_ref,
    dfirst_ref,
    datt_ref,
    gdn_ref,
    gup_ref,
    gout_ref,
    stats_ref,
    gbup_ref,
    wout_v,
    wup_v,
    wdn_v,
    attp,
    fa,
    da,
    dfa,
    act,
    slope,
    dup,
    stage,
    recv,
    normed_v,
    first_v,
    dnorm_v,
    gdn_v,
    gdn_r,
    gup_v,
    gup_r,
    gout_v,
    gout_r,
    gb_v,
    gb_r,
    dattst,
    ap_ss,
    ap_rs,
    sc_ss,
    sc_rs,
    ag_ss,
    ag_rs,
    gx_ss,
    gx_rs,
    dx_ss,
    dx_rs,
    loc,
):
    S, n, C, L, D, hc, F1 = dims
    Dn, F2, Ph = D // n, 2 * F1, C * L
    z = lax.axis_index("seq")
    s = lax.axis_index("shard")
    core = lax.rem(s, 2)
    chip = s // 2
    other = 1 - core
    partner = (z, 2 * chip + other)

    loads = [
        pltpu.make_async_copy(wout_ref, wout_v.at[core], loc.at[0]),
        pltpu.make_async_copy(wout_o_ref, wout_v.at[other], loc.at[1]),
        pltpu.make_async_copy(wup_ref, wup_v, loc.at[2]),
        pltpu.make_async_copy(wdn_ref, wdn_v.at[core], loc.at[3]),
        pltpu.make_async_copy(wdn_o_ref, wdn_v.at[other], loc.at[4]),
    ]
    for load in loads:
        load.start()

    def peer(j):
        return (z, 2 * flip(chip, j, C) + core)

    barrier = pltpu.get_barrier_semaphore()
    pl.semaphore_signal(barrier, inc=1, device_id=partner, device_id_type=MESH)
    for j in range(1, C):
        pl.semaphore_signal(barrier, inc=1, device_id=peer(j), device_id_type=MESH)
    pl.semaphore_wait(barrier, C)

    def put_stat(row, value):
        for i in range(n):
            stats_ref[i, row : row + 1] = value[:, i * hc : (i + 1) * hc]

    def give(i, src, dst):
        remote(src, dst, gx_ss.at[i], gx_rs.at[i], partner).start()

    def taken(i, src, dst):
        await_recv(dst, gx_rs.at[i], partner)

    def spread(r, buf):
        for j in range(C - 1, 0, -1):
            remote(buf.at[chip], buf.at[chip], ag_ss.at[r, j], ag_rs.at[r, j], peer(j)).start()

    def arrived(r, buf, j):
        @pl.when(j > 0)
        def _():
            c = flip(chip, j, C)
            await_recv(buf.at[c], ag_rs.at[r, j], (z, 2 * c + core))

    def hand(r, j, part):
        stage[r, j] = part.astype(BF16)
        remote(stage.at[r, j], recv.at[r, j], sc_ss.at[r, j], sc_rs.at[r, j], peer(j)).start()

    def collected(r, total):
        for j in range(1, C):
            await_recv(recv.at[r, j], sc_rs.at[r, j], peer(j))
            total = total + recv[r, j].astype(F32)
        return total

    par = jnp.concatenate([par_ref[i] for i in range(n)], axis=1)
    b_out, gain1, shift1 = par[0:1], par[1:2], par[2:3]
    b_down, gain2, shift2 = par[3:4], par[4:5], par[5:6]

    remote(att_ref.at[:, other], attp, ap_ss.at[0], ap_rs.at[0], partner).start()
    loads[0].wait()
    loads[1].wait()
    await_recv(attp, ap_rs.at[0], partner)

    def out_part(j):
        c = flip(chip, j, C)
        return rows_dot(att_ref[c, core], wout_v[core]) + rows_dot(attp[c], wout_v[other])

    def out_step(k, carry):
        hand(0, C - 1 - k, out_part(C - 1 - k))
        return carry

    lax.fori_loop(0, C - 1, out_step, 0)
    first_sum = collected(0, out_part(0) + hidden_ref[...] + b_out)
    normed_one, inverse_one = layer_stats(first_sum)
    normed_v[...] = normed_one
    first_norm = normed_one * gain1 + shift1
    first_v[...] = first_norm
    fa[chip] = first_norm.astype(BF16)
    spread(0, fa)

    loads[2].wait()
    loads[3].wait()
    loads[4].wait()
    first_core = core == 0
    bup_mine, bup_theirs = bup_ref[...], bup_o_ref[...]
    bias_up = jnp.concatenate(
        [jnp.where(first_core, bup_mine, bup_theirs), jnp.where(first_core, bup_theirs, bup_mine)],
        axis=1,
    )

    def up_part(j):
        c = flip(chip, j, C)
        pre = rows_dot(fa[c], wup_v[...].reshape(D, F2)) + bias_up
        half = 0.5 * (1.0 + lax.erf(pre * root_half))
        act[c] = (pre * half).astype(BF16)
        slope[c] = half + pre * jnp.exp(-0.5 * pre * pre) * inv_root_two_pi
        return rows_dot(act[c], wdn_v[...].reshape(F2, D))

    own = up_part(0)

    def up_step(j, carry):
        arrived(0, fa, j)
        hand(1, j, up_part(j))
        return carry

    lax.fori_loop(1, C, up_step, 0)
    second_sum = collected(1, own + first_v[...] + b_down)
    normed_two, inverse_two = layer_stats(second_sum)
    result_ref[...] = (normed_two * gain2 + shift2).astype(BF16)
    grad_rows = cot_ref[...].astype(F32)
    put_stat(0, col_sum(grad_rows * normed_two))
    put_stat(1, col_sum(grad_rows))
    d_second = layer_back(grad_rows * gain2, normed_two, inverse_two)
    put_stat(2, col_sum(d_second))
    dnorm_v[...] = d_second
    da[chip] = d_second.astype(BF16)
    spread(1, da)

    def down_back(j):
        c = flip(chip, j, C)
        d_up = rows_dot_t(da[c], wdn_v[...].reshape(F2, D)) * slope[c]
        gb_v[...] += col_sum(d_up)
        dup[c] = d_up.astype(BF16)
        return rows_dot_t(dup[c], wup_v[...].reshape(D, F2))

    gb_v[...] = jnp.zeros_like(gb_v)
    own = down_back(0)

    def back_step(j, carry):
        arrived(1, da, j)
        hand(2, j, down_back(j))
        return carry

    lax.fori_loop(1, C, back_step, 0)
    dnorm_v[...] = dnorm_v[...] + own

    tile = 256
    da_all = da[...].reshape(Ph, D)

    def down_grad(t, carry):
        cols = pl.ds(pl.multiple_of(t * tile, tile), tile)
        gdn_v[pl.ds(pl.multiple_of(t * tile, tile), tile), :] = cols_dot(
            act[:, :, cols].reshape(Ph, tile), da_all
        ).astype(BF16)
        return carry

    lax.fori_loop(0, F2 // tile, down_grad, 0)
    half_rows = pl.ds(pl.multiple_of(other * F1, F1), F1)
    give(0, gdn_v.at[half_rows], gdn_r)

    d_first_norm = collected(2, dnorm_v[...])
    normed_one = normed_v[...]
    put_stat(3, col_sum(d_first_norm * normed_one))
    put_stat(4, col_sum(d_first_norm))
    d_first = layer_back(d_first_norm * gain1, normed_one, inverse_one)
    put_stat(5, col_sum(d_first))
    stats_ref[:, 6:8] = jnp.zeros((n, 2, hc), F32)
    dfirst_ref[...] = d_first
    dfa[chip] = d_first.astype(BF16)
    spread(2, dfa)

    def up_grad(c, carry):
        cols = pl.ds(pl.multiple_of(c * 2 * Dn, 128), 2 * Dn)
        res = cols_dot(fa[:, :, cols].reshape(Ph, 2 * Dn), dup[...].reshape(Ph, F2)).astype(BF16)
        gup_v[c, 0] = res[:Dn]
        gup_v[c, 1] = res[Dn:]
        return carry

    lax.fori_loop(0, C, up_grad, 0)
    give(1, gup_v.at[:, other], gup_r)
    gb_r[0] = jnp.where(first_core, gb_v[:, F1:], gb_v[:, :F1])
    give(2, gb_r.at[0], gb_r.at[1])

    def att_back(j, carry):
        arrived(2, dfa, j)
        c = flip(chip, j, C)
        datt_ref[c, core] = rows_dot_t(dfa[c], wout_v[core]).astype(BF16)
        dattst[j] = rows_dot_t(dfa[c], wout_v[other]).astype(BF16)
        remote(dattst.at[j], datt_ref.at[c, core], dx_ss.at[j], dx_rs.at[j], partner).start()
        return carry

    lax.fori_loop(0, C, att_back, 0)
    dfa_all = dfa[...].reshape(Ph, D)
    gout_v[0] = cols_dot(attp[...].reshape(Ph, hc), dfa_all).astype(BF16)
    give(3, gout_v.at[0], gout_r)
    gout_v[1] = cols_dot(att_ref[:, core].reshape(Ph, hc), dfa_all).astype(BF16)

    taken(0, None, gdn_r)
    own_rows = pl.ds(pl.multiple_of(core * F1, F1), F1)
    gdn_ref[...] = (gdn_v[own_rows, :].astype(F32) + gdn_r[...].astype(F32)).astype(BF16)
    taken(1, None, gup_r)
    gup_ref[...] = (gup_v[:, core].astype(F32) + gup_r[...].astype(F32)).astype(BF16)
    taken(2, None, gb_r.at[1])
    gbup_ref[...] = jnp.where(first_core, gb_v[:, :F1], gb_v[:, F1:]) + gb_r[1]
    taken(3, None, gout_r)
    gout_ref[...] = (gout_v[1].astype(F32) + gout_r[...].astype(F32)).astype(BF16)

    await_send(attp, ap_ss.at[0], partner)
    await_send(gdn_r, gx_ss.at[0], partner)
    await_send(gup_r, gx_ss.at[1], partner)
    await_send(gb_r.at[0], gx_ss.at[2], partner)
    await_send(gout_r, gx_ss.at[3], partner)

    def settle(j, carry):
        c = flip(chip, j, C)
        await_recv(datt_ref.at[c, other], dx_rs.at[j], partner)
        await_send(dattst.at[j], dx_ss.at[j], partner)

        @pl.when(j > 0)
        def _():
            for r in range(3):
                await_send(stage.at[r, j], sc_ss.at[r, j], peer(j))
            await_send(fa.at[chip], ag_ss.at[0, j], peer(j))
            await_send(da.at[chip], ag_ss.at[1, j], peer(j))
            await_send(dfa.at[chip], ag_ss.at[2, j], peer(j))

        return carry

    lax.fori_loop(0, C, settle, 0)


def middle_call(S, n, att, hidden, cot, par, wout, wout_o, wup2, wdn, wdn_o, bup, bup_o):
    C = n // 2
    L, D = hidden.shape
    hc = D // n
    F1 = wdn.shape[0]
    F2 = 2 * F1
    dims = (S, n, C, L, D, hc, F1)
    dma = pltpu.SemaphoreType.DMA
    vm = pl.BlockSpec(memory_space=pltpu.VMEM)
    anyw = pl.BlockSpec(memory_space=pl.ANY)
    sds = jax.ShapeDtypeStruct
    Dn = D // n
    return pl.pallas_call(
        functools.partial(middle_kernel, dims),
        out_shape=(
            sds((L, D), BF16),
            sds((L, D), F32),
            sds((C, 2, L, hc), BF16),
            sds((F1, D), BF16),
            sds((C, Dn, F2), BF16),
            sds((hc, D), BF16),
            sds((n, 8, hc), F32),
            sds((1, F1), F32),
        ),
        in_specs=[vm, vm, vm, vm, anyw, anyw, anyw, anyw, anyw, vm, vm],
        out_specs=(vm,) * 8,
        scratch_shapes=[
            pltpu.VMEM((2, hc, D), BF16),
            pltpu.VMEM((n, Dn, F2), BF16),
            pltpu.VMEM((2, F1, D), BF16),
            pltpu.VMEM((C, L, hc), BF16),
            pltpu.VMEM((C, L, D), BF16),
            pltpu.VMEM((C, L, D), BF16),
            pltpu.VMEM((C, L, D), BF16),
            pltpu.VMEM((C, L, F2), BF16),
            pltpu.VMEM((C, L, F2), F32),
            pltpu.VMEM((C, L, F2), BF16),
            pltpu.VMEM((3, C, L, D), BF16),
            pltpu.VMEM((3, C, L, D), BF16),
            pltpu.VMEM((L, D), F32),
            pltpu.VMEM((L, D), F32),
            pltpu.VMEM((L, D), F32),
            pltpu.VMEM((F2, D), BF16),
            pltpu.VMEM((F1, D), BF16),
            pltpu.VMEM((C, 2, Dn, F2), BF16),
            pltpu.VMEM((C, Dn, F2), BF16),
            pltpu.VMEM((2, hc, D), BF16),
            pltpu.VMEM((hc, D), BF16),
            pltpu.VMEM((1, F2), F32),
            pltpu.VMEM((2, 1, F1), F32),
            pltpu.VMEM((C, L, hc), BF16),
            dma((1,)),
            dma((1,)),
            dma((3, C)),
            dma((3, C)),
            dma((3, C)),
            dma((3, C)),
            dma((4,)),
            dma((4,)),
            dma((C,)),
            dma((C,)),
            dma((5,)),
        ],
        compiler_params=pltpu.CompilerParams(
            collective_id=1, has_side_effects=True, vmem_limit_bytes=VMEM_LIMIT
        ),
        name="middle_stage",
    )(att, hidden, cot, par, wout, wout_o, wup2, wdn, wdn_o, bup, bup_o)


def exit_kernel(
    dims,
    dq_ref,
    dkv_ref,
    hid_ref,
    wq_ref,
    dfirst_ref,
    stats_ref,
    gbup_ref,
    ginp_ref,
    dh_ref,
    gqkv_ref,
    small_ref,
    gbo_ref,
    zr,
    own3,
    got3,
    x6,
    stage,
    recv,
    dhb,
    gq_v,
    gq_r,
    st_r,
    st_v,
    zst,
    zgb,
    zk_ss,
    zk_rs,
    x_ss,
    x_rs,
    sc_ss,
    sc_rs,
    st_ss,
    st_rs,
    zs_ss,
    zs_rs,
    gq_ss,
    gq_rs,
    zl_ss,
    zl_rs,
    ag_ss,
    ag_rs,
    pf_ss,
    pf_rs,
    loc,
):
    S, n, C, L, D, hc, F1 = dims
    Dn, Ph = D // n, C * L
    z = lax.axis_index("seq")
    s = lax.axis_index("shard")
    core = lax.rem(s, 2)
    chip = s // 2
    other = 1 - core
    twin = 2 * chip + other
    partner = (z, twin)
    first_core = core == 0

    def peer(j):
        return (z, 2 * flip(chip, j, C) + core)

    barrier = pltpu.get_barrier_semaphore()
    for d in range(1, n):
        pl.semaphore_signal(barrier, inc=1, device_id=(z, flip(s, d, n)), device_id_type=MESH)
    for d in range(1, S):
        pl.semaphore_signal(barrier, inc=1, device_id=(lax.rem(z + d, S), s), device_id_type=MESH)
    pl.semaphore_wait(barrier, n - 1 + S - 1)

    for j in range(C - 1, -1, -1):
        c = flip(chip, j, C)

        @pl.when(z > 0)
        def _():
            remote(
                dkv_ref.at[0, c], zr.at[1, c], zk_ss.at[j, 0], zk_rs.at[j, 1], (z - 1, s)
            ).start()

        @pl.when(z < S - 1)
        def _():
            remote(
                dkv_ref.at[2, c], zr.at[0, c], zk_ss.at[j, 1], zk_rs.at[j, 0], (z + 1, s)
            ).start()

    st_r[s] = stats_ref[s]
    for d in range(1, n):
        to = flip(s, d, n)
        remote(stats_ref.at[to], st_r.at[s], st_ss.at[d], st_rs.at[d], (z, to)).start()

    def fold(k, carry):
        j = C - 1 - k
        c = flip(chip, j, C)
        whole = dkv_ref[1, c].astype(F32)

        @pl.when(z > 0)
        def _():
            await_recv(zr.at[0, c], zk_rs.at[j, 0], (z - 1, s))

        @pl.when(z < S - 1)
        def _():
            await_recv(zr.at[1, c], zk_rs.at[j, 1], (z + 1, s))

        whole = whole + jnp.where(z > 0, zr[0, c].astype(F32), 0.0)
        whole = whole + jnp.where(z < S - 1, zr[1, c].astype(F32), 0.0)
        whole = whole.astype(BF16)
        own3[c, :, :, :hc] = dq_ref[c]
        own3[c, :, :, hc:] = whole
        remote(own3.at[c, other], got3.at[c], x_ss.at[j], x_rs.at[j], partner).start()
        sums = jnp.sum(own3[c].astype(F32), axis=(0, 1), keepdims=False)
        st_v[0:1] += sums[None, :hc]
        st_v[1:2] += sums[None, 2 * hc :]
        return carry

    st_v[...] = jnp.zeros_like(st_v)
    lax.fori_loop(0, C, fold, 0)

    def partial(j):
        c = flip(chip, j, C)
        await_recv(got3.at[c], x_rs.at[j], partner)
        mine, theirs = own3[c, core], got3[c]
        low = jnp.where(first_core, mine, theirs)
        high = jnp.where(first_core, theirs, mine)
        pieces = []
        for part in range(3):
            pieces += [low[:, part * hc : (part + 1) * hc], high[:, part * hc : (part + 1) * hc]]
        x6[c] = jnp.concatenate(pieces, axis=1)
        return rows_dot_t(x6[c], wq_ref[...].reshape(D, 6 * hc))

    def scatter(k, carry):
        j = C - 1 - k
        stage[j] = partial(j).astype(BF16)
        remote(stage.at[j], recv.at[j], sc_ss.at[j], sc_rs.at[j], peer(j)).start()
        return carry

    lax.fori_loop(0, C - 1, scatter, 0)
    total = partial(0) + dfirst_ref[...]

    def qkv_grad(c, carry):
        cols = pl.ds(pl.multiple_of(c * 2 * Dn, 128), 2 * Dn)
        res = cols_dot(hid_ref[:, :, cols].reshape(Ph, 2 * Dn), x6[...].reshape(Ph, 6 * hc))
        gq_v[c, 0] = res[:Dn].astype(BF16)
        gq_v[c, 1] = res[Dn:].astype(BF16)
        return carry

    lax.fori_loop(0, C, qkv_grad, 0)
    remote(gq_v.at[:, other], gq_r, gq_ss.at[0], gq_rs.at[0], partner).start()

    sums = st_r[s]
    for d in range(1, n):
        src = flip(s, d, n)
        await_recv(st_r.at[src], st_rs.at[d], (z, src))
    sums = st_r[0]
    for i in range(1, n):
        sums = sums + st_r[i]
    zst[z] = sums
    zst[z, 6:8] = st_v[...]
    zgb[z] = gbup_ref[...]
    for d in range(1, S):
        to = (lax.rem(z + d, S), s)
        remote(zst.at[z], zst.at[z], zs_ss.at[d, 0], zs_rs.at[d, 0], to).start()
        remote(zgb.at[z], zgb.at[z], zs_ss.at[d, 1], zs_rs.at[d, 1], to).start()

    for j in range(1, C):
        await_recv(recv.at[j], sc_rs.at[j], peer(j))
        total = total + recv[j].astype(F32)
    ginp = total.astype(BF16)
    ginp_ref[...] = ginp
    dhb[...] = ginp
    keep = pltpu.make_async_copy(dhb, dh_ref.at[z, s], loc.at[0])
    keep.start()

    def broadcast(src, at):
        for j in range(C - 1, 0, -1):
            remote(src, dh_ref.at[at, s], ag_ss.at[at, j], ag_rs.at[at, j], peer(j)).start()
        remote(src, dh_ref.at[at, s], pf_ss.at[at, 0], pf_rs.at[at, 0], partner).start()

    @pl.when(z < S - 1)
    def _():
        remote(dhb, dh_ref.at[z, s], zl_ss.at[z, 0], zl_rs.at[z, 0], (z + 1, s)).start()

    @pl.when(z > 0)
    def _():
        remote(dhb, dh_ref.at[z, s], zl_ss.at[z, 1], zl_rs.at[z, 1], (z - 1, s)).start()

    broadcast(dhb, z)
    for d in range(1, S):

        @pl.when(z - d >= 0)
        def _():
            at = z - d
            await_recv(dh_ref.at[at, s], zl_rs.at[at, 0], (z - 1, s))

            @pl.when(z < S - 1)
            def _():
                remote(
                    dh_ref.at[at, s], dh_ref.at[at, s], zl_ss.at[at, 0], zl_rs.at[at, 0], (z + 1, s)
                ).start()

            broadcast(dh_ref.at[at, s], at)

        @pl.when(z + d <= S - 1)
        def _():
            at = z + d
            await_recv(dh_ref.at[at, s], zl_rs.at[at, 1], (z + 1, s))

            @pl.when(z > 0)
            def _():
                remote(
                    dh_ref.at[at, s], dh_ref.at[at, s], zl_ss.at[at, 1], zl_rs.at[at, 1], (z - 1, s)
                ).start()

            broadcast(dh_ref.at[at, s], at)

    def relay(at):
        for j in range(1, C):
            src = 2 * flip(chip, j, C) + core
            await_recv(dh_ref.at[at, src], ag_rs.at[at, j], (z, src))
            remote(
                dh_ref.at[at, src], dh_ref.at[at, src], pf_ss.at[at, j], pf_rs.at[at, j], partner
            ).start()

    relay(z)
    for d in range(1, S):

        @pl.when(z - d >= 0)
        def _():
            relay(z - d)

        @pl.when(z + d <= S - 1)
        def _():
            relay(z + d)

    await_recv(gq_r, gq_rs.at[0], partner)
    gqkv_ref[...] = (gq_v[:, core].astype(F32) + gq_r[...].astype(F32)).astype(BF16)
    for d in range(1, S):
        src = lax.rem(z + S - d, S)
        await_recv(zst.at[src], zs_rs.at[d, 0], (src, s))
        await_recv(zgb.at[src], zs_rs.at[d, 1], (src, s))
    small, big = zst[0], zgb[0]
    for i in range(1, S):
        small = small + zst[i]
        big = big + zgb[i]
    small_ref[...] = small
    gbo_ref[...] = big

    keep.wait()

    def settle_plane(at, carry):
        for j in range(C):
            src = 2 * flip(chip, j, C) + other
            await_recv(dh_ref.at[at, src], pf_rs.at[at, j], partner)
            await_send(dhb, pf_ss.at[at, j], partner)
            if j > 0:
                await_send(dhb, ag_ss.at[at, j], peer(j))
        return carry

    lax.fori_loop(0, S, settle_plane, 0)
    for at in range(S):

        @pl.when((z >= at) & (z < S - 1))
        def _():
            await_send(dhb, zl_ss.at[at, 0], (z + 1, s))

        @pl.when((z <= at) & (z > 0))
        def _():
            await_send(dhb, zl_ss.at[at, 1], (z - 1, s))

    for j in range(C):

        @pl.when(z > 0)
        def _():
            await_send(zr.at[0, 0], zk_ss.at[j, 0], (z - 1, s))

        @pl.when(z < S - 1)
        def _():
            await_send(zr.at[0, 0], zk_ss.at[j, 1], (z + 1, s))

        await_send(got3.at[0], x_ss.at[j], partner)
        if j > 0:
            await_send(stage.at[j], sc_ss.at[j], peer(j))
    for d in range(1, n):
        await_send(st_r.at[s], st_ss.at[d], (z, flip(s, d, n)))
    for d in range(1, S):
        to = (lax.rem(z + d, S), s)
        await_send(zst.at[z], zs_ss.at[d, 0], to)
        await_send(zgb.at[z], zs_ss.at[d, 1], to)
    await_send(gq_r, gq_ss.at[0], partner)


def exit_call(S, n, dq, dkv, hid_half, wq, dfirst, stats, gbup):
    C = n // 2
    L, D = dfirst.shape
    hc = D // n
    F1 = gbup.shape[1]
    Dn = D // n
    dims = (S, n, C, L, D, hc, F1)
    dma = pltpu.SemaphoreType.DMA
    vm = pl.BlockSpec(memory_space=pltpu.VMEM)
    anyw = pl.BlockSpec(memory_space=pl.ANY)
    sds = jax.ShapeDtypeStruct
    return pl.pallas_call(
        functools.partial(exit_kernel, dims),
        out_shape=(
            sds((L, D), BF16),
            sds((S, n, L, D), BF16),
            sds((C, Dn, 6 * hc), BF16),
            sds((8, hc), F32),
            sds((1, F1), F32),
        ),
        in_specs=[vm] * 7,
        out_specs=(vm, anyw, vm, vm, vm),
        scratch_shapes=[
            pltpu.VMEM((2, C, 2, L, 2 * hc), BF16),
            pltpu.VMEM((C, 2, L, 3 * hc), BF16),
            pltpu.VMEM((C, L, 3 * hc), BF16),
            pltpu.VMEM((C, L, 6 * hc), BF16),
            pltpu.VMEM((C, L, D), BF16),
            pltpu.VMEM((C, L, D), BF16),
            pltpu.VMEM((L, D), BF16),
            pltpu.VMEM((C, 2, Dn, 6 * hc), BF16),
            pltpu.VMEM((C, Dn, 6 * hc), BF16),
            pltpu.VMEM((n, 8, hc), F32),
            pltpu.VMEM((2, hc), F32),
            pltpu.VMEM((S, 8, hc), F32),
            pltpu.VMEM((S, 1, F1), F32),
            dma((C, 2)),
            dma((C, 2)),
            dma((C,)),
            dma((C,)),
            dma((C,)),
            dma((C,)),
            dma((n,)),
            dma((n,)),
            dma((S, 2)),
            dma((S, 2)),
            dma((1,)),
            dma((1,)),
            dma((S, 2)),
            dma((S, 2)),
            dma((S, C)),
            dma((S, C)),
            dma((S, C)),
            dma((S, C)),
            dma((1,)),
        ],
        compiler_params=pltpu.CompilerParams(
            collective_id=2, has_side_effects=True, vmem_limit_bytes=VMEM_LIMIT
        ),
        name="exit_stage",
    )(dq, dkv, hid_half, wq, dfirst, stats, gbup)


def table_kernel(dims, base_ref, pos_ref, dh_ref, out_ref, buf, sems):
    S, P_, R, D, rt = dims
    base = base_ref[0, 0]

    def load(at, slot):
        return pltpu.make_async_copy(dh_ref.at[at], buf.at[slot], sems.at[slot])

    load(0, 0).start()
    for at in range(S):
        slot = at % 2
        if at + 1 < S:
            load(at + 1, 1 - slot).start()
        load(at, slot).wait()

        def rows_tile(t, carry):
            start = pl.multiple_of(t * rt, rt)
            ids = lax.broadcasted_iota(jnp.int32, (rt, P_), 0) + (start + base)
            hot = jnp.where(ids == pos_ref[at], 1.0, 0.0).astype(BF16)
            part = rows_dot(hot, buf[slot])
            if at == 0:
                out_ref[pl.ds(start, rt), :] = part
            else:
                out_ref[pl.ds(start, rt), :] += part
            return carry

        lax.fori_loop(0, R // rt, rows_tile, 0)


def table_call(S, n, R, base, pos, dh):
    L, D = dh.shape[2:]
    P_ = n * L
    vm = pl.BlockSpec(memory_space=pltpu.VMEM)
    sm = pl.BlockSpec(memory_space=pltpu.SMEM)
    anyw = pl.BlockSpec(memory_space=pl.ANY)
    return pl.pallas_call(
        functools.partial(table_kernel, (S, P_, R, D, 256)),
        out_shape=jax.ShapeDtypeStruct((R, D), F32),
        in_specs=[sm, vm, anyw],
        out_specs=vm,
        scratch_shapes=[pltpu.VMEM((2, P_, D), BF16), pltpu.SemaphoreType.DMA((2,))],
        compiler_params=pltpu.CompilerParams(vmem_limit_bytes=VMEM_LIMIT),
        name="table_stage",
    )(base, pos.reshape(S, 1, P_), dh.reshape(S, P_, D))


def owner_kernel(
    dims, gup_ref, gqkv_ref, up_ref, qkv_ref, up_r, qkv_r, up_ss, up_rs, qk_ss, qk_rs
):
    n, C, D, hc, F2 = dims
    z = lax.axis_index("seq")
    s = lax.axis_index("shard")
    core = lax.rem(s, 2)
    chip = s // 2

    def peer(j):
        return (z, 2 * flip(chip, j, C) + core)

    barrier = pltpu.get_barrier_semaphore()
    for j in range(1, C):
        pl.semaphore_signal(barrier, inc=1, device_id=peer(j), device_id_type=MESH)
    pl.semaphore_wait(barrier, C - 1)
    for j in range(C - 1, 0, -1):
        c = flip(chip, j, C)
        remote(gup_ref.at[c], up_r.at[chip], up_ss.at[j], up_rs.at[j], peer(j)).start()
        remote(gqkv_ref.at[c], qkv_r.at[chip], qk_ss.at[j], qk_rs.at[j], peer(j)).start()
    up_r[chip] = gup_ref[chip]
    qkv_r[chip] = gqkv_ref[chip]
    for j in range(1, C):
        c = flip(chip, j, C)
        await_recv(up_r.at[c], up_rs.at[j], peer(j))
        await_recv(qkv_r.at[c], qk_rs.at[j], peer(j))
    h2 = 2 * hc
    for c in range(C):
        up_ref[:, c * F2 : (c + 1) * F2] = up_r[c].astype(F32)
        for part in range(3):
            qkv_ref[:, part * D + c * h2 : part * D + (c + 1) * h2] = qkv_r[
                c, :, part * h2 : (part + 1) * h2
            ].astype(F32)
    for j in range(1, C):
        await_send(up_r.at[chip], up_ss.at[j], peer(j))
        await_send(qkv_r.at[chip], qk_ss.at[j], peer(j))


def owner_call(n, gup, gqkv):
    C, Dn, F2 = gup.shape
    D = Dn * n
    hc = D // n
    vm = pl.BlockSpec(memory_space=pltpu.VMEM)
    dma = pltpu.SemaphoreType.DMA
    return pl.pallas_call(
        functools.partial(owner_kernel, (n, C, D, hc, F2)),
        out_shape=(
            jax.ShapeDtypeStruct((Dn, C * F2), F32),
            jax.ShapeDtypeStruct((Dn, 3 * D), F32),
        ),
        in_specs=[vm, vm],
        out_specs=(vm, vm),
        scratch_shapes=[
            pltpu.VMEM(gup.shape, BF16),
            pltpu.VMEM(gqkv.shape, BF16),
            dma((C,)),
            dma((C,)),
            dma((C,)),
            dma((C,)),
        ],
        compiler_params=pltpu.CompilerParams(
            collective_id=3, has_side_effects=True, vmem_limit_bytes=VMEM_LIMIT
        ),
        name="owner_stage",
    )(gup, gqkv)


QUERY_BLOCK = 256
KEY_BLOCK = 256


def local(
    inputs,
    positions,
    segments,
    pos_table,
    w_qkv,
    b_query,
    b_value,
    w_out,
    b_out,
    ln1_gain,
    ln1_bias,
    w_up,
    b_up,
    w_down,
    b_down,
    ln2_gain,
    ln2_bias,
    cotangent,
):
    S, n = lax.axis_size("seq"), lax.axis_size("shard")
    L, D = inputs.shape
    P_, hc, C = L * n, D // n, n // 2
    R = pos_table.shape[0]
    par = jnp.stack(
        [b_out, ln1_gain, ln1_bias, b_down, ln2_gain, ln2_bias, b_query, b_value]
    ).astype(F32)
    bup = b_up.astype(F32)[None, :]
    q, kv, hid_half, hidden, wq, wup2, wdn_o, wout_o, par_all, bup_o, pos_glob = entry_call(
        S, n, positions[None, :], inputs, pos_table, w_qkv, w_up, w_down, w_out, par, bup
    )
    bounds, lohi = ranges(segments, P_, QUERY_BLOCK, KEY_BLOCK)
    q = q.reshape(P_, hc)
    kv = kv.reshape(3 * P_, 2 * hc)
    att, lse = attend_call(q, kv, bounds, lohi, QUERY_BLOCK, KEY_BLOCK)
    result, dfirst, datt, gdn, gup, gout, stats, gbup = middle_call(
        S,
        n,
        att.reshape(C, 2, L, hc),
        hidden,
        cotangent,
        par_all,
        w_out,
        wout_o,
        wup2,
        w_down,
        wdn_o,
        bup,
        bup_o,
    )
    gdn, gup, gout = lax.psum((gdn, gup, gout), "seq")
    dq, dkv = attend_back_call(
        q, kv, bounds, lohi, att, datt.reshape(P_, hc), lse, QUERY_BLOCK, KEY_BLOCK
    )
    ginp, dh, gqkv, small, gbo = exit_call(
        S,
        n,
        dq.reshape(C, 2, L, hc),
        dkv.reshape(3, C, 2, L, 2 * hc),
        hid_half,
        wq,
        dfirst,
        stats,
        gbup,
    )
    gqkv = lax.psum(gqkv, "seq")
    base = (lax.axis_index("shard") * R).astype(jnp.int32).reshape(1, 1)
    gtable = table_call(S, n, R, base, pos_glob, dh)
    up, qkv = owner_call(n, gup, gqkv)
    return (
        result,
        ginp,
        gtable,
        qkv,
        small[6],
        small[7],
        gout.astype(F32),
        small[5],
        small[3],
        small[4],
        up,
        gbo[0],
        gdn.astype(F32),
        small[2],
        small[0],
        small[1],
    )


def solution(mesh):
    in_specs = (
        P(("seq", "shard"), None),
        P(("seq", "shard")),
        P(),
        P("shard", None),
        P("shard", None),
        P("shard"),
        P("shard"),
        P("shard", None),
        P("shard"),
        P("shard"),
        P("shard"),
        P("shard", None),
        P("shard"),
        P("shard", None),
        P("shard"),
        P("shard"),
        P("shard"),
        P(("seq", "shard"), None),
    )
    out_specs = (
        P(("seq", "shard"), None),
        P(("seq", "shard"), None),
        P("shard", None),
        P("shard", None),
        P("shard"),
        P("shard"),
        P("shard", None),
        P("shard"),
        P("shard"),
        P("shard"),
        P("shard", None),
        P("shard"),
        P("shard", None),
        P("shard"),
        P("shard"),
        P("shard"),
    )
    return jax.shard_map(local, mesh=mesh, in_specs=in_specs, out_specs=out_specs, check_vma=False)
```

time: 1750 us -> 446 us (0.25)
  waiting for transfers between devices: 1010 us -> 103 us
  Pallas kernels: 0 us -> 307 us
  matrix products: 198 us -> 0 us
  local copies, waits for them, and re-layouts: 171 us -> 6.68 us
  blocking collectives: 148 us -> 0 us
  other arithmetic: 148 us -> 10.8 us
  loops' own time: 27.4 us -> 0 us
  starting transfers between devices: 26.4 us -> 0.04 us
    reduce_scatter x4 -> x0, waiting for transfers between devices: 530 us -> none  [the longest x1 231 us: local(): lax.psum_scatter(lax.map(one_owner, owners).reshape(lax.axis_size('shard'...]
    pallas_call x0 -> x7, Pallas kernels: none -> 307 us  [the longest x1 88.6 us: exit_call(): pl.pallas_call(functools.partial(exit_kernel, dims), out_shape=(sds((L, D...]
    psum x1, waiting for transfers between devices: 316 us -> 103 us  [local(): gdn, gup, gout = lax.psum((gdn, gup, gout), 'seq')]
    dot_general x75 -> x0, matrix products: 198 us -> none  [the longest x16 45.7 us: block_scores(): jnp.einsum('qhd,khd->hqk', query_three, key_block, preferred_element_type...]
    all_gather x7 -> x0, waiting for transfers between devices: 131 us -> none  [the longest x1 92.3 us: local(): lax.all_gather(pos_table, 'shard', axis=0, tiled=True)]
    all_gather x9 -> x0, blocking collectives: 76.1 us -> none  [the longest x1 8.97 us: local(): lax.all_gather(b_out, 'shard', axis=0, tiled=True)]
    slice x14 -> x2, local copies, waits for them, and re-layouts: 53.1 us -> 0.18 us  [ranges(): bounds = jnp.stack([low[::bq] // bk, (high[bq - 1::bq] + bk - 1) // bk])]
    dynamic_update_slice x32 -> x0, local copies, waits for them, and re-layouts: 48.4 us -> none  [the longest x16 24.2 us: backward_one_block(): lax.dynamic_update_slice_in_dim(grad_value_all, value_part, offset, 0)]
  transfers between devices with their start and end apart: 18 -> 1, of which waited for: 11 -> 1; matrix products, arithmetic and copies ran while one was open for 11% -> 0% of each run, Pallas kernels for 0% -> 4%
where the time goes in v1:
time: 446 us; the launch traced here: 442 us
  Pallas kernels  307 us (69%)
  waiting for transfers between devices  103 us (23%)
  between operations  14.2 us (3%)
  other arithmetic  10.8 us (2%)
  local copies, waits for them, and re-layouts  6.68 us (1%)
    psum x1, waiting for transfers between devices, local(): gdn, gup, gout = lax.psum((gdn, gup, gout), 'seq')  103 us
    pallas_call x1, Pallas kernels, exit_call(): pl.pallas_call(functools.partial(exit_kernel, dims), out_shape=(sds((L, D...  88.6 us
    pallas_call x1, Pallas kernels, middle_call(): pl.pallas_call(functools.partial(middle_kernel, dims), out_shape=(sds((L,...  87.9 us
    pallas_call x1, Pallas kernels, entry_call(): pl.pallas_call(functools.partial(entry_kernel, dims), out_shape=(sds((C,...  59.8 us
    pallas_call x1, Pallas kernels, owner_call(): pl.pallas_call(functools.partial(owner_kernel, (n, C, D, hc, F2)), out_sh...  26.6 us
    pallas_call x1, Pallas kernels, table_call(): pl.pallas_call(functools.partial(table_kernel, (S, P_, R, D, 256)), out_s...  15.8 us
    pallas_call x1, Pallas kernels, attend_back_call(): pl.pallas_call(functools.partial(attend_back_kernel, (P_, hc, hh, bq, bk)...  15.4 us
    pallas_call x1, Pallas kernels, attend_call(): pl.pallas_call(functools.partial(attend_kernel, (P_, hc, hh, bq, bk)), ou...  13.2 us
  transfers between devices with their start and end apart: 1, of which 1 were waited for; matrix products, arithmetic and copies ran while one was open for 0% of the time, Pallas kernels for 4%

profile of v1, /device:TPU:0, one launch (start us, length us, event | category | flops | bytes accessed | tf_op | source)
XLA Modules:
  0.0 442.0 jit_solution(12196804585033488886)
XLA Ops:
  7.2 0.8 stack.52
  8.0 0.6 convert_element_type.18.par_ref
  8.6 1.3 broadcast_in_dim.15
  9.9 0.7 dynamic_slice.3
  10.6 4.3 convert_reduce_fusion.1
  14.9 0.1 slice.31
  15.1 0.6 pad_add_fusion.1.bounds_ref
  15.7 0.6 pad_add_fusion.lohi_ref
  16.3 59.8 %entry_stage.1 = (bf16[4,2,128,128]{3,2,1,0:T(8,128)(2,1)}, bf16[3,4,2,128,256]{4,3,2,1,0:T(8,128)(2,1)}, bf16[4,128,1024]{2,1,0:T(8,128)(2,1)}, f32[128,1024]{1...) custom-call(s32[1,128]{1,0:T(1,128)} %bitcast.57, ...), custom_call_target="tpu_custom_call" | custom-call | tf_op jit(solution)/shard_map/entry_stage/pallas_call | solution.py:398
  76.1 13.2 %attend_stage.1 = (bf16[1024,128]{1,0:T(8,128)(2,1)}, f32[2,1024]{1,0:T(2,128)}) custom-call(s32[2,4]{1,0:T(2,128)} %pad_add_fusion.1.bounds_ref, bf16[1024,128]{1,0:T(8,128)(2,1)} %bitcast.46, bf16[3072,256]{1,0:T(8,128)(2,1)} %bitcast.43, s32[2,1024]{1,0:T(2,128)} %pad_add_fusion.lohi_ref), custom_call_target="tpu_custom_call" | custom-call | tf_op jit(solution)/shard_map/attend_stage/pallas_call | solution.py:519
  89.3 87.9 %middle_stage.1 = (bf16[128,1024]{1,0:T(8,128)(2,1)}, f32[128,1024]{1,0:T(8,128)}, bf16[4,2,128,128]{3,2,1,0:T(8,128)(2,1)}, bf16[512,1024]{1,0:T(8,128)(2,1)}, ...) custom-call(bf16[4,2,128,128]{3,2,1,0:T(8,128)(2,1)} %bitcast.48, ...), custom_call_target="tpu_custom_call" | custom-call | tf_op jit(solution)/shard_map/middle_stage/pallas_call | solution.py:935
  177.2 15.4 %attend_back_stage.1 = (bf16[1024,128]{1,0:T(8,128)(2,1)}, bf16[3072,256]{1,0:T(8,128)(2,1)}) custom-call(s32[2,4]{1,0:T(2,128)} %pad_add_fusion.1.bounds_ref, bf16[1024,128]{1,0:T(8,128)(2,1)} %bitcast.47, bf16[3072,256]{1,0:T(8,128)(2,1)} %bitcast.44, s32[2,1024]{1,0:T(2,128)} %pad_add_fusion.lohi_ref, bf16[1024,128]{1,0:T(8,128)(2,1)} %get-tuple-element.48.att_ref, ...), custom_call_target="tpu_custom_call" | custom-call | tf_op jit(solution)/shard_map/attend_back_stage/pallas_call | solution.py:598
  192.6 88.6 %exit_stage.1 = (bf16[128,1024]{1,0:T(8,128)(2,1)}, bf16[4,8,128,1024]{3,2,1,0:T(8,128)(2,1)}, bf16[4,128,768]{2,1,0:T(8,128)(2,1)}, f32[8,128]{1,0:T(8,128)}, f32[1,512]{1,0:T(1,128)}) custom-call(bf16[4,2,128,128]{3,2,1,0:T(8,128)(2,1)} %bitcast.50, bf16[3,4,2,128,256]{4,3,2,1,0:T(8,128)(2,1)} %bitcast.45, ...), custom_call_target="tpu_custom_call" | custom-call | tf_op jit(solution)/shard_map/exit_stage/pallas_call | solution.py:1292
  281.3 15.8 %table_stage.1 = f32[1024,1024]{1,0:T(8,128)} custom-call(s32[1,1]{1,0:T(1,128)} %bitcast.20.base_ref, s32[4,1,1024]{2,1,0:T(1,128)} %bitcast.53, bf16[4,1024,1024]{2,1,0:T(8,128)(2,1)} %bitcast.42), custom_call_target="tpu_custom_call" | custom-call | tf_op jit(solution)/shard_map/table_stage/pallas_call | solution.py:1378
  297.1 0.5 slice_bitcast_fusion
  297.6 103.1 %all-reduce.3.cloned.1.call-done = (bf16[4,128,1024]{2,1,0:T(8,128)(2,1)}, bf16[4,128,768]{2,1,0:T(8,128)(2,1)}, bf16[128,1024]{1,0:T(8,128)(2,1)}, bf16[512,1024]{1,0:T(8,128)(2,1)}) async-done(((bf16[4,128,1024]{2,1,0:T(8,128)(2,1)}, bf16[4,128,768]{2,1,0:T(8,128)(2,1)}, bf16[128,1024]{1,0:T(8,128)(2,1)}, bf16[512,1024]{1,0:T(8,128)(2,1)}), (bf16[4,128,1024]{2,1,0:T(8,128)(2,1)}, ...) | async-done | bytes 3145744 | tf_op jit(solution)/shard_map/psum | solution.py:1510
  400.7 1.9 convert_element_type.19
  402.6 26.6 %owner_stage.1 = (f32[128,4096]{1,0:T(8,128)}, f32[128,3072]{1,0:T(8,128)}) custom-call(bf16[4,128,1024]{2,1,0:T(8,128)(2,1)} %get-tuple-element.78.gup_ref, bf16[4,128,768]{2,1,0:T(8,128)(2,1)} %get-tuple-element.79.gqkv_ref), custom_call_target="tpu_custom_call" | custom-call | tf_op jit(solution)/shard_map/owner_stage/pallas_call | solution.py:1433
  429.2 1.6 convert_element_type.20
  430.7 0.7 copy.43
  431.4 0.7 copy.44
  432.2 1.1 copy.45
  433.3 1.3 copy.46
  434.6 0.6 copy.47
  (20 shorter events, 0.2 us)
Async XLA Ops:
  7.2 393.5 %all-reduce.3.cloned.1.call-start = ((), (), s32[]{:S(2)}) async-start(), calls=%async_computation | async-start | bytes 6291456 | tf_op jit(solution)/shard_map/psum | solution.py:1510
  281.3 15.8 %copy-start.5 = (f32[8,128]{1,0:T(8,128)S(1)}, f32[8,128]{1,0:T(8,128)}, u32[]{:S(2)}) copy-start(f32[8,128]{1,0:T(8,128)} %get-tuple-element.71) | copy-start | bytes 12292
  400.7 28.5 %copy-start.2 = (bf16[512,1024]{1,0:T(8,128)(2,1)S(1)}, bf16[512,1024]{1,0:T(8,128)(2,1)}, u32[]{:S(2)}) copy-start(bf16[512,1024]{1,0:T(8,128)(2,1)} %get-tuple-element.81) | copy-start | bytes 3145732
  402.6 28.2 %copy-start.3 = (bf16[128,1024]{1,0:T(8,128)(2,1)S(1)}, bf16[128,1024]{1,0:T(8,128)(2,1)}, u32[]{:S(2)}) copy-start(bf16[128,1024]{1,0:T(8,128)(2,1)} %get-tuple-element.108) | copy-start | bytes 786436
  429.1 2.3 copy-start.4
  429.2 3.0 copy-start.1
  430.7 2.6 copy-start
  433.3 1.3 copy-start.6
Sparse Core Ops, SparseCore 0:
  281.4 119.2 all-reduce.2

commit v2 on v1

--- a/solution.py
+++ b/solution.py
@@ -50,6 +50,100 @@
     remote(src, src, sem, sem, device).wait_send()
 
 
+class Chain:
+    def __init__(self, S, z, s, own, land, cross, fin, sems, lag=3):
+        self.S, self.s, self.lag, self.sems = S, s, lag, sems
+        self.own, self.land, self.cross, self.fin = own, land, cross, fin
+        low = 1 - (2 * z) // S
+        self.depth = low * z + (1 - low) * (S - 1 - z)
+        self.inward = (z + 2 * low - 1, s)
+        self.outward = (z + 1 - 2 * low, s)
+        self.mid = S // 2 - 1
+        self.pieces = own.shape[0]
+        self.slots = self.pieces + lag * self.mid + lag * max(self.mid - 1, 0)
+
+    def give_out(self, start, stop):
+        @pl.when(self.depth == 0)
+        def _():
+            def step(p, carry):
+                remote(
+                    self.own.at[p], self.land.at[p], self.sems.at[0, p], self.sems.at[1, p], self.inward
+                ).start()
+                return carry
+
+            lax.fori_loop(start, stop, step, 0)
+
+    def slot(self, k):
+        p = k - self.lag * (self.depth - 1)
+
+        @pl.when((self.depth > 0) & (p >= 0) & (p < self.pieces))
+        def _():
+            await_recv(self.land.at[p], self.sems.at[1, p], self.outward)
+            both = self.own[p].astype(F32) + self.land[p].astype(F32)
+            self.own[p] = both.astype(BF16)
+
+            @pl.when(self.depth < self.mid)
+            def _():
+                remote(
+                    self.own.at[p], self.land.at[p], self.sems.at[0, p], self.sems.at[1, p], self.inward
+                ).start()
+
+            @pl.when(self.depth == self.mid)
+            def _():
+                remote(
+                    self.own.at[p], self.cross.at[p], self.sems.at[2, p], self.sems.at[3, p], self.inward
+                ).start()
+
+        x = k - self.lag * self.mid
+
+        @pl.when((self.depth == self.mid) & (x >= 0) & (x < self.pieces))
+        def _():
+            await_recv(self.cross.at[x], self.sems.at[3, x], self.inward)
+            both = self.own[x].astype(F32) + self.cross[x].astype(F32)
+            self.fin[x] = both.astype(BF16)
+            remote(
+                self.fin.at[x], self.fin.at[x], self.sems.at[4, x], self.sems.at[5, x], self.outward
+            ).start()
+
+        b = k - self.lag * self.mid - self.lag * (self.mid - self.depth)
+
+        @pl.when((self.depth < self.mid) & (self.depth > 0) & (b >= 0) & (b < self.pieces))
+        def _():
+            await_recv(self.fin.at[b], self.sems.at[5, b], self.inward)
+            remote(
+                self.fin.at[b], self.fin.at[b], self.sems.at[4, b], self.sems.at[5, b], self.outward
+            ).start()
+
+    def run(self, start, stop):
+        def step(k, carry):
+            self.slot(k)
+            return carry
+
+        lax.fori_loop(start, stop, step, 0)
+
+    def settle(self):
+        def step(p, carry):
+            @pl.when(self.depth == 0)
+            def _():
+                await_recv(self.fin.at[p], self.sems.at[5, p], self.inward)
+
+            @pl.when(self.depth < self.mid)
+            def _():
+                await_send(self.own.at[p], self.sems.at[0, p], self.inward)
+
+            @pl.when(self.depth == self.mid)
+            def _():
+                await_send(self.own.at[p], self.sems.at[2, p], self.inward)
+
+            @pl.when(self.depth > 0)
+            def _():
+                await_send(self.fin.at[p], self.sems.at[4, p], self.outward)
+
+            return carry
+
+        lax.fori_loop(0, self.pieces, step, 0)
+
+
 def rows_dot(a, b):
     return lax.dot_general(a, b, (((1,), (0,)), ((), ())), preferred_element_type=F32)
 
@@ -71,8 +165,16 @@
     wup_ref,
     wdn_ref,
     wout_ref,
-    par_ref,
-    bup_ref,
+    seg_ref,
+    bup_in_ref,
+    row0_ref,
+    row1_ref,
+    row2_ref,
+    row3_ref,
+    row4_ref,
+    row5_ref,
+    row6_ref,
+    row7_ref,
     q_ref,
     kv_ref,
     hid_half_ref,
@@ -82,8 +184,9 @@
     wdn_o_ref,
     wout_o_ref,
     par_all_ref,
-    bup_o_ref,
+    bup2_ref,
     pos_glob_ref,
+    lohi_ref,
     table_v,
     pstage,
     precv,
@@ -92,7 +195,8 @@
     qst,
     kvst,
     wup_own,
-    wq_tmp,
+    par_ref,
+    bup_ref,
     pos_ss,
     pos_rs,
     par_ss,
@@ -148,6 +252,15 @@
     )
     own_wup_in.start()
 
+    rows = (row0_ref, row1_ref, row2_ref, row3_ref, row4_ref, row5_ref, row6_ref, row7_ref)
+    for i, row in enumerate(rows):
+        par_ref[i : i + 1] = row[...].astype(F32)
+    bup_ref[...] = bup_in_ref[...].astype(F32)
+    F1 = F2 // 2
+    bup_mine = pl.ds(pl.multiple_of(core * F1, 128), F1)
+    bup_theirs = pl.ds(pl.multiple_of(other * F1, 128), F1)
+    bup2_ref[:, bup_mine] = bup_ref[...]
+
     barrier = pltpu.get_barrier_semaphore()
     for d in range(1, n):
         pl.semaphore_signal(barrier, inc=1, device_id=(z, flip(s, d, n)), device_id_type=MESH)
@@ -184,6 +297,24 @@
                 (z, 2 * pc + core),
             ).start()
     remote(wq_ref.at[s], wq_ref.at[s], wqf_ss.at[0], wqf_rs.at[0], (z, partner)).start()
+
+    own_segs = jnp.concatenate([seg_ref[z * n + i] for i in range(n)], axis=1)
+
+    def count(g, carry):
+        low, high = carry
+        keys = jnp.broadcast_to(seg_ref[g], (L, L)).T
+        lows, highs = [], []
+        for i in range(n):
+            mine = own_segs[:, i * L : (i + 1) * L]
+            lows.append(jnp.sum(jnp.where(keys < mine, 1.0, 0.0), axis=0, keepdims=True))
+            highs.append(jnp.sum(jnp.where(keys <= mine, 1.0, 0.0), axis=0, keepdims=True))
+        return low + jnp.concatenate(lows, axis=1), high + jnp.concatenate(highs, axis=1)
+
+    none = jnp.zeros((1, n * L), F32)
+    low, high = lax.fori_loop(0, S * n, count, (none, none))
+    origin = ((z - 1) * n * L).astype(F32)
+    lohi_ref[0:1] = low - origin
+    lohi_ref[1:2] = high - origin
 
     for d in range(1, n):
         src = flip(s, d, n)
@@ -266,7 +397,7 @@
     remote(wup_own, wup2_ref.at[s], wupf_ss.at[0], wupf_rs.at[0], (z, partner)).start()
     remote(wdn_ref, wdn_o_ref, misc_ss.at[0], misc_rs.at[0], (z, partner)).start()
     remote(wout_ref, wout_o_ref, misc_ss.at[1], misc_rs.at[1], (z, partner)).start()
-    remote(bup_ref, bup_o_ref, misc_ss.at[2], misc_rs.at[2], (z, partner)).start()
+    remote(bup_ref, bup2_ref.at[:, bup_mine], misc_ss.at[2], misc_rs.at[2], (z, partner)).start()
 
     for j in range(C):
         src = 2 * flip(chip, j, C) + other
@@ -376,14 +507,14 @@
         await_recv(pos_glob_ref.at[src], posz_rs.at[d], (src, s))
         await_send(pos_glob_ref.at[z], posz_ss.at[d], (lax.rem(z + d, S), s))
     for i, (mine, got) in enumerate(
-        ((wdn_ref, wdn_o_ref), (wout_ref, wout_o_ref), (bup_ref, bup_o_ref))
+        ((wdn_ref, wdn_o_ref), (wout_ref, wout_o_ref), (bup_ref, bup2_ref.at[:, bup_theirs]))
     ):
         await_recv(got, misc_rs.at[i], (z, partner))
         await_send(mine, misc_ss.at[i], (z, partner))
     own_wup_out.wait()
 
 
-def entry_call(S, n, pos, inp, table, wqkv, wup, wdn, wout, par, bup):
+def entry_call(S, n, pos, inp, table, wqkv, wup, wdn, wout, seg, bup, rows):
     C = n // 2
     L, D = inp.shape
     hc = D // n
@@ -407,11 +538,12 @@
             sds((F1, D), BF16),
             sds((D // n, D), BF16),
             sds((n, 8, hc), F32),
-            sds((1, F1), F32),
+            sds((1, F2), F32),
             sds((S, n, 1, L), jnp.int32),
+            sds((2, n * L), F32),
         ),
-        in_specs=[vm, vm, anyw, anyw, anyw, anyw, anyw, vm, vm],
-        out_specs=(vm, vm, vm, vm, vm, anyw, anyw, anyw, vm, vm, vm),
+        in_specs=[vm, vm, anyw, anyw, anyw, anyw, anyw] + [vm] * 10,
+        out_specs=(vm, vm, vm, vm, vm, anyw, anyw, anyw, vm, vm, vm, vm),
         scratch_shapes=[
             pltpu.VMEM((R, D), BF16),
             pltpu.VMEM((C, L, D), BF16),
@@ -421,7 +553,8 @@
             pltpu.VMEM((C, L, hc), BF16),
             pltpu.VMEM((C, L, 2 * hc), BF16),
             pltpu.VMEM((D // n, F2), BF16),
-            pltpu.VMEM((8, 128), BF16),
+            pltpu.VMEM((8, hc), F32),
+            pltpu.VMEM((1, F1), F32),
             dma((n,)),
             dma((n,)),
             dma((n,)),
@@ -454,10 +587,16 @@
             collective_id=0, has_side_effects=True, vmem_limit_bytes=VMEM_LIMIT
         ),
         name="entry_stage",
-    )(pos, inp, table, wqkv, wup, wdn, wout, par, bup)
-
-
-def attend_kernel(dims, bounds_ref, q_ref, kv_ref, lohi_ref, att_ref, lse_ref, vt_ref):
+    )(pos, inp, table, wqkv, wup, wdn, wout, seg, bup, *rows)
+
+
+def key_blocks(lohi_ref, rows, bk):
+    first = jnp.min(lohi_ref[0:1, rows]).astype(jnp.int32)
+    last = jnp.max(lohi_ref[1:2, rows]).astype(jnp.int32)
+    return first // bk, (last + bk - 1) // bk
+
+
+def attend_kernel(dims, q_ref, kv_ref, lohi_ref, att_ref, lse_ref, vt_ref):
     P_, hc, hh, bq, bk = dims
     lanes = lax.broadcasted_iota(jnp.int32, (bq, hc), 1) // HEAD_DIM
     nq = P_ // bq
@@ -467,13 +606,16 @@
         vt_ref[kb] = kv_ref[pl.ds(at, bk), hc:].T
         return carry
 
-    lax.fori_loop(bounds_ref[0, 0], bounds_ref[1, nq - 1], flip_value, 0)
+    first, last = key_blocks(lohi_ref, pl.ds(0, P_), bk)
+    lax.fori_loop(first, last, flip_value, 0)
 
     def one_query_block(qi, carry):
         rows = pl.ds(pl.multiple_of(qi * bq, bq), bq)
         query = q_ref[rows, :]
         heads_q = [jnp.where(lanes == h, query, jnp.zeros_like(query)) for h in range(hh)]
-        low, high = lohi_ref[0:1, rows], lohi_ref[1:2, rows]
+        low = lohi_ref[0:1, rows].astype(jnp.int32)
+        high = lohi_ref[1:2, rows].astype(jnp.int32)
+        first, last = key_blocks(lohi_ref, rows, bk)
 
         def one_key_block(kb, state):
             at = pl.multiple_of(kb * bk, bk)
@@ -501,7 +643,7 @@
             )
             for _ in range(hh)
         )
-        state = lax.fori_loop(bounds_ref[0, qi], bounds_ref[1, qi], one_key_block, start)
+        state = lax.fori_loop(first, last, one_key_block, start)
         mixed = jnp.concatenate([acc / total for _, total, acc in state], axis=0)
         att_ref[rows, :] = mixed.T.astype(BF16)
         for h in range(hh):
@@ -511,27 +653,26 @@
     lax.fori_loop(0, nq, one_query_block, 0)
 
 
-def attend_call(q, kv, bounds, lohi, bq, bk):
+def attend_call(q, kv, lohi, bq, bk):
     P_, hc = q.shape
     hh = hc // HEAD_DIM
     vm = pl.BlockSpec(memory_space=pltpu.VMEM)
-    sm = pl.BlockSpec(memory_space=pltpu.SMEM)
     return pl.pallas_call(
         functools.partial(attend_kernel, (P_, hc, hh, bq, bk)),
         out_shape=(
             jax.ShapeDtypeStruct((P_, hc), BF16),
             jax.ShapeDtypeStruct((hh, P_), F32),
         ),
-        in_specs=[sm, vm, vm, vm],
+        in_specs=[vm, vm, vm],
         out_specs=(vm, vm),
         scratch_shapes=[pltpu.VMEM((3 * P_ // bk, hc, bk), BF16)],
         compiler_params=pltpu.CompilerParams(vmem_limit_bytes=VMEM_LIMIT),
         name="attend_stage",
-    )(bounds, q, kv, lohi)
+    )(q, kv, lohi)
 
 
 def attend_back_kernel(
-    dims, bounds_ref, q_ref, kv_ref, lohi_ref, att_ref, datt_ref, lse_ref, dq_ref, dkv_ref, kt_ref, acc_ref
+    dims, q_ref, kv_ref, lohi_ref, att_ref, datt_ref, lse_ref, dq_ref, dkv_ref, kt_ref, acc_ref
 ):
     P_, hc, hh, bq, bk = dims
     lanes = lax.broadcasted_iota(jnp.int32, (bq, hc), 1) // HEAD_DIM
@@ -543,7 +684,8 @@
         kt_ref[kb] = kv_ref[pl.ds(at, bk), :hc].T
         return carry
 
-    lax.fori_loop(bounds_ref[0, 0], bounds_ref[1, nq - 1], flip_key, 0)
+    first, last = key_blocks(lohi_ref, pl.ds(0, P_), bk)
+    lax.fori_loop(first, last, flip_key, 0)
 
     def one_query_block(qi, carry):
         rows = pl.ds(pl.multiple_of(qi * bq, bq), bq)
@@ -559,7 +701,9 @@
             for h in range(hh)
         ]
         logs = [lse_ref[h : h + 1, rows] for h in range(hh)]
-        low, high = lohi_ref[0:1, rows], lohi_ref[1:2, rows]
+        low = lohi_ref[0:1, rows].astype(jnp.int32)
+        high = lohi_ref[1:2, rows].astype(jnp.int32)
+        first, last = key_blocks(lohi_ref, rows, bk)
 
         def one_key_block(kb, state):
             at = pl.multiple_of(kb * bk, bk)
@@ -582,7 +726,7 @@
             return tuple(fresh)
 
         start = tuple(jnp.zeros((HEAD_DIM, bq), F32) for _ in range(hh))
-        state = lax.fori_loop(bounds_ref[0, qi], bounds_ref[1, qi], one_key_block, start)
+        state = lax.fori_loop(first, last, one_key_block, start)
         dq_ref[rows, :] = (jnp.concatenate(state, axis=0).T * score_scale).astype(BF16)
         return carry
 
@@ -590,18 +734,17 @@
     dkv_ref[...] = acc_ref[...].astype(BF16)
 
 
-def attend_back_call(q, kv, bounds, lohi, att, datt, lse, bq, bk):
+def attend_back_call(q, kv, lohi, att, datt, lse, bq, bk):
     P_, hc = q.shape
     hh = hc // HEAD_DIM
     vm = pl.BlockSpec(memory_space=pltpu.VMEM)
-    sm = pl.BlockSpec(memory_space=pltpu.SMEM)
     return pl.pallas_call(
         functools.partial(attend_back_kernel, (P_, hc, hh, bq, bk)),
         out_shape=(
             jax.ShapeDtypeStruct((P_, hc), BF16),
             jax.ShapeDtypeStruct((3 * P_, 2 * hc), BF16),
         ),
-        in_specs=[sm, vm, vm, vm, vm, vm, vm],
+        in_specs=[vm, vm, vm, vm, vm, vm],
         out_specs=(vm, vm),
         scratch_shapes=[
             pltpu.VMEM((3 * P_ // bk, hc, bk), BF16),
@@ -609,17 +752,7 @@
         ],
         compiler_params=pltpu.CompilerParams(vmem_limit_bytes=VMEM_LIMIT),
         name="attend_back_stage",
-    )(bounds, q, kv, lohi, att, datt, lse)
-
-
-def ranges(segments, P_, bq, bk):
-    z = lax.axis_index("seq")
-    own = lax.dynamic_slice_in_dim(segments, z * P_, P_)
-    low = jnp.sum((segments[:, None] < own[None, :]).astype(jnp.int32), axis=0) - (z - 1) * P_
-    high = jnp.sum((segments[:, None] <= own[None, :]).astype(jnp.int32), axis=0) - (z - 1) * P_
-    lohi = jnp.stack([low, high])
-    bounds = jnp.stack([low[::bq] // bk, (high[bq - 1 :: bq] + bk - 1) // bk])
-    return bounds, lohi
+    )(q, kv, lohi, att, datt, lse)
 
 
 def layer_stats(summed):
@@ -650,7 +783,6 @@
     wdn_ref,
     wdn_o_ref,
     bup_ref,
-    bup_o_ref,
     result_ref,
     dfirst_ref,
     datt_ref,
@@ -659,6 +791,7 @@
     gout_ref,
     stats_ref,
     gbup_ref,
+    gdn_done_ref,
     wout_v,
     wup_v,
     wdn_v,
@@ -676,6 +809,10 @@
     dnorm_v,
     gdn_v,
     gdn_r,
+    gdn_h,
+    gdn_l,
+    gdn_x,
+    gdn_f,
     gup_v,
     gup_r,
     gout_v,
@@ -693,6 +830,7 @@
     gx_rs,
     dx_ss,
     dx_rs,
+    zsem,
     loc,
 ):
     S, n, C, L, D, hc, F1 = dims
@@ -721,7 +859,9 @@
     pl.semaphore_signal(barrier, inc=1, device_id=partner, device_id_type=MESH)
     for j in range(1, C):
         pl.semaphore_signal(barrier, inc=1, device_id=peer(j), device_id_type=MESH)
-    pl.semaphore_wait(barrier, C)
+    for d in (1, S - 1):
+        pl.semaphore_signal(barrier, inc=1, device_id=(lax.rem(z + d, S), s), device_id_type=MESH)
+    pl.semaphore_wait(barrier, C + 2)
 
     def put_stat(row, value):
         for i in range(n):
@@ -783,11 +923,7 @@
     loads[3].wait()
     loads[4].wait()
     first_core = core == 0
-    bup_mine, bup_theirs = bup_ref[...], bup_o_ref[...]
-    bias_up = jnp.concatenate(
-        [jnp.where(first_core, bup_mine, bup_theirs), jnp.where(first_core, bup_theirs, bup_mine)],
-        axis=1,
-    )
+    bias_up = bup_ref[...]
 
     def up_part(j):
         c = flip(chip, j, C)
@@ -838,17 +974,41 @@
     tile = 256
     da_all = da[...].reshape(Ph, D)
 
-    def down_grad(t, carry):
+    per_half = F1 // tile
+    per_tile = gdn_v.shape[1] // per_half
+
+    def down_grad(i, carry):
+        t = lax.rem(i + other * per_half, 2 * per_half)
         cols = pl.ds(pl.multiple_of(t * tile, tile), tile)
-        gdn_v[pl.ds(pl.multiple_of(t * tile, tile), tile), :] = cols_dot(
-            act[:, :, cols].reshape(Ph, tile), da_all
-        ).astype(BF16)
-        return carry
-
-    lax.fori_loop(0, F2 // tile, down_grad, 0)
-    half_rows = pl.ds(pl.multiple_of(other * F1, F1), F1)
-    give(0, gdn_v.at[half_rows], gdn_r)
-
+        res = cols_dot(act[:, :, cols].reshape(Ph, tile), da_all).astype(BF16)
+        gdn_v[t // per_half, pl.ds(lax.rem(t, per_half) * per_tile, per_tile)] = res.reshape(
+            per_tile, tile // per_tile, D
+        )
+        return carry
+
+    lax.fori_loop(0, per_half, down_grad, 0)
+    give(0, gdn_v.at[other], gdn_r)
+    lax.fori_loop(per_half, 2 * per_half, down_grad, 0)
+
+    def up_grad(c, carry):
+        cols = pl.ds(pl.multiple_of(c * 2 * Dn, 128), 2 * Dn)
+        res = cols_dot(fa[:, :, cols].reshape(Ph, 2 * Dn), dup[...].reshape(Ph, F2)).astype(BF16)
+        gup_v[c, 0] = res[:Dn]
+        gup_v[c, 1] = res[Dn:]
+        return carry
+
+    early = gdn_h.shape[0]
+    taken(0, None, gdn_r)
+    gdn_h[...] = (gdn_v[core, :early].astype(F32) + gdn_r[:early].astype(F32)).astype(BF16)
+    gdn_ref[...] = (gdn_v[core, early:].astype(F32) + gdn_r[early:].astype(F32)).astype(BF16)
+    chain = Chain(S, z, s, gdn_h, gdn_l, gdn_x, gdn_f, zsem)
+    chain.give_out(0, early)
+
+    lax.fori_loop(0, C, up_grad, 0)
+    give(1, gup_v.at[:, other], gup_r)
+    gb_r[0] = jnp.where(first_core, gb_v[:, F1:], gb_v[:, :F1])
+    give(2, gb_r.at[0], gb_r.at[1])
+    chain.run(0, 2)
     d_first_norm = collected(2, dnorm_v[...])
     normed_one = normed_v[...]
     put_stat(3, col_sum(d_first_norm * normed_one))
@@ -860,19 +1020,8 @@
     dfa[chip] = d_first.astype(BF16)
     spread(2, dfa)
 
-    def up_grad(c, carry):
-        cols = pl.ds(pl.multiple_of(c * 2 * Dn, 128), 2 * Dn)
-        res = cols_dot(fa[:, :, cols].reshape(Ph, 2 * Dn), dup[...].reshape(Ph, F2)).astype(BF16)
-        gup_v[c, 0] = res[:Dn]
-        gup_v[c, 1] = res[Dn:]
-        return carry
-
-    lax.fori_loop(0, C, up_grad, 0)
-    give(1, gup_v.at[:, other], gup_r)
-    gb_r[0] = jnp.where(first_core, gb_v[:, F1:], gb_v[:, :F1])
-    give(2, gb_r.at[0], gb_r.at[1])
-
     def att_back(j, carry):
+        chain.run(2 * j + 2, 2 * j + 4)
         arrived(2, dfa, j)
         c = flip(chip, j, C)
         datt_ref[c, core] = rows_dot_t(dfa[c], wout_v[core]).astype(BF16)
@@ -886,9 +1035,7 @@
     give(3, gout_v.at[0], gout_r)
     gout_v[1] = cols_dot(att_ref[:, core].reshape(Ph, hc), dfa_all).astype(BF16)
 
-    taken(0, None, gdn_r)
-    own_rows = pl.ds(pl.multiple_of(core * F1, F1), F1)
-    gdn_ref[...] = (gdn_v[own_rows, :].astype(F32) + gdn_r[...].astype(F32)).astype(BF16)
+    chain.run(2 * C + 2, chain.slots)
     taken(1, None, gup_r)
     gup_ref[...] = (gup_v[:, core].astype(F32) + gup_r[...].astype(F32)).astype(BF16)
     taken(2, None, gb_r.at[1])
@@ -896,6 +1043,8 @@
     taken(3, None, gout_r)
     gout_ref[...] = (gout_v[1].astype(F32) + gout_r[...].astype(F32)).astype(BF16)
 
+    chain.settle()
+    gdn_done_ref[...] = gdn_f[...]
     await_send(attp, ap_ss.at[0], partner)
     await_send(gdn_r, gx_ss.at[0], partner)
     await_send(gup_r, gx_ss.at[1], partner)
@@ -920,7 +1069,7 @@
     lax.fori_loop(0, C, settle, 0)
 
 
-def middle_call(S, n, att, hidden, cot, par, wout, wout_o, wup2, wdn, wdn_o, bup, bup_o):
+def middle_call(S, n, att, hidden, cot, par, wout, wout_o, wup2, wdn, wdn_o, bup):
     C = n // 2
     L, D = hidden.shape
     hc = D // n
@@ -932,20 +1081,22 @@
     anyw = pl.BlockSpec(memory_space=pl.ANY)
     sds = jax.ShapeDtypeStruct
     Dn = D // n
+    pc, early = 16, EARLY_PIECES
     return pl.pallas_call(
         functools.partial(middle_kernel, dims),
         out_shape=(
             sds((L, D), BF16),
             sds((L, D), F32),
             sds((C, 2, L, hc), BF16),
-            sds((F1, D), BF16),
+            sds((pc - early, F1 // pc, D), BF16),
             sds((C, Dn, F2), BF16),
             sds((hc, D), BF16),
             sds((n, 8, hc), F32),
             sds((1, F1), F32),
+            sds((early, F1 // pc, D), BF16),
         ),
-        in_specs=[vm, vm, vm, vm, anyw, anyw, anyw, anyw, anyw, vm, vm],
-        out_specs=(vm,) * 8,
+        in_specs=[vm, vm, vm, vm, anyw, anyw, anyw, anyw, anyw, vm],
+        out_specs=(vm,) * 9,
         scratch_shapes=[
             pltpu.VMEM((2, hc, D), BF16),
             pltpu.VMEM((n, Dn, F2), BF16),
@@ -962,8 +1113,12 @@
             pltpu.VMEM((L, D), F32),
             pltpu.VMEM((L, D), F32),
             pltpu.VMEM((L, D), F32),
-            pltpu.VMEM((F2, D), BF16),
-            pltpu.VMEM((F1, D), BF16),
+            pltpu.VMEM((2, pc, F1 // pc, D), BF16),
+            pltpu.VMEM((pc, F1 // pc, D), BF16),
+            pltpu.VMEM((early, F1 // pc, D), BF16),
+            pltpu.VMEM((early, F1 // pc, D), BF16),
+            pltpu.VMEM((early, F1 // pc, D), BF16),
+            pltpu.VMEM((early, F1 // pc, D), BF16),
             pltpu.VMEM((C, 2, Dn, F2), BF16),
             pltpu.VMEM((C, Dn, F2), BF16),
             pltpu.VMEM((2, hc, D), BF16),
@@ -981,13 +1136,14 @@
             dma((4,)),
             dma((C,)),
             dma((C,)),
+            dma((6, early)),
             dma((5,)),
         ],
         compiler_params=pltpu.CompilerParams(
             collective_id=1, has_side_effects=True, vmem_limit_bytes=VMEM_LIMIT
         ),
         name="middle_stage",
-    )(att, hidden, cot, par, wout, wout_o, wup2, wdn, wdn_o, bup, bup_o)
+    )(att, hidden, cot, par, wout, wout_o, wup2, wdn, wdn_o, bup)
 
 
 def exit_kernel(
@@ -999,9 +1155,17 @@
     dfirst_ref,
     stats_ref,
     gbup_ref,
+    pos_ref,
+    gupc_ref,
+    goutc_ref,
+    gdnc_ref,
     ginp_ref,
     dh_ref,
-    gqkv_ref,
+    gq_f,
+    up_f,
+    out_f,
+    dn_f,
+    gtable_ref,
     small_ref,
     gbo_ref,
     zr,
@@ -1013,6 +1177,21 @@
     dhb,
     gq_v,
     gq_r,
+    gq_s,
+    gq_o,
+    gq_l,
+    gq_x,
+    up_o,
+    up_l,
+    up_x,
+    out_o,
+    out_l,
+    out_x,
+    dn_o,
+    dn_l,
+    dn_x,
+    plane,
+    prod,
     st_r,
     st_v,
     zst,
@@ -1029,6 +1208,14 @@
     zs_rs,
     gq_ss,
     gq_rs,
+    gx_ss,
+    gx_rs,
+    ua_ss,
+    ua_rs,
+    qc,
+    uc,
+    oc,
+    dc,
     zl_ss,
     zl_rs,
     ag_ss,
@@ -1037,7 +1224,7 @@
     pf_rs,
     loc,
 ):
-    S, n, C, L, D, hc, F1 = dims
+    S, n, C, L, D, hc, F1, R, rt = dims
     Dn, Ph = D // n, C * L
     z = lax.axis_index("seq")
     s = lax.axis_index("shard")
@@ -1072,6 +1259,26 @@
             remote(
                 dkv_ref.at[2, c], zr.at[0, c], zk_ss.at[j, 1], zk_rs.at[j, 0], (z + 1, s)
             ).start()
+
+    quarter = Dn // 4
+    mine = pl.ds(4 * chip, 4)
+
+    def block_of(j):
+        return pl.ds(4 * flip(chip, j, C), 4)
+
+    for j in range(C - 1, 0, -1):
+        remote(
+            gupc_ref.at[flip(chip, j, C)], up_o.at[mine], ua_ss.at[j], ua_rs.at[j], peer(j)
+        ).start()
+    up_o[mine] = gupc_ref[chip]
+    out_o[...] = goutc_ref[...].reshape(4, quarter, D)
+    dn_o[...] = gdnc_ref[...]
+    wide = Chain(S, z, s, up_o, up_l, up_x, up_f, uc)
+    square = Chain(S, z, s, out_o, out_l, out_x, out_f, oc)
+    late = Chain(S, z, s, dn_o, dn_l, dn_x, dn_f, dc)
+    inner = Chain(S, z, s, gq_o, gq_l, gq_x, gq_f, qc)
+    late.give_out(0, late.pieces)
+    square.give_out(0, square.pieces)
 
     st_r[s] = stats_ref[s]
     for d in range(1, n):
@@ -1129,8 +1336,7 @@
     def qkv_grad(c, carry):
         cols = pl.ds(pl.multiple_of(c * 2 * Dn, 128), 2 * Dn)
         res = cols_dot(hid_ref[:, :, cols].reshape(Ph, 2 * Dn), x6[...].reshape(Ph, 6 * hc))
-        gq_v[c, 0] = res[:Dn].astype(BF16)
-        gq_v[c, 1] = res[Dn:].astype(BF16)
+        gq_v[c] = res.astype(BF16).reshape(2, 4, quarter, 6 * hc)
         return carry
 
     lax.fori_loop(0, C, qkv_grad, 0)
@@ -1152,6 +1358,18 @@
         remote(zgb.at[z], zgb.at[z], zs_ss.at[d, 1], zs_rs.at[d, 1], to).start()
 
     for j in range(1, C):
+        await_recv(up_o.at[block_of(j)], ua_rs.at[j], peer(j))
+    wide.give_out(0, wide.pieces // 2)
+    late.run(0, 6)
+    await_recv(gq_r, gq_rs.at[0], partner)
+    gq_s[...] = (gq_v[:, core].astype(F32) + gq_r[...].astype(F32)).astype(BF16)
+    for j in range(C - 1, 0, -1):
+        remote(
+            gq_s.at[flip(chip, j, C)], gq_o.at[mine], gx_ss.at[j], gx_rs.at[j], peer(j)
+        ).start()
+    gq_o[mine] = gq_s[chip]
+
+    for j in range(1, C):
         await_recv(recv.at[j], sc_rs.at[j], peer(j))
         total = total + recv[j].astype(F32)
     ginp = total.astype(BF16)
@@ -1174,6 +1392,9 @@
         remote(dhb, dh_ref.at[z, s], zl_ss.at[z, 1], zl_rs.at[z, 1], (z - 1, s)).start()
 
     broadcast(dhb, z)
+    late.run(6, late.slots)
+    square.run(0, square.slots)
+    wide.run(0, 2)
     for d in range(1, S):
 
         @pl.when(z - d >= 0)
@@ -1210,19 +1431,56 @@
                 dh_ref.at[at, src], dh_ref.at[at, src], pf_ss.at[at, j], pf_rs.at[at, j], partner
             ).start()
 
-    relay(z)
-    for d in range(1, S):
-
-        @pl.when(z - d >= 0)
-        def _():
-            relay(z - d)
-
-        @pl.when(z + d <= S - 1)
-        def _():
-            relay(z + d)
-
-    await_recv(gq_r, gq_rs.at[0], partner)
-    gqkv_ref[...] = (gq_v[:, core].astype(F32) + gq_r[...].astype(F32)).astype(BF16)
+    wide.give_out(wide.pieces // 2, wide.pieces)
+    for j in range(1, C):
+        await_recv(gq_o.at[block_of(j)], gx_rs.at[j], peer(j))
+    inner.give_out(0, inner.pieces)
+
+    def plane_sum(t, carry):
+        at = flip(z, t, S)
+        relay(at)
+
+        wide.run(2 + 6 * t, 8 + 6 * t)
+        inner.run(6 * (t - 1), 6 * t)
+
+        for j in range(C):
+            src = 2 * flip(chip, j, C) + other
+            await_recv(dh_ref.at[at, src], pf_rs.at[at, j], partner)
+
+        @pl.when(t == 0)
+        def _():
+            keep.wait()
+
+        load = pltpu.make_async_copy(dh_ref.at[at], plane, loc.at[1])
+        load.start()
+        load.wait()
+
+        def rows_tile(r, inner):
+            start = pl.multiple_of(r * rt, rt)
+            ids = lax.broadcasted_iota(jnp.int32, (rt, L), 0) + (start + s * R)
+            hot = jnp.concatenate(
+                [jnp.where(ids == pos_ref[at, i], 1.0, 0.0).astype(BF16) for i in range(n)], axis=1
+            )
+            prod[at, pl.ds(start, rt), :] = rows_dot(hot, plane[...].reshape(n * L, D))
+            return inner
+
+        lax.fori_loop(0, R // rt, rows_tile, 0)
+        return carry
+
+    lax.fori_loop(0, S, plane_sum, 0)
+
+    def add_tile(r, carry):
+        at = pl.ds(pl.multiple_of(r * rt, rt), rt)
+        rows = prod[0, at]
+        for i in range(1, S):
+            rows = rows + prod[i, at]
+        gtable_ref[at] = rows.astype(BF16)
+        return carry
+
+    lax.fori_loop(0, R // rt, add_tile, 0)
+
+    wide.run(2 + 6 * S, wide.slots)
+    inner.run(6 * (S - 1), inner.slots)
     for d in range(1, S):
         src = lax.rem(z + S - d, S)
         await_recv(zst.at[src], zs_rs.at[d, 0], (src, s))
@@ -1234,12 +1492,8 @@
     small_ref[...] = small
     gbo_ref[...] = big
 
-    keep.wait()
-
     def settle_plane(at, carry):
         for j in range(C):
-            src = 2 * flip(chip, j, C) + other
-            await_recv(dh_ref.at[at, src], pf_rs.at[at, j], partner)
             await_send(dhb, pf_ss.at[at, j], partner)
             if j > 0:
                 await_send(dhb, ag_ss.at[at, j], peer(j))
@@ -1275,16 +1529,24 @@
         to = (lax.rem(z + d, S), s)
         await_send(zst.at[z], zs_ss.at[d, 0], to)
         await_send(zgb.at[z], zs_ss.at[d, 1], to)
+    for j in range(1, C):
+        await_send(gq_s.at[chip], gx_ss.at[j], peer(j))
+        await_send(gupc_ref.at[chip], ua_ss.at[j], peer(j))
+    wide.settle()
+    square.settle()
+    late.settle()
+    inner.settle()
     await_send(gq_r, gq_ss.at[0], partner)
 
 
-def exit_call(S, n, dq, dkv, hid_half, wq, dfirst, stats, gbup):
+def exit_call(S, n, R, dq, dkv, hid_half, wq, dfirst, stats, gbup, pos, gupc, goutc, gdnc):
     C = n // 2
     L, D = dfirst.shape
     hc = D // n
     F1 = gbup.shape[1]
     Dn = D // n
-    dims = (S, n, C, L, D, hc, F1)
+    F2 = gupc.shape[3]
+    dims = (S, n, C, L, D, hc, F1, R, 256)
     dma = pltpu.SemaphoreType.DMA
     vm = pl.BlockSpec(memory_space=pltpu.VMEM)
     anyw = pl.BlockSpec(memory_space=pl.ANY)
@@ -1294,12 +1556,16 @@
         out_shape=(
             sds((L, D), BF16),
             sds((S, n, L, D), BF16),
-            sds((C, Dn, 6 * hc), BF16),
+            sds((4 * C, Dn // 4, 6 * hc), BF16),
+            sds((4 * C, Dn // 4, F2), BF16),
+            sds((4, Dn // 4, D), BF16),
+            sds(gdnc.shape, BF16),
+            sds((R, D), BF16),
             sds((8, hc), F32),
             sds((1, F1), F32),
         ),
-        in_specs=[vm] * 7,
-        out_specs=(vm, anyw, vm, vm, vm),
+        in_specs=[vm] * 11,
+        out_specs=(vm, anyw) + (vm,) * 7,
         scratch_shapes=[
             pltpu.VMEM((2, C, 2, L, 2 * hc), BF16),
             pltpu.VMEM((C, 2, L, 3 * hc), BF16),
@@ -1308,8 +1574,23 @@
             pltpu.VMEM((C, L, D), BF16),
             pltpu.VMEM((C, L, D), BF16),
             pltpu.VMEM((L, D), BF16),
-            pltpu.VMEM((C, 2, Dn, 6 * hc), BF16),
-            pltpu.VMEM((C, Dn, 6 * hc), BF16),
+            pltpu.VMEM((C, 2, 4, Dn // 4, 6 * hc), BF16),
+            pltpu.VMEM((C, 4, Dn // 4, 6 * hc), BF16),
+            pltpu.VMEM((C, 4, Dn // 4, 6 * hc), BF16),
+            pltpu.VMEM((4 * C, Dn // 4, 6 * hc), BF16),
+            pltpu.VMEM((4 * C, Dn // 4, 6 * hc), BF16),
+            pltpu.VMEM((4 * C, Dn // 4, 6 * hc), BF16),
+            pltpu.VMEM((4 * C, Dn // 4, F2), BF16),
+            pltpu.VMEM((4 * C, Dn // 4, F2), BF16),
+            pltpu.VMEM((4 * C, Dn // 4, F2), BF16),
+            pltpu.VMEM((4, Dn // 4, D), BF16),
+            pltpu.VMEM((4, Dn // 4, D), BF16),
+            pltpu.VMEM((4, Dn // 4, D), BF16),
+            pltpu.VMEM(gdnc.shape, BF16),
+            pltpu.VMEM(gdnc.shape, BF16),
+            pltpu.VMEM(gdnc.shape, BF16),
+            pltpu.VMEM((n, L, D), BF16),
+            pltpu.VMEM((S, R, D), F32),
             pltpu.VMEM((n, 8, hc), F32),
             pltpu.VMEM((2, hc), F32),
             pltpu.VMEM((S, 8, hc), F32),
@@ -1326,135 +1607,143 @@
             dma((S, 2)),
             dma((1,)),
             dma((1,)),
+            dma((C,)),
+            dma((C,)),
+            dma((C,)),
+            dma((C,)),
+            dma((6, 4 * C)),
+            dma((6, 4 * C)),
+            dma((6, 4)),
+            dma((6, gdnc.shape[0])),
             dma((S, 2)),
             dma((S, 2)),
             dma((S, C)),
             dma((S, C)),
             dma((S, C)),
             dma((S, C)),
-            dma((1,)),
+            dma((2,)),
         ],
         compiler_params=pltpu.CompilerParams(
             collective_id=2, has_side_effects=True, vmem_limit_bytes=VMEM_LIMIT
         ),
         name="exit_stage",
-    )(dq, dkv, hid_half, wq, dfirst, stats, gbup)
-
-
-def table_kernel(dims, base_ref, pos_ref, dh_ref, out_ref, buf, sems):
-    S, P_, R, D, rt = dims
-    base = base_ref[0, 0]
-
-    def load(at, slot):
-        return pltpu.make_async_copy(dh_ref.at[at], buf.at[slot], sems.at[slot])
-
-    load(0, 0).start()
-    for at in range(S):
-        slot = at % 2
-        if at + 1 < S:
-            load(at + 1, 1 - slot).start()
-        load(at, slot).wait()
-
-        def rows_tile(t, carry):
-            start = pl.multiple_of(t * rt, rt)
-            ids = lax.broadcasted_iota(jnp.int32, (rt, P_), 0) + (start + base)
-            hot = jnp.where(ids == pos_ref[at], 1.0, 0.0).astype(BF16)
-            part = rows_dot(hot, buf[slot])
-            if at == 0:
-                out_ref[pl.ds(start, rt), :] = part
-            else:
-                out_ref[pl.ds(start, rt), :] += part
-            return carry
-
-        lax.fori_loop(0, R // rt, rows_tile, 0)
-
-
-def table_call(S, n, R, base, pos, dh):
-    L, D = dh.shape[2:]
-    P_ = n * L
-    vm = pl.BlockSpec(memory_space=pltpu.VMEM)
-    sm = pl.BlockSpec(memory_space=pltpu.SMEM)
-    anyw = pl.BlockSpec(memory_space=pl.ANY)
+    )(dq, dkv, hid_half, wq, dfirst, stats, gbup, pos, gupc, goutc, gdnc)
+
+
+def finish_kernel(
+    dims,
+    table_ref,
+    gq_ref,
+    up_ref,
+    out_ref,
+    early_ref,
+    late_ref,
+    res_ref,
+    inp_ref,
+    small_ref,
+    gb_ref,
+    table_o,
+    gq_o,
+    up_o,
+    out_o,
+    dn_o,
+    res_o,
+    inp_o,
+    gb_o,
+    *small_o,
+):
+    C, D, hc = dims
+    i = pl.program_id(0)
+    h2 = 2 * hc
+    F2 = up_ref.shape[3]
+    table_o[...] = table_ref[...].astype(F32)
+    for c in range(C):
+        up_o[:, c * F2 : (c + 1) * F2] = up_ref[c, 0].astype(F32)
+        for part in range(3):
+            gq_o[:, part * D + c * h2 : part * D + (c + 1) * h2] = gq_ref[
+                c, 0, :, part * h2 : (part + 1) * h2
+            ].astype(F32)
+    out_o[...] = out_ref[0].astype(F32)
+    piece = early_ref.shape[0] * early_ref.shape[1]
+    dn_o[...] = jnp.where(i < 4, early_ref[...], late_ref[...]).reshape(piece, D).astype(F32)
+    res_o[...] = res_ref[...]
+    inp_o[...] = inp_ref[...]
+    gb_o[...] = gb_ref[...]
+    for r, o in enumerate(small_o):
+        o[...] = small_ref[r : r + 1]
+
+
+def finish_call(n, table, gq, up, out, early, late, res, inp, small, gb):
+    C = n // 2
+    R, D = table.shape
+    L = res.shape[0]
+    Dn = D // n
+    hc = Dn
+    q, F2 = up.shape[1:]
+    h = q // 2
+    piece = early.shape[1]
+    F1 = gb.shape[1]
+    sds = jax.ShapeDtypeStruct
+    steps = 8
+    two = lambda rows, cols: pl.BlockSpec((rows, cols), lambda i: (i, 0))
+    quad = lambda cols: pl.BlockSpec((C, 1, h, cols), lambda i: (0, i // 2, i % 2, 0))
+    fixed = lambda rows, cols: pl.BlockSpec((rows, cols), lambda i: (0, 0))
     return pl.pallas_call(
-        functools.partial(table_kernel, (S, P_, R, D, 256)),
-        out_shape=jax.ShapeDtypeStruct((R, D), F32),
-        in_specs=[sm, vm, anyw],
-        out_specs=vm,
-        scratch_shapes=[pltpu.VMEM((2, P_, D), BF16), pltpu.SemaphoreType.DMA((2,))],
+        functools.partial(finish_kernel, (C, D, hc)),
+        grid=(steps,),
+        out_shape=(
+            sds((R, D), F32),
+            sds((Dn, 3 * D), F32),
+            sds((Dn, C * F2), F32),
+            sds((Dn, D), F32),
+            sds((F1, D), F32),
+            sds((L, D), BF16),
+            sds((L, D), BF16),
+            sds((1, F1), F32),
+        )
+        + (sds((1, hc), F32),) * 8,
+        in_specs=[
+            two(R // steps, D),
+            quad(6 * hc),
+            quad(F2),
+            pl.BlockSpec((1, h, D), lambda i: (i // 2, i % 2, 0)),
+            pl.BlockSpec((2, piece, D), lambda i: (jnp.minimum(i, 3), 0, 0)),
+            pl.BlockSpec((2, piece, D), lambda i: (jnp.maximum(i - 4, 0), 0, 0)),
+            two(L // steps, D),
+            two(L // steps, D),
+            fixed(8, hc),
+            fixed(1, F1),
+        ],
+        out_specs=(
+            two(R // steps, D),
+            two(h, 3 * D),
+            two(h, C * F2),
+            two(h, D),
+            two(2 * piece, D),
+            two(L // steps, D),
+            two(L // steps, D),
+            fixed(1, F1),
+        )
+        + (fixed(1, hc),) * 8,
         compiler_params=pltpu.CompilerParams(vmem_limit_bytes=VMEM_LIMIT),
-        name="table_stage",
-    )(base, pos.reshape(S, 1, P_), dh.reshape(S, P_, D))
-
-
-def owner_kernel(
-    dims, gup_ref, gqkv_ref, up_ref, qkv_ref, up_r, qkv_r, up_ss, up_rs, qk_ss, qk_rs
-):
-    n, C, D, hc, F2 = dims
-    z = lax.axis_index("seq")
-    s = lax.axis_index("shard")
-    core = lax.rem(s, 2)
-    chip = s // 2
-
-    def peer(j):
-        return (z, 2 * flip(chip, j, C) + core)
-
-    barrier = pltpu.get_barrier_semaphore()
-    for j in range(1, C):
-        pl.semaphore_signal(barrier, inc=1, device_id=peer(j), device_id_type=MESH)
-    pl.semaphore_wait(barrier, C - 1)
-    for j in range(C - 1, 0, -1):
-        c = flip(chip, j, C)
-        remote(gup_ref.at[c], up_r.at[chip], up_ss.at[j], up_rs.at[j], peer(j)).start()
-        remote(gqkv_ref.at[c], qkv_r.at[chip], qk_ss.at[j], qk_rs.at[j], peer(j)).start()
-    up_r[chip] = gup_ref[chip]
-    qkv_r[chip] = gqkv_ref[chip]
-    for j in range(1, C):
-        c = flip(chip, j, C)
-        await_recv(up_r.at[c], up_rs.at[j], peer(j))
-        await_recv(qkv_r.at[c], qk_rs.at[j], peer(j))
-    h2 = 2 * hc
-    for c in range(C):
-        up_ref[:, c * F2 : (c + 1) * F2] = up_r[c].astype(F32)
-        for part in range(3):
-            qkv_ref[:, part * D + c * h2 : part * D + (c + 1) * h2] = qkv_r[
-                c, :, part * h2 : (part + 1) * h2
-            ].astype(F32)
-    for j in range(1, C):
-        await_send(up_r.at[chip], up_ss.at[j], peer(j))
-        await_send(qkv_r.at[chip], qk_ss.at[j], peer(j))
-
-
-def owner_call(n, gup, gqkv):
-    C, Dn, F2 = gup.shape
-    D = Dn * n
-    hc = D // n
-    vm = pl.BlockSpec(memory_space=pltpu.VMEM)
-    dma = pltpu.SemaphoreType.DMA
-    return pl.pallas_call(
-        functools.partial(owner_kernel, (n, C, D, hc, F2)),
-        out_shape=(
-            jax.ShapeDtypeStruct((Dn, C * F2), F32),
-            jax.ShapeDtypeStruct((Dn, 3 * D), F32),
-        ),
-        in_specs=[vm, vm],
-        out_specs=(vm, vm),
-        scratch_shapes=[
-            pltpu.VMEM(gup.shape, BF16),
-            pltpu.VMEM(gqkv.shape, BF16),
-            dma((C,)),
-            dma((C,)),
-            dma((C,)),
-            dma((C,)),
-        ],
-        compiler_params=pltpu.CompilerParams(
-            collective_id=3, has_side_effects=True, vmem_limit_bytes=VMEM_LIMIT
-        ),
-        name="owner_stage",
-    )(gup, gqkv)
+        name="finish_stage",
+    )(
+        table,
+        gq.reshape(C, 4, q, 6 * hc),
+        up.reshape(C, 4, q, F2),
+        out,
+        early,
+        late,
+        res,
+        inp,
+        small,
+        gb,
+    )
 
 
 QUERY_BLOCK = 256
 KEY_BLOCK = 256
+EARLY_PIECES = 8
 
 
 def local(
@@ -1481,18 +1770,26 @@
     L, D = inputs.shape
     P_, hc, C = L * n, D // n, n // 2
     R = pos_table.shape[0]
-    par = jnp.stack(
-        [b_out, ln1_gain, ln1_bias, b_down, ln2_gain, ln2_bias, b_query, b_value]
-    ).astype(F32)
-    bup = b_up.astype(F32)[None, :]
-    q, kv, hid_half, hidden, wq, wup2, wdn_o, wout_o, par_all, bup_o, pos_glob = entry_call(
-        S, n, positions[None, :], inputs, pos_table, w_qkv, w_up, w_down, w_out, par, bup
+    row = lambda v: v.reshape(1, -1)
+    rows = [row(v) for v in (b_out, ln1_gain, ln1_bias, b_down, ln2_gain, ln2_bias, b_query, b_value)]
+    q, kv, hid_half, hidden, wq, wup2, wdn_o, wout_o, par_all, bup2, pos_glob, lohi = entry_call(
+        S,
+        n,
+        row(positions),
+        inputs,
+        pos_table,
+        w_qkv,
+        w_up,
+        w_down,
+        w_out,
+        segments.reshape(S * n, 1, L),
+        row(b_up),
+        rows,
     )
-    bounds, lohi = ranges(segments, P_, QUERY_BLOCK, KEY_BLOCK)
     q = q.reshape(P_, hc)
     kv = kv.reshape(3 * P_, 2 * hc)
-    att, lse = attend_call(q, kv, bounds, lohi, QUERY_BLOCK, KEY_BLOCK)
-    result, dfirst, datt, gdn, gup, gout, stats, gbup = middle_call(
+    att, lse = attend_call(q, kv, lohi, QUERY_BLOCK, KEY_BLOCK)
+    result, dfirst, datt, gdn_late, gup, gout, stats, gbup, gdn_early = middle_call(
         S,
         n,
         att.reshape(C, 2, L, hc),
@@ -1504,16 +1801,15 @@
         wup2,
         w_down,
         wdn_o,
-        bup,
-        bup_o,
+        bup2,
     )
-    gdn, gup, gout = lax.psum((gdn, gup, gout), "seq")
     dq, dkv = attend_back_call(
-        q, kv, bounds, lohi, att, datt.reshape(P_, hc), lse, QUERY_BLOCK, KEY_BLOCK
+        q, kv, lohi, att, datt.reshape(P_, hc), lse, QUERY_BLOCK, KEY_BLOCK
     )
-    ginp, dh, gqkv, small, gbo = exit_call(
+    ginp, dh, gqkv, gup, gout, gdn_late, gtable, small, gbo = exit_call(
         S,
         n,
+        R,
         dq.reshape(C, 2, L, hc),
         dkv.reshape(3, C, 2, L, 2 * hc),
         hid_half,
@@ -1521,25 +1817,29 @@
         dfirst,
         stats,
         gbup,
+        pos_glob,
+        gup.reshape(C, 4, D // n // 4, gup.shape[2]),
+        gout,
+        gdn_late,
     )
-    gqkv = lax.psum(gqkv, "seq")
-    base = (lax.axis_index("shard") * R).astype(jnp.int32).reshape(1, 1)
-    gtable = table_call(S, n, R, base, pos_glob, dh)
-    up, qkv = owner_call(n, gup, gqkv)
+    gtable, gqkv, gup, gout, gdn, result, ginp, gbo, *small = finish_call(
+        n, gtable, gqkv, gup, gout, gdn_early, gdn_late, result, ginp, small, gbo
+    )
+    small = [v[0] for v in small]
     return (
         result,
         ginp,
         gtable,
-        qkv,
+        gqkv,
         small[6],
         small[7],
-        gout.astype(F32),
+        gout,
         small[5],
         small[3],
         small[4],
-        up,
+        gup,
         gbo[0],
-        gdn.astype(F32),
+        gdn,
         small[2],
         small[0],
         small[1],

time: 446 us -> 328 us (0.74); the launches traced: 442 us -> 330 us
  waiting for transfers between devices: 103 us -> 0 us
  Pallas kernels: 307 us -> 328 us
  between operations: 14.2 us -> 0.83 us
  other arithmetic: 10.8 us -> 0 us
  local copies, waits for them, and re-layouts: 6.68 us -> 1.26 us
    psum x1 -> x0, waiting for transfers between devices: 103 us -> none  [local(): gdn, gup, gout = lax.psum((gdn, gup, gout), 'seq')]
    pallas_call x1, Pallas kernels: 88.6 us -> 126 us  [exit_call(): pl.pallas_call(functools.partial(exit_kernel, dims), out_shape=(sds((L, D...]
    pallas_call x2 -> x1, Pallas kernels: 42.4 us -> 8.17 us  [finish_call(): pl.pallas_call(functools.partial(finish_kernel, (C, D, hc)), grid=(steps,...]
    pallas_call x1, Pallas kernels: 87.9 us -> 95.7 us  [middle_call(): pl.pallas_call(functools.partial(middle_kernel, dims), out_shape=(sds((L,...]
    pallas_call x1, Pallas kernels: 13.2 us -> 17.9 us  [attend_call(): pl.pallas_call(functools.partial(attend_kernel, (P_, hc, hh, bq, bk)), ou...]
    pallas_call x1, Pallas kernels: 15.4 us -> 20 us  [attend_back_call(): pl.pallas_call(functools.partial(attend_back_kernel, (P_, hc, hh, bq, bk)...]
    unnamed x19 -> x0, local copies, waits for them, and re-layouts: 4.47 us -> none
  transfers between devices with their start and end apart: 1 -> 0, of which waited for: 1 -> 0; matrix products, arithmetic and copies ran while one was open for 0% -> 0% of each run, Pallas kernels for 4% -> 0%
where the time goes in v2:
time: 328 us; the launch traced here: 330 us
  Pallas kernels  328 us (100%)
    pallas_call x1, Pallas kernels, exit_call(): pl.pallas_call(functools.partial(exit_kernel, dims), out_shape=(sds((L, D...  126 us
    pallas_call x1, Pallas kernels, middle_call(): pl.pallas_call(functools.partial(middle_kernel, dims), out_shape=(sds((L,...  95.7 us
    pallas_call x1, Pallas kernels, entry_call(): pl.pallas_call(functools.partial(entry_kernel, dims), out_shape=(sds((C,...  60 us
    pallas_call x1, Pallas kernels, attend_back_call(): pl.pallas_call(functools.partial(attend_back_kernel, (P_, hc, hh, bq, bk)...  20 us
    pallas_call x1, Pallas kernels, attend_call(): pl.pallas_call(functools.partial(attend_kernel, (P_, hc, hh, bq, bk)), ou...  17.9 us
    pallas_call x1, Pallas kernels, finish_call(): pl.pallas_call(functools.partial(finish_kernel, (C, D, hc)), grid=(steps,...  8.17 us

profile of v2, /device:TPU:0, one launch (start us, length us, event | category | flops | bytes accessed | tf_op | source)
XLA Modules:
  0.0 329.6 jit_solution(7396240764798552860)
XLA Ops:
  0.6 1.3 reshape.94.bup_in_ref
  1.9 60.0 %entry_stage.1 = (bf16[4,2,128,128]{3,2,1,0:T(8,128)(2,1)}, bf16[3,4,2,128,256]{4,3,2,1,0:T(8,128)(2,1)}, bf16[4,128,1024]{2,1,0:T(8,128)(2,1)}, f32[128,1024]{1...) custom-call(s32[1,128]{1,0:T(1,128)} %bitcast.40, ...), custom_call_target="tpu_custom_call" | custom-call | tf_op jit(solution)/shard_map/entry_stage/pallas_call | solution.py:529
  61.9 17.9 %attend_stage.1 = (bf16[1024,128]{1,0:T(8,128)(2,1)}, f32[2,1024]{1,0:T(2,128)}) custom-call(bf16[1024,128]{1,0:T(8,128)(2,1)} %bitcast.32, bf16[3072,256]{1,0:T(8,128)(2,1)} %bitcast.28, f32[2,1024]{1,0:T(2,128)} %get-tuple-element.67.lohi_ref), custom_call_target="tpu_custom_call" | custom-call | tf_op jit(solution)/shard_map/attend_stage/pallas_call | solution.py:660
  79.8 95.7 %middle_stage.1 = (bf16[128,1024]{1,0:T(8,128)(2,1)}, f32[128,1024]{1,0:T(8,128)}, bf16[4,2,128,128]{3,2,1,0:T(8,128)(2,1)}, bf16[8,32,1024]{2,1,0:T(8,128)(2,1)...) custom-call(bf16[4,2,128,128]{3,2,1,0:T(8,128)(2,1)} %bitcast.34, ...), custom_call_target="tpu_custom_call" | custom-call | tf_op jit(solution)/shard_map/middle_stage/pallas_call | solution.py:1085
  175.6 20.0 %attend_back_stage.1 = (bf16[1024,128]{1,0:T(8,128)(2,1)}, bf16[3072,256]{1,0:T(8,128)(2,1)}) custom-call(bf16[1024,128]{1,0:T(8,128)(2,1)} %bitcast.33, bf16[3072,256]{1,0:T(8,128)(2,1)} %bitcast.29, f32[2,1024]{1,0:T(2,128)} %get-tuple-element.67.lohi_ref, bf16[1024,128]{1,0:T(8,128)(2,1)} %get-tuple-element.68.att_ref, bf16[1024,128]{1,0:T(8,128)(2,1)} %bitcast.38, ...), custom_call_target="tpu_custom_call" | custom-call | tf_op jit(solution)/shard_map/attend_back_stage/pallas_call | solution.py:741
  195.5 125.7 %exit_stage.1 = (bf16[128,1024]{1,0:T(8,128)(2,1)}, bf16[4,8,128,1024]{3,2,1,0:T(8,128)(2,1)}, bf16[16,32,768]{2,1,0:T(8,128)(2,1)}, bf16[16,32,1024]{2,1,0:T(8,...) custom-call(bf16[4,2,128,128]{3,2,1,0:T(8,128)(2,1)} %bitcast.37, ...), custom_call_target="tpu_custom_call" | custom-call | tf_op jit(solution)/shard_map/exit_stage/pallas_call | solution.py:1554
  321.3 8.2 %finish_stage.1 = (f32[1024,1024]{1,0:T(8,128)}, f32[128,3072]{1,0:T(8,128)}, f32[128,4096]{1,0:T(8,128)}, f32[128,1024]{1,0:T(8,128)}, f32[512,1024]{1,0:T(8,12...) custom-call(bf16[1024,1024]{1,0:T(8,128)(2,1)} %get-tuple-element.88, ...), custom_call_target="tpu_custom_call" | custom-call | tf_op jit(solution)/shard_map/finish_stage/pallas_call | solution.py:1691

commit v3 on v2

--- a/solution.py
+++ b/solution.py
@@ -18,7 +18,8 @@
 MESH = pl.DeviceIdType.MESH
 F32 = jnp.float32
 BF16 = jnp.bfloat16
-VMEM_LIMIT = 60 * 1024 * 1024
+MIB = 1024 * 1024
+ENTRY_VMEM, ATTEND_VMEM, MIDDLE_VMEM, BACK_VMEM, EXIT_VMEM = 24, 16, 44, 20, 48
 
 
 def flip(value, mask, width):
@@ -158,15 +159,15 @@
 
 def entry_kernel(
     dims,
-    pos_ref,
-    inp_ref,
+    pos_hbm,
+    inp_hbm,
     table_ref,
     wqkv_ref,
     wup_ref,
     wdn_ref,
     wout_ref,
-    seg_ref,
-    bup_in_ref,
+    seg_hbm,
+    bup_in_hbm,
     row0_ref,
     row1_ref,
     row2_ref,
@@ -187,6 +188,11 @@
     bup2_ref,
     pos_glob_ref,
     lohi_ref,
+    pos_ref,
+    inp_ref,
+    seg_ref,
+    bup_in_ref,
+    rows_ref,
     table_v,
     pstage,
     precv,
@@ -235,6 +241,18 @@
     h2 = 2 * hc
     Dn = D // n
 
+    rows = (row0_ref, row1_ref, row2_ref, row3_ref, row4_ref, row5_ref, row6_ref, row7_ref)
+    smalls = [
+        pltpu.make_async_copy(pos_hbm, pos_ref, loc.at[6]),
+        pltpu.make_async_copy(seg_hbm, seg_ref, loc.at[7]),
+        pltpu.make_async_copy(bup_in_hbm, bup_in_ref, loc.at[8]),
+    ] + [
+        pltpu.make_async_copy(row, rows_ref.at[i], loc.at[9 + i]) for i, row in enumerate(rows)
+    ]
+    for small in smalls:
+        small.start()
+    inp_copy = pltpu.make_async_copy(inp_hbm, inp_ref, loc.at[17])
+    inp_copy.start()
     table_copy = pltpu.make_async_copy(table_ref, table_v, loc.at[0])
     table_copy.start()
     own_wq = []
@@ -252,9 +270,10 @@
     )
     own_wup_in.start()
 
-    rows = (row0_ref, row1_ref, row2_ref, row3_ref, row4_ref, row5_ref, row6_ref, row7_ref)
-    for i, row in enumerate(rows):
-        par_ref[i : i + 1] = row[...].astype(F32)
+    for small in smalls:
+        small.wait()
+    for i in range(8):
+        par_ref[i : i + 1] = rows_ref[i].astype(F32)
     bup_ref[...] = bup_in_ref[...].astype(F32)
     F1 = F2 // 2
     bup_mine = pl.ds(pl.multiple_of(core * F1, 128), F1)
@@ -329,6 +348,7 @@
         ).start()
 
     table_copy.wait()
+    inp_copy.wait()
     lane_ids = lax.broadcasted_iota(jnp.int32, (L, R), 1) + s * R
 
     def picked(block):
@@ -525,6 +545,7 @@
     dma = pltpu.SemaphoreType.DMA
     vm = pl.BlockSpec(memory_space=pltpu.VMEM)
     anyw = pl.BlockSpec(memory_space=pl.ANY)
+    hbm = pl.BlockSpec(memory_space=pltpu.HBM)
     sds = jax.ShapeDtypeStruct
     return pl.pallas_call(
         functools.partial(entry_kernel, dims),
@@ -542,9 +563,14 @@
             sds((S, n, 1, L), jnp.int32),
             sds((2, n * L), F32),
         ),
-        in_specs=[vm, vm, anyw, anyw, anyw, anyw, anyw] + [vm] * 10,
+        in_specs=[hbm] * 17,
         out_specs=(vm, vm, vm, vm, vm, anyw, anyw, anyw, vm, vm, vm, vm),
         scratch_shapes=[
+            pltpu.VMEM((1, L), jnp.int32),
+            pltpu.VMEM((L, D), BF16),
+            pltpu.VMEM((S * n, 1, L), jnp.int32),
+            pltpu.VMEM((1, F1), BF16),
+            pltpu.VMEM((8, 1, hc), BF16),
             pltpu.VMEM((R, D), BF16),
             pltpu.VMEM((C, L, D), BF16),
             pltpu.VMEM((C, L, D), BF16),
@@ -581,13 +607,16 @@
             dma((C, 2)),
             dma((C, 4)),
             dma((C, 4)),
-            dma((6,)),
+            dma((18,)),
         ],
         compiler_params=pltpu.CompilerParams(
-            collective_id=0, has_side_effects=True, vmem_limit_bytes=VMEM_LIMIT
+            collective_id=0, has_side_effects=True, vmem_limit_bytes=ENTRY_VMEM * MIB
         ),
         name="entry_stage",
-    )(pos, inp, table, wqkv, wup, wdn, wout, seg, bup, *rows)
+    )(*[
+        pltpu.with_memory_space_constraint(v, pltpu.HBM)
+        for v in (pos, inp, table, wqkv, wup, wdn, wout, seg, bup, *rows)
+    ])
 
 
 def key_blocks(lohi_ref, rows, bk):
@@ -666,7 +695,7 @@
         in_specs=[vm, vm, vm],
         out_specs=(vm, vm),
         scratch_shapes=[pltpu.VMEM((3 * P_ // bk, hc, bk), BF16)],
-        compiler_params=pltpu.CompilerParams(vmem_limit_bytes=VMEM_LIMIT),
+        compiler_params=pltpu.CompilerParams(vmem_limit_bytes=ATTEND_VMEM * MIB),
         name="attend_stage",
     )(q, kv, lohi)
 
@@ -750,7 +779,7 @@
             pltpu.VMEM((3 * P_ // bk, hc, bk), BF16),
             pltpu.VMEM((3 * P_, 2 * hc), F32),
         ],
-        compiler_params=pltpu.CompilerParams(vmem_limit_bytes=VMEM_LIMIT),
+        compiler_params=pltpu.CompilerParams(vmem_limit_bytes=BACK_VMEM * MIB),
         name="attend_back_stage",
     )(q, kv, lohi, att, datt, lse)
 
@@ -1140,7 +1169,7 @@
             dma((5,)),
         ],
         compiler_params=pltpu.CompilerParams(
-            collective_id=1, has_side_effects=True, vmem_limit_bytes=VMEM_LIMIT
+            collective_id=1, has_side_effects=True, vmem_limit_bytes=MIDDLE_VMEM * MIB
         ),
         name="middle_stage",
     )(att, hidden, cot, par, wout, wout_o, wup2, wdn, wdn_o, bup)
@@ -1334,6 +1363,7 @@
     total = partial(0) + dfirst_ref[...]
 
     def qkv_grad(c, carry):
+        late.slot(c)
         cols = pl.ds(pl.multiple_of(c * 2 * Dn, 128), 2 * Dn)
         res = cols_dot(hid_ref[:, :, cols].reshape(Ph, 2 * Dn), x6[...].reshape(Ph, 6 * hc))
         gq_v[c] = res.astype(BF16).reshape(2, 4, quarter, 6 * hc)
@@ -1359,8 +1389,7 @@
 
     for j in range(1, C):
         await_recv(up_o.at[block_of(j)], ua_rs.at[j], peer(j))
-    wide.give_out(0, wide.pieces // 2)
-    late.run(0, 6)
+    late.run(C, C + 2)
     await_recv(gq_r, gq_rs.at[0], partner)
     gq_s[...] = (gq_v[:, core].astype(F32) + gq_r[...].astype(F32)).astype(BF16)
     for j in range(C - 1, 0, -1):
@@ -1392,9 +1421,9 @@
         remote(dhb, dh_ref.at[z, s], zl_ss.at[z, 1], zl_rs.at[z, 1], (z - 1, s)).start()
 
     broadcast(dhb, z)
-    late.run(6, late.slots)
+    wide.give_out(0, wide.pieces)
+    late.run(C + 2, late.slots)
     square.run(0, square.slots)
-    wide.run(0, 2)
     for d in range(1, S):
 
         @pl.when(z - d >= 0)
@@ -1422,6 +1451,12 @@
                 ).start()
 
             broadcast(dh_ref.at[at, s], at)
+
+        if d == 2:
+            for j in range(1, C):
+                await_recv(gq_o.at[block_of(j)], gx_rs.at[j], peer(j))
+            inner.give_out(0, inner.pieces)
+        wide.run(3 * (d - 1), 3 * d)
 
     def relay(at):
         for j in range(1, C):
@@ -1431,17 +1466,14 @@
                 dh_ref.at[at, src], dh_ref.at[at, src], pf_ss.at[at, j], pf_rs.at[at, j], partner
             ).start()
 
-    wide.give_out(wide.pieces // 2, wide.pieces)
-    for j in range(1, C):
-        await_recv(gq_o.at[block_of(j)], gx_rs.at[j], peer(j))
-    inner.give_out(0, inner.pieces)
+    seen = 3 * (S - 1)
 
     def plane_sum(t, carry):
         at = flip(z, t, S)
         relay(at)
 
-        wide.run(2 + 6 * t, 8 + 6 * t)
-        inner.run(6 * (t - 1), 6 * t)
+        wide.run(seen + 5 * t, seen + 5 * t + 5)
+        inner.run(6 * (t - 2), 6 * (t - 1))
 
         for j in range(C):
             src = 2 * flip(chip, j, C) + other
@@ -1479,8 +1511,8 @@
 
     lax.fori_loop(0, R // rt, add_tile, 0)
 
-    wide.run(2 + 6 * S, wide.slots)
-    inner.run(6 * (S - 1), inner.slots)
+    wide.run(seen + 5 * S, wide.slots)
+    inner.run(6 * (S - 2), inner.slots)
     for d in range(1, S):
         src = lax.rem(z + S - d, S)
         await_recv(zst.at[src], zs_rs.at[d, 0], (src, s))
@@ -1624,7 +1656,7 @@
             dma((2,)),
         ],
         compiler_params=pltpu.CompilerParams(
-            collective_id=2, has_side_effects=True, vmem_limit_bytes=VMEM_LIMIT
+            collective_id=2, has_side_effects=True, vmem_limit_bytes=EXIT_VMEM * MIB
         ),
         name="exit_stage",
     )(dq, dkv, hid_half, wq, dfirst, stats, gbup, pos, gupc, goutc, gdnc)
@@ -1725,7 +1757,7 @@
             fixed(1, F1),
         )
         + (fixed(1, hc),) * 8,
-        compiler_params=pltpu.CompilerParams(vmem_limit_bytes=VMEM_LIMIT),
+        compiler_params=pltpu.CompilerParams(vmem_limit_bytes=ATTEND_VMEM * MIB),
         name="finish_stage",
     )(
         table,
@@ -1741,8 +1773,9 @@
     )
 
 
-QUERY_BLOCK = 256
-KEY_BLOCK = 256
+QUERY_BLOCK = 512
+KEY_BLOCK = 512
+BACK_KEY_BLOCK = 256
 EARLY_PIECES = 8
 
 
@@ -1804,7 +1837,7 @@
         bup2,
     )
     dq, dkv = attend_back_call(
-        q, kv, lohi, att, datt.reshape(P_, hc), lse, QUERY_BLOCK, KEY_BLOCK
+        q, kv, lohi, att, datt.reshape(P_, hc), lse, QUERY_BLOCK, BACK_KEY_BLOCK
     )
     ginp, dh, gqkv, gup, gout, gdn_late, gtable, small, gbo = exit_call(
         S,

time: 328 us -> 306 us (0.933)
  Pallas kernels: 328 us -> 299 us
  local copies, waits for them, and re-layouts: 1.26 us -> 5.14 us
    pallas_call x1, Pallas kernels: 20 us -> 9.41 us  [attend_back_call(): pl.pallas_call(functools.partial(attend_back_kernel, (P_, hc, hh, bq, bk)...]
    pallas_call x1, Pallas kernels: 17.9 us -> 7.66 us  [attend_call(): pl.pallas_call(functools.partial(attend_kernel, (P_, hc, hh, bq, bk)), ou...]
    unnamed x0 -> x14, local copies, waits for them, and re-layouts: none -> 3.88 us
where the time goes in v3:
time: 306 us; the launch traced here: 305 us
  Pallas kernels  299 us (98%)
  local copies, waits for them, and re-layouts  5.14 us (2%)
    pallas_call x1, Pallas kernels, exit_call(): pl.pallas_call(functools.partial(exit_kernel, dims), out_shape=(sds((L, D...  125 us
    pallas_call x1, Pallas kernels, middle_call(): pl.pallas_call(functools.partial(middle_kernel, dims), out_shape=(sds((L,...  94.3 us
    pallas_call x1, Pallas kernels, entry_call(): pl.pallas_call(functools.partial(entry_kernel, dims), out_shape=(sds((C,...  57.3 us
    pallas_call x1, Pallas kernels, attend_back_call(): pl.pallas_call(functools.partial(attend_back_kernel, (P_, hc, hh, bq, bk)...  9.41 us
    pallas_call x1, Pallas kernels, attend_call(): pl.pallas_call(functools.partial(attend_kernel, (P_, hc, hh, bq, bk)), ou...  7.66 us

profile of v3, /device:TPU:0, one launch (start us, length us, event | category | flops | bytes accessed | tf_op | source)
XLA Modules:
  0.0 305.0 jit_solution(13076607696625447381)
XLA Ops:
  0.6 1.3 reshape.94.bup_in_hbm
  1.9 0.0 copy-start.5
  1.9 0.0 copy-start.6
  1.9 57.3 %entry_stage.1 = (bf16[4,2,128,128]{3,2,1,0:T(8,128)(2,1)S(1)}, bf16[3,4,2,128,256]{4,3,2,1,0:T(8,128)(2,1)S(1)}, bf16[4,128,1024]{2,1,0:T(8,128)(2,1)S(1)}, f32...) custom-call(s32[1,128]{1,0:T(1,128)} %bitcast.40, ...), custom_call_target="tpu_custom_call" | custom-call | tf_op jit(solution)/shard_map/entry_stage/pallas_call | solution.py:550
  59.2 0.0 copy-start.2
  59.2 1.1 copy-done.2
  60.3 0.0 copy-start
  60.3 7.7 %attend_stage.1 = (bf16[1024,128]{1,0:T(8,128)(2,1)S(1)}, f32[2,1024]{1,0:T(2,128)S(1)}) custom-call(bf16[1024,128]{1,0:T(8,128)(2,1)S(1)} %bitcast.32, bf16[3072,256]{1,0:T(8,128)(2,1)S(1)} %bitcast.28, f32[2,1024]{1,0:T(2,128)S(1)} %get-tuple-element.67.lohi_ref), custom_call_target="tpu_custom_call" | custom-call | tf_op jit(solution)/shard_map/attend_stage/pallas_call | solution.py:689
  68.0 0.0 copy-done.5
  68.0 0.0 copy-done.6
  68.0 0.0 copy-done
  68.0 94.3 %middle_stage.1 = (bf16[128,1024]{1,0:T(8,128)(2,1)S(1)}, f32[128,1024]{1,0:T(8,128)S(1)}, bf16[4,2,128,128]{3,2,1,0:T(8,128)(2,1)S(1)}, bf16[8,32,1024]{2,1,0:T...) custom-call(bf16[4,2,128,128]{3,2,1,0:T(8,128)(2,1)S(1)} %bitcast.34, ...), custom_call_target="tpu_custom_call" | custom-call | tf_op jit(solution)/shard_map/middle_stage/pallas_call | solution.py:1114
  162.3 0.0 copy-start.4
  162.3 9.4 %attend_back_stage.1 = (bf16[1024,128]{1,0:T(8,128)(2,1)S(1)}, bf16[3072,256]{1,0:T(8,128)(2,1)S(1)}) custom-call(bf16[1024,128]{1,0:T(8,128)(2,1)S(1)} %bitcast.33, bf16[3072,256]{1,0:T(8,128)(2,1)S(1)} %bitcast.29, f32[2,1024]{1,0:T(2,128)S(1)} %get-tuple-element.67.lohi_ref, bf16[1024,128]{1,0:T(8,128)(2,1)S(1)} %get-tuple-element.68.att_ref, ...), custom_call_target="tpu_custom_call" | custom-call | tf_op jit(solution)/shard_map/attend_back_stage/pallas_call | solution.py:770
  171.7 0.0 copy-done.4
  171.7 0.0 copy-start.3
  171.8 1.1 copy-done.3
  172.9 125.2 %exit_stage.1 = (bf16[128,1024]{1,0:T(8,128)(2,1)S(1)}, bf16[4,8,128,1024]{3,2,1,0:T(8,128)(2,1)}, bf16[16,32,768]{2,1,0:T(8,128)(2,1)S(1)}, bf16[16,32,1024]{2,...) custom-call(bf16[4,2,128,128]{3,2,1,0:T(8,128)(2,1)S(1)} %bitcast.37, ...), custom_call_target="tpu_custom_call" | custom-call | tf_op jit(solution)/shard_map/exit_stage/pallas_call | solution.py:1586
  298.1 0.0 copy-start.1
  298.1 1.6 copy-done.1
  299.7 5.2 %finish_stage.1 = (f32[1024,1024]{1,0:T(8,128)}, f32[128,3072]{1,0:T(8,128)}, f32[128,4096]{1,0:T(8,128)}, f32[128,1024]{1,0:T(8,128)}, f32[512,1024]{1,0:T(8,12...) custom-call(bf16[1024,1024]{1,0:T(8,128)(2,1)S(1)} %copy-done.1, ...), custom_call_target="tpu_custom_call" | custom-call | tf_op jit(solution)/shard_map/finish_stage/pallas_call | solution.py:1723
Async XLA Ops:
  1.9 66.1 %copy-start.5 = (bf16[128,1024]{1,0:T(8,128)(2,1)S(1)}, bf16[128,1024]{1,0:T(8,128)(2,1)}, u32[]{:S(2)}) copy-start(bf16[128,1024]{1,0:T(8,128)(2,1)} %wout_ref.3) | copy-start | bytes 786436
  1.9 66.1 %copy-start.6 = (bf16[128,1024]{1,0:T(8,128)(2,1)S(1)}, bf16[128,1024]{1,0:T(8,128)(2,1)}, u32[]{:S(2)}) copy-start(bf16[128,1024]{1,0:T(8,128)(2,1)} %cot_ref.1) | copy-start | bytes 786436
  59.2 1.1 copy-start.2
  60.3 7.7 %copy-start = (bf16[512,1024]{1,0:T(8,128)(2,1)S(1)}, bf16[512,1024]{1,0:T(8,128)(2,1)}, u32[]{:S(2)}) copy-start(bf16[512,1024]{1,0:T(8,128)(2,1)} %wdn_ref.3) | copy-start | bytes 3145732
  162.3 9.4 %copy-start.4 = (bf16[4,128,1024]{2,1,0:T(8,128)(2,1)}, bf16[4,128,1024]{2,1,0:T(8,128)(2,1)S(1)}, u32[]{:S(2)}) copy-start(bf16[4,128,1024]{2,1,0:T(8,128)(2,1)S(1)} %get-tuple-element.85) | copy-start | bytes 3145732
  171.7 1.1 copy-start.3
  298.1 1.6 copy-start.1

commit v4 on v3

--- a/solution.py
+++ b/solution.py
@@ -143,6 +143,126 @@
             return carry
 
         lax.fori_loop(0, self.pieces, step, 0)
+
+
+class Gather:
+    def __init__(self, C, chip, peer, rows, slot, ss, rs):
+        self.C, self.chip, self.peer, self.rows, self.slot = C, chip, peer, rows, slot
+        self.ss, self.rs = ss, rs
+
+    def half(self, ref, h):
+        return ref.at[pl.ds(h * (self.rows // 2), self.rows // 2)]
+
+    def block(self, j):
+        return self.slot(flip(self.chip, j, self.C))
+
+    def send(self, src):
+        dst = self.slot(self.chip)
+        if self.C == 4:
+            for j, first in ((1, 0), (2, 1)):
+                for h in (first, 1 - first):
+                    remote(
+                        self.half(src, h), self.half(dst, h), self.ss.at[j, h], self.rs.at[j, h], self.peer(j)
+                    ).start()
+        else:
+            for j in range(self.C - 1, 0, -1):
+                remote(src, dst, self.ss.at[j, 0], self.rs.at[j, 0], self.peer(j)).start()
+
+    def relay(self):
+        if self.C == 4:
+            for j, h, to in ((1, 0, 2), (2, 1, 1)):
+                part = self.half(self.block(j), h)
+                await_recv(part, self.rs.at[j, h], self.peer(j))
+                remote(part, part, self.ss.at[3, h], self.rs.at[3, h], self.peer(to)).start()
+
+    def arrived(self, j):
+        if self.C == 4:
+            for want, h in ((1, 1), (2, 0), (3, 0), (3, 1)):
+
+                @pl.when(j == want)
+                def _(want=want, h=h):
+                    await_recv(self.half(self.block(want), h), self.rs.at[want, h], self.peer(want))
+        else:
+
+            @pl.when(j > 0)
+            def _():
+                await_recv(self.block(j), self.rs.at[j, 0], self.peer(j))
+
+    def settle(self):
+        own = self.slot(self.chip)
+        if self.C == 4:
+            for j in range(1, 4):
+                for h in range(2):
+                    await_send(self.half(own, h), self.ss.at[j, h], self.peer(j))
+        else:
+            for j in range(1, self.C):
+                await_send(own, self.ss.at[j, 0], self.peer(j))
+
+
+class Scatter:
+    def __init__(self, C, peer, rows, stage, recv, ss, rs):
+        self.C, self.peer, self.rows = C, peer, rows
+        self.stage, self.recv, self.ss, self.rs = stage, recv, ss, rs
+
+    def give(self, j, h, to):
+        part = pl.ds(h * (self.rows // 2), self.rows // 2)
+        remote(
+            self.stage.at[j, part], self.recv.at[j, part], self.ss.at[j, h], self.rs.at[j, h], self.peer(to)
+        ).start()
+
+    def take(self, j, h, source):
+        part = pl.ds(h * (self.rows // 2), self.rows // 2)
+        await_recv(self.recv.at[j, part], self.rs.at[j, h], self.peer(source))
+        return part
+
+    def send(self, make):
+        if self.C != 4:
+
+            def step(k, carry):
+                j = self.C - 1 - k
+                self.stage[j] = make(j).astype(BF16)
+                remote(
+                    self.stage.at[j], self.recv.at[j], self.ss.at[j, 0], self.rs.at[j, 0], self.peer(j)
+                ).start()
+                return carry
+
+            lax.fori_loop(0, self.C - 1, step, 0)
+            return make(0)
+        self.stage[3] = make(3).astype(BF16)
+        self.give(3, 0, 2)
+        self.give(3, 1, 1)
+        self.stage[1] = make(1).astype(BF16)
+        self.give(1, 1, 1)
+        self.stage[2] = make(2).astype(BF16)
+        self.give(2, 0, 2)
+        own = make(0)
+        for h, source, j in ((0, 2, 1), (1, 1, 2)):
+            part = self.take(3, h, source)
+            both = self.stage[j, part].astype(F32) + self.recv[3, part].astype(F32)
+            self.stage[j, part] = both.astype(BF16)
+            self.give(j, h, j)
+        return own
+
+    def collect(self, total):
+        if self.C != 4:
+            for j in range(1, self.C):
+                await_recv(self.recv.at[j], self.rs.at[j, 0], self.peer(j))
+                total = total + self.recv[j].astype(F32)
+            return total
+        for j in (1, 2):
+            self.take(j, 2 - j, j)
+            self.take(j, j - 1, j)
+            total = total + self.recv[j].astype(F32)
+        return total
+
+    def settle(self):
+        for j in range(1, self.C):
+            if self.C == 4:
+                for h in range(2):
+                    part = pl.ds(h * (self.rows // 2), self.rows // 2)
+                    await_send(self.stage.at[j, part], self.ss.at[j, h], self.peer(j))
+            else:
+                await_send(self.stage.at[j], self.ss.at[j, 0], self.peer(j))
 
 
 def rows_dot(a, b):
@@ -366,19 +486,16 @@
         await_recv(precv.at[j], rsp_rs.at[j], (z, partner))
         return mine + precv[j].astype(F32)
 
-    send_partner(C - 1)
-
-    def scatter_step(k, carry):
-        j = C - 1 - k
-        send_partner(j - 1)
-        cstage[j] = combined(j).astype(BF16)
-        remote(
-            cstage.at[j], crecv.at[j], rsc_ss.at[j], rsc_rs.at[j], (z, 2 * flip(chip, j, C) + core)
-        ).start()
+    def peer(j):
+        return (z, 2 * flip(chip, j, C) + core)
+
+    def partner_step(k, carry):
+        send_partner(C - 1 - k)
         return carry
 
-    lax.fori_loop(0, C - 1, scatter_step, 0)
-    hidden = combined(0) + inp_ref[...].astype(F32)
+    lax.fori_loop(0, C, partner_step, 0)
+    rows_sum = Scatter(C, peer, L, cstage, crecv, rsc_ss, rsc_rs)
+    hidden = rows_sum.send(combined) + inp_ref[...].astype(F32)
 
     for j in range(1, C):
         src = 2 * flip(chip, j, C) + core
@@ -388,19 +505,11 @@
             )
         remote(wq_ref.at[src], wq_ref.at[src], wqf_ss.at[j], wqf_rs.at[j], (z, partner)).start()
 
-    for j in range(1, C):
-        await_recv(crecv.at[j], rsc_rs.at[j], (z, 2 * flip(chip, j, C) + core))
-        hidden = hidden + crecv[j].astype(F32)
+    hidden = rows_sum.collect(hidden)
     hidden_ref[...] = hidden
     hid_half_ref[chip] = hidden.astype(BF16)
-    for j in range(C - 1, 0, -1):
-        remote(
-            hid_half_ref.at[chip],
-            hid_half_ref.at[chip],
-            ag_ss.at[j],
-            ag_rs.at[j],
-            (z, 2 * flip(chip, j, C) + core),
-        ).start()
+    gather = Gather(C, chip, peer, L, lambda c: hid_half_ref.at[c], ag_ss, ag_rs)
+    gather.send(hid_half_ref.at[chip])
 
     own_wup_in.wait()
     own_wup_out = pltpu.make_async_copy(wup_own, wup2_ref.at[s], loc.at[5])
@@ -432,10 +541,7 @@
     def project(j, carry):
         c = flip(chip, j, C)
 
-        @pl.when(j > 0)
-        def _():
-            await_recv(hid_half_ref.at[c], ag_rs.at[j], (z, 2 * c + core))
-
+        gather.arrived(j)
         res = rows_dot(hid_half_ref[c], wq_ref[...].reshape(D, 3 * h2))
         query = (res[:, :h2] + bias_q).astype(BF16) * score_scale
         key = res[:, h2 : 2 * h2].astype(BF16)
@@ -472,6 +578,7 @@
         ).start()
         return carry
 
+    gather.relay()
     lax.fori_loop(0, C, project, 0)
 
     for j in range(1, C):
@@ -509,14 +616,13 @@
         return carry
 
     lax.fori_loop(0, C, settle, 0)
+    gather.settle()
+    rows_sum.settle()
     for j in range(1, C):
-        peer = (z, 2 * flip(chip, j, C) + core)
-        await_send(cstage.at[j], rsc_ss.at[j], peer)
-        await_send(hid_half_ref.at[chip], ag_ss.at[j], peer)
-        await_send(wup_own, wup_ss.at[j], peer)
+        await_send(wup_own, wup_ss.at[j], peer(j))
         for part in range(3):
             await_send(
-                wq_ref.at[s, :, part * h2 : (part + 1) * h2], wq_ss.at[j, part], peer
+                wq_ref.at[s, :, part * h2 : (part + 1) * h2], wq_ss.at[j, part], peer(j)
             )
     for d in range(1, n):
         peer = (z, flip(s, d, n))
@@ -599,10 +705,10 @@
             dma((3,)),
             dma((C,)),
             dma((C,)),
-            dma((C,)),
-            dma((C,)),
-            dma((C,)),
-            dma((C,)),
+            dma((C, 2)),
+            dma((C, 2)),
+            dma((C, 2)),
+            dma((C, 2)),
             dma((C, 2)),
             dma((C, 2)),
             dma((C, 4)),
@@ -902,23 +1008,21 @@
     def taken(i, src, dst):
         await_recv(dst, gx_rs.at[i], partner)
 
-    def spread(r, buf):
-        for j in range(C - 1, 0, -1):
-            remote(buf.at[chip], buf.at[chip], ag_ss.at[r, j], ag_rs.at[r, j], peer(j)).start()
-
-    def arrived(r, buf, j):
-        @pl.when(j > 0)
-        def _():
-            c = flip(chip, j, C)
-            await_recv(buf.at[c], ag_rs.at[r, j], (z, 2 * c + core))
+    def gather_of(r, buf):
+        return Gather(C, chip, peer, L, lambda c: buf.at[c], ag_ss.at[r], ag_rs.at[r])
+
+    gathers = [gather_of(0, fa), gather_of(1, da), gather_of(2, dfa)]
+    out_sum = Scatter(C, peer, L, stage.at[0], recv.at[0], sc_ss.at[0], sc_rs.at[0])
 
     def hand(r, j, part):
         stage[r, j] = part.astype(BF16)
-        remote(stage.at[r, j], recv.at[r, j], sc_ss.at[r, j], sc_rs.at[r, j], peer(j)).start()
+        remote(
+            stage.at[r, j], recv.at[r, j], sc_ss.at[r, j, 0], sc_rs.at[r, j, 0], peer(j)
+        ).start()
 
     def collected(r, total):
         for j in range(1, C):
-            await_recv(recv.at[r, j], sc_rs.at[r, j], peer(j))
+            await_recv(recv.at[r, j], sc_rs.at[r, j, 0], peer(j))
             total = total + recv[r, j].astype(F32)
         return total
 
@@ -935,18 +1039,13 @@
         c = flip(chip, j, C)
         return rows_dot(att_ref[c, core], wout_v[core]) + rows_dot(attp[c], wout_v[other])
 
-    def out_step(k, carry):
-        hand(0, C - 1 - k, out_part(C - 1 - k))
-        return carry
-
-    lax.fori_loop(0, C - 1, out_step, 0)
-    first_sum = collected(0, out_part(0) + hidden_ref[...] + b_out)
+    first_sum = out_sum.collect(out_sum.send(out_part) + hidden_ref[...] + b_out)
     normed_one, inverse_one = layer_stats(first_sum)
     normed_v[...] = normed_one
     first_norm = normed_one * gain1 + shift1
     first_v[...] = first_norm
     fa[chip] = first_norm.astype(BF16)
-    spread(0, fa)
+    gathers[0].send(fa.at[chip])
 
     loads[2].wait()
     loads[3].wait()
@@ -963,9 +1062,10 @@
         return rows_dot(act[c], wdn_v[...].reshape(F2, D))
 
     own = up_part(0)
+    gathers[0].relay()
 
     def up_step(j, carry):
-        arrived(0, fa, j)
+        gathers[0].arrived(j)
         hand(1, j, up_part(j))
         return carry
 
@@ -980,7 +1080,7 @@
     put_stat(2, col_sum(d_second))
     dnorm_v[...] = d_second
     da[chip] = d_second.astype(BF16)
-    spread(1, da)
+    gathers[1].send(da.at[chip])
 
     def down_back(j):
         c = flip(chip, j, C)
@@ -991,9 +1091,10 @@
 
     gb_v[...] = jnp.zeros_like(gb_v)
     own = down_back(0)
+    gathers[1].relay()
 
     def back_step(j, carry):
-        arrived(1, da, j)
+        gathers[1].arrived(j)
         hand(2, j, down_back(j))
         return carry
 
@@ -1047,11 +1148,16 @@
     stats_ref[:, 6:8] = jnp.zeros((n, 2, hc), F32)
     dfirst_ref[...] = d_first
     dfa[chip] = d_first.astype(BF16)
-    spread(2, dfa)
+    gathers[2].send(dfa.at[chip])
 
     def att_back(j, carry):
         chain.run(2 * j + 2, 2 * j + 4)
-        arrived(2, dfa, j)
+
+        @pl.when(j == 1)
+        def _():
+            gathers[2].relay()
+
+        gathers[2].arrived(j)
         c = flip(chip, j, C)
         datt_ref[c, core] = rows_dot_t(dfa[c], wout_v[core]).astype(BF16)
         dattst[j] = rows_dot_t(dfa[c], wout_v[other]).astype(BF16)
@@ -1073,6 +1179,9 @@
     gout_ref[...] = (gout_v[1].astype(F32) + gout_r[...].astype(F32)).astype(BF16)
 
     chain.settle()
+    out_sum.settle()
+    for gather in gathers:
+        gather.settle()
     gdn_done_ref[...] = gdn_f[...]
     await_send(attp, ap_ss.at[0], partner)
     await_send(gdn_r, gx_ss.at[0], partner)
@@ -1087,11 +1196,8 @@
 
         @pl.when(j > 0)
         def _():
-            for r in range(3):
-                await_send(stage.at[r, j], sc_ss.at[r, j], peer(j))
-            await_send(fa.at[chip], ag_ss.at[0, j], peer(j))
-            await_send(da.at[chip], ag_ss.at[1, j], peer(j))
-            await_send(dfa.at[chip], ag_ss.at[2, j], peer(j))
+            for r in range(1, 3):
+                await_send(stage.at[r, j], sc_ss.at[r, j, 0], peer(j))
 
         return carry
 
@@ -1157,10 +1263,10 @@
             pltpu.VMEM((C, L, hc), BF16),
             dma((1,)),
             dma((1,)),
-            dma((3, C)),
-            dma((3, C)),
-            dma((3, C)),
-            dma((3, C)),
+            dma((3, C, 2)),
+            dma((3, C, 2)),
+            dma((3, C, 2)),
+            dma((3, C, 2)),
             dma((4,)),
             dma((4,)),
             dma((C,)),
@@ -1308,6 +1414,17 @@
     inner = Chain(S, z, s, gq_o, gq_l, gq_x, gq_f, qc)
     late.give_out(0, late.pieces)
     square.give_out(0, square.pieces)
+    starts = [0, late.pieces, late.pieces + square.pieces]
+    starts.append(starts[2] + wide.pieces)
+    last_step = starts[3] + inner.slots
+
+    def chain_step(m, carry=0):
+        for chain, begin in zip((late, square, wide, inner), starts):
+            chain.slot(m - begin)
+        return carry
+
+    def chain_steps(begin, end):
+        lax.fori_loop(begin, end, chain_step, 0)
 
     st_r[s] = stats_ref[s]
     for d in range(1, n):
@@ -1353,17 +1470,12 @@
         x6[c] = jnp.concatenate(pieces, axis=1)
         return rows_dot_t(x6[c], wq_ref[...].reshape(D, 6 * hc))
 
-    def scatter(k, carry):
-        j = C - 1 - k
-        stage[j] = partial(j).astype(BF16)
-        remote(stage.at[j], recv.at[j], sc_ss.at[j], sc_rs.at[j], peer(j)).start()
-        return carry
-
-    lax.fori_loop(0, C - 1, scatter, 0)
-    total = partial(0) + dfirst_ref[...]
+    tokens_sum = Scatter(C, peer, L, stage, recv, sc_ss, sc_rs)
+    total = tokens_sum.send(partial) + dfirst_ref[...]
+    chain_steps(0, 2)
 
     def qkv_grad(c, carry):
-        late.slot(c)
+        chain_step(2 + c)
         cols = pl.ds(pl.multiple_of(c * 2 * Dn, 128), 2 * Dn)
         res = cols_dot(hid_ref[:, :, cols].reshape(Ph, 2 * Dn), x6[...].reshape(Ph, 6 * hc))
         gq_v[c] = res.astype(BF16).reshape(2, 4, quarter, 6 * hc)
@@ -1389,7 +1501,8 @@
 
     for j in range(1, C):
         await_recv(up_o.at[block_of(j)], ua_rs.at[j], peer(j))
-    late.run(C, C + 2)
+    wide.give_out(0, 4)
+    chain_steps(C + 2, C + 4)
     await_recv(gq_r, gq_rs.at[0], partner)
     gq_s[...] = (gq_v[:, core].astype(F32) + gq_r[...].astype(F32)).astype(BF16)
     for j in range(C - 1, 0, -1):
@@ -1398,19 +1511,32 @@
         ).start()
     gq_o[mine] = gq_s[chip]
 
-    for j in range(1, C):
-        await_recv(recv.at[j], sc_rs.at[j], peer(j))
-        total = total + recv[j].astype(F32)
+    total = tokens_sum.collect(total)
     ginp = total.astype(BF16)
     ginp_ref[...] = ginp
     dhb[...] = ginp
     keep = pltpu.make_async_copy(dhb, dh_ref.at[z, s], loc.at[0])
     keep.start()
 
+    def gather_of(at):
+        return Gather(
+            C, chip, peer, L, lambda c: dh_ref.at[at, 2 * c + core], ag_ss.at[at], ag_rs.at[at]
+        )
+
     def broadcast(src, at):
-        for j in range(C - 1, 0, -1):
-            remote(src, dh_ref.at[at, s], ag_ss.at[at, j], ag_rs.at[at, j], peer(j)).start()
+        gather_of(at).send(src)
         remote(src, dh_ref.at[at, s], pf_ss.at[at, 0], pf_rs.at[at, 0], partner).start()
+
+    def pass_on(d):
+        @pl.when(z - d >= 0)
+        def _():
+            gather_of(z - d).relay()
+
+        if d:
+
+            @pl.when(z + d <= S - 1)
+            def _():
+                gather_of(z + d).relay()
 
     @pl.when(z < S - 1)
     def _():
@@ -1421,9 +1547,8 @@
         remote(dhb, dh_ref.at[z, s], zl_ss.at[z, 1], zl_rs.at[z, 1], (z - 1, s)).start()
 
     broadcast(dhb, z)
-    wide.give_out(0, wide.pieces)
-    late.run(C + 2, late.slots)
-    square.run(0, square.slots)
+    wide.give_out(4, wide.pieces)
+    chain_steps(C + 4, C + 7)
     for d in range(1, S):
 
         @pl.when(z - d >= 0)
@@ -1456,24 +1581,25 @@
             for j in range(1, C):
                 await_recv(gq_o.at[block_of(j)], gx_rs.at[j], peer(j))
             inner.give_out(0, inner.pieces)
-        wide.run(3 * (d - 1), 3 * d)
+        pass_on(d - 1)
+        chain_steps(C + 3 + 4 * d, C + 7 + 4 * d)
 
     def relay(at):
         for j in range(1, C):
             src = 2 * flip(chip, j, C) + core
-            await_recv(dh_ref.at[at, src], ag_rs.at[at, j], (z, src))
+            gather_of(at).arrived(j)
             remote(
                 dh_ref.at[at, src], dh_ref.at[at, src], pf_ss.at[at, j], pf_rs.at[at, j], partner
             ).start()
 
-    seen = 3 * (S - 1)
+    pass_on(S - 1)
+    seen = C + 3 + 4 * S
 
     def plane_sum(t, carry):
         at = flip(z, t, S)
+        chain_step(seen + 6 * t)
         relay(at)
-
-        wide.run(seen + 5 * t, seen + 5 * t + 5)
-        inner.run(6 * (t - 2), 6 * (t - 1))
+        chain_step(seen + 6 * t + 1)
 
         for j in range(C):
             src = 2 * flip(chip, j, C) + other
@@ -1487,14 +1613,15 @@
         load.start()
         load.wait()
 
-        def rows_tile(r, inner):
+        def rows_tile(r, carry):
+            chain_step(seen + 6 * t + 2 + r)
             start = pl.multiple_of(r * rt, rt)
             ids = lax.broadcasted_iota(jnp.int32, (rt, L), 0) + (start + s * R)
             hot = jnp.concatenate(
                 [jnp.where(ids == pos_ref[at, i], 1.0, 0.0).astype(BF16) for i in range(n)], axis=1
             )
             prod[at, pl.ds(start, rt), :] = rows_dot(hot, plane[...].reshape(n * L, D))
-            return inner
+            return carry
 
         lax.fori_loop(0, R // rt, rows_tile, 0)
         return carry
@@ -1511,8 +1638,7 @@
 
     lax.fori_loop(0, R // rt, add_tile, 0)
 
-    wide.run(seen + 5 * S, wide.slots)
-    inner.run(6 * (S - 2), inner.slots)
+    chain_steps(seen + 6 * S, last_step)
     for d in range(1, S):
         src = lax.rem(z + S - d, S)
         await_recv(zst.at[src], zs_rs.at[d, 0], (src, s))
@@ -1527,8 +1653,7 @@
     def settle_plane(at, carry):
         for j in range(C):
             await_send(dhb, pf_ss.at[at, j], partner)
-            if j > 0:
-                await_send(dhb, ag_ss.at[at, j], peer(j))
+        gather_of(at).settle()
         return carry
 
     lax.fori_loop(0, S, settle_plane, 0)
@@ -1553,8 +1678,6 @@
             await_send(zr.at[0, 0], zk_ss.at[j, 1], (z + 1, s))
 
         await_send(got3.at[0], x_ss.at[j], partner)
-        if j > 0:
-            await_send(stage.at[j], sc_ss.at[j], peer(j))
     for d in range(1, n):
         await_send(st_r.at[s], st_ss.at[d], (z, flip(s, d, n)))
     for d in range(1, S):
@@ -1564,6 +1687,7 @@
     for j in range(1, C):
         await_send(gq_s.at[chip], gx_ss.at[j], peer(j))
         await_send(gupc_ref.at[chip], ua_ss.at[j], peer(j))
+    tokens_sum.settle()
     wide.settle()
     square.settle()
     late.settle()
@@ -1631,8 +1755,8 @@
             dma((C, 2)),
             dma((C,)),
             dma((C,)),
-            dma((C,)),
-            dma((C,)),
+            dma((C, 2)),
+            dma((C, 2)),
             dma((n,)),
             dma((n,)),
             dma((S, 2)),
@@ -1649,8 +1773,8 @@
             dma((6, gdnc.shape[0])),
             dma((S, 2)),
             dma((S, 2)),
-            dma((S, C)),
-            dma((S, C)),
+            dma((S, C, 2)),
+            dma((S, C, 2)),
             dma((S, C)),
             dma((S, C)),
             dma((2,)),

time: 306 us -> 279 us (0.912)
  Pallas kernels: 299 us -> 272 us
    pallas_call x1, Pallas kernels: 94.3 us -> 78.1 us  [middle_call(): pl.pallas_call(functools.partial(middle_kernel, dims), out_shape=(sds((L,...]
    pallas_call x1, Pallas kernels: 125 us -> 117 us  [exit_call(): pl.pallas_call(functools.partial(exit_kernel, dims), out_shape=(sds((L, D...]
    pallas_call x1, Pallas kernels: 57.3 us -> 52.3 us  [entry_call(): pl.pallas_call(functools.partial(entry_kernel, dims), out_shape=(sds((C,...]
where the time goes in v4:
time: 279 us; the launch traced here: 278 us
  Pallas kernels  272 us (97%)
  local copies, waits for them, and re-layouts  5.14 us (2%)
    pallas_call x1, Pallas kernels, exit_call(): pl.pallas_call(functools.partial(exit_kernel, dims), out_shape=(sds((L, D...  117 us
    pallas_call x1, Pallas kernels, middle_call(): pl.pallas_call(functools.partial(middle_kernel, dims), out_shape=(sds((L,...  78.1 us
    pallas_call x1, Pallas kernels, entry_call(): pl.pallas_call(functools.partial(entry_kernel, dims), out_shape=(sds((C,...  52.3 us
    pallas_call x1, Pallas kernels, attend_back_call(): pl.pallas_call(functools.partial(attend_back_kernel, (P_, hc, hh, bq, bk)...  11.7 us
    pallas_call x1, Pallas kernels, attend_call(): pl.pallas_call(functools.partial(attend_kernel, (P_, hc, hh, bq, bk)), ou...  7.66 us

profile of v4, /device:TPU:0, one launch (start us, length us, event | category | flops | bytes accessed | tf_op | source)
XLA Modules:
  0.0 277.6 jit_solution(6022547848667681295)
XLA Ops:
  0.6 1.3 reshape.94.bup_in_hbm
  1.9 0.0 copy-start.5
  1.9 0.0 copy-start.6
  1.9 52.3 %entry_stage.1 = (bf16[4,2,128,128]{3,2,1,0:T(8,128)(2,1)S(1)}, bf16[3,4,2,128,256]{4,3,2,1,0:T(8,128)(2,1)S(1)}, bf16[4,128,1024]{2,1,0:T(8,128)(2,1)S(1)}, f32...) custom-call(s32[1,128]{1,0:T(1,128)} %bitcast.40, ...), custom_call_target="tpu_custom_call" | custom-call | tf_op jit(solution)/shard_map/entry_stage/pallas_call | solution.py:656
  54.2 0.0 copy-start.2
  54.2 1.1 copy-done.2
  55.3 0.0 copy-start
  55.4 7.7 %attend_stage.1 = (bf16[1024,128]{1,0:T(8,128)(2,1)S(1)}, f32[2,1024]{1,0:T(2,128)S(1)}) custom-call(bf16[1024,128]{1,0:T(8,128)(2,1)S(1)} %bitcast.32, bf16[3072,256]{1,0:T(8,128)(2,1)S(1)} %bitcast.28, f32[2,1024]{1,0:T(2,128)S(1)} %get-tuple-element.67.lohi_ref), custom_call_target="tpu_custom_call" | custom-call | tf_op jit(solution)/shard_map/attend_stage/pallas_call | solution.py:795
  63.0 0.0 copy-done.5
  63.0 0.0 copy-done.6
  63.0 0.0 copy-done
  63.0 78.1 %middle_stage.1 = (bf16[128,1024]{1,0:T(8,128)(2,1)S(1)}, f32[128,1024]{1,0:T(8,128)S(1)}, bf16[4,2,128,128]{3,2,1,0:T(8,128)(2,1)S(1)}, bf16[8,32,1024]{2,1,0:T...) custom-call(bf16[4,2,128,128]{3,2,1,0:T(8,128)(2,1)S(1)} %bitcast.34, ...), custom_call_target="tpu_custom_call" | custom-call | tf_op jit(solution)/shard_map/middle_stage/pallas_call | solution.py:1220
  141.2 0.0 copy-start.4
  141.2 11.7 %attend_back_stage.1 = (bf16[1024,128]{1,0:T(8,128)(2,1)S(1)}, bf16[3072,256]{1,0:T(8,128)(2,1)S(1)}) custom-call(bf16[1024,128]{1,0:T(8,128)(2,1)S(1)} %bitcast.33, bf16[3072,256]{1,0:T(8,128)(2,1)S(1)} %bitcast.29, f32[2,1024]{1,0:T(2,128)S(1)} %get-tuple-element.67.lohi_ref, bf16[1024,128]{1,0:T(8,128)(2,1)S(1)} %get-tuple-element.68.att_ref, ...), custom_call_target="tpu_custom_call" | custom-call | tf_op jit(solution)/shard_map/attend_back_stage/pallas_call | solution.py:876
  152.9 0.0 copy-done.4
  153.0 0.0 copy-start.3
  153.0 1.1 copy-done.3
  154.1 116.6 %exit_stage.1 = (bf16[128,1024]{1,0:T(8,128)(2,1)S(1)}, bf16[4,8,128,1024]{3,2,1,0:T(8,128)(2,1)}, bf16[16,32,768]{2,1,0:T(8,128)(2,1)S(1)}, bf16[16,32,1024]{2,...) custom-call(bf16[4,2,128,128]{3,2,1,0:T(8,128)(2,1)S(1)} %bitcast.37, ...), custom_call_target="tpu_custom_call" | custom-call | tf_op jit(solution)/shard_map/exit_stage/pallas_call | solution.py:1710
  270.7 0.0 copy-start.1
  270.7 1.6 copy-done.1
  272.3 5.2 %finish_stage.1 = (f32[1024,1024]{1,0:T(8,128)}, f32[128,3072]{1,0:T(8,128)}, f32[128,4096]{1,0:T(8,128)}, f32[128,1024]{1,0:T(8,128)}, f32[512,1024]{1,0:T(8,12...) custom-call(bf16[1024,1024]{1,0:T(8,128)(2,1)S(1)} %copy-done.1, ...), custom_call_target="tpu_custom_call" | custom-call | tf_op jit(solution)/shard_map/finish_stage/pallas_call | solution.py:1847
Async XLA Ops:
  1.9 61.1 %copy-start.5 = (bf16[128,1024]{1,0:T(8,128)(2,1)S(1)}, bf16[128,1024]{1,0:T(8,128)(2,1)}, u32[]{:S(2)}) copy-start(bf16[128,1024]{1,0:T(8,128)(2,1)} %wout_ref.3) | copy-start | bytes 786436
  1.9 61.1 %copy-start.6 = (bf16[128,1024]{1,0:T(8,128)(2,1)S(1)}, bf16[128,1024]{1,0:T(8,128)(2,1)}, u32[]{:S(2)}) copy-start(bf16[128,1024]{1,0:T(8,128)(2,1)} %cot_ref.1) | copy-start | bytes 786436
  54.2 1.1 copy-start.2
  55.3 7.7 %copy-start = (bf16[512,1024]{1,0:T(8,128)(2,1)S(1)}, bf16[512,1024]{1,0:T(8,128)(2,1)}, u32[]{:S(2)}) copy-start(bf16[512,1024]{1,0:T(8,128)(2,1)} %wdn_ref.3) | copy-start | bytes 3145732
  141.2 11.8 %copy-start.4 = (bf16[4,128,1024]{2,1,0:T(8,128)(2,1)}, bf16[4,128,1024]{2,1,0:T(8,128)(2,1)S(1)}, u32[]{:S(2)}) copy-start(bf16[4,128,1024]{2,1,0:T(8,128)(2,1)S(1)} %get-tuple-element.85) | copy-start | bytes 3145732
  153.0 1.1 copy-start.3
  270.7 1.6 copy-start.1

commit v5 on v4

--- a/solution.py
+++ b/solution.py
@@ -19,7 +19,7 @@
 F32 = jnp.float32
 BF16 = jnp.bfloat16
 MIB = 1024 * 1024
-ENTRY_VMEM, ATTEND_VMEM, MIDDLE_VMEM, BACK_VMEM, EXIT_VMEM = 24, 16, 44, 20, 48
+ENTRY_VMEM, ATTEND_VMEM, MIDDLE_VMEM, BACK_VMEM, EXIT_VMEM = 24, 16, 40, 20, 42
 
 
 def flip(value, mask, width):
@@ -52,7 +52,7 @@
 
 
 class Chain:
-    def __init__(self, S, z, s, own, land, cross, fin, sems, lag=3):
+    def __init__(self, S, z, s, own, land, cross, fin, sems, lag=4):
         self.S, self.s, self.lag, self.sems = S, s, lag, sems
         self.own, self.land, self.cross, self.fin = own, land, cross, fin
         low = 1 - (2 * z) // S
@@ -1131,7 +1131,7 @@
     taken(0, None, gdn_r)
     gdn_h[...] = (gdn_v[core, :early].astype(F32) + gdn_r[:early].astype(F32)).astype(BF16)
     gdn_ref[...] = (gdn_v[core, early:].astype(F32) + gdn_r[early:].astype(F32)).astype(BF16)
-    chain = Chain(S, z, s, gdn_h, gdn_l, gdn_x, gdn_f, zsem)
+    chain = Chain(S, z, s, gdn_h, gdn_l, gdn_x, gdn_f, zsem, 2)
     chain.give_out(0, early)
 
     lax.fori_loop(0, C, up_grad, 0)
@@ -1501,7 +1501,7 @@
 
     for j in range(1, C):
         await_recv(up_o.at[block_of(j)], ua_rs.at[j], peer(j))
-    wide.give_out(0, 4)
+    wide.give_out(0, 2)
     chain_steps(C + 2, C + 4)
     await_recv(gq_r, gq_rs.at[0], partner)
     gq_s[...] = (gq_v[:, core].astype(F32) + gq_r[...].astype(F32)).astype(BF16)
@@ -1547,10 +1547,9 @@
         remote(dhb, dh_ref.at[z, s], zl_ss.at[z, 1], zl_rs.at[z, 1], (z - 1, s)).start()
 
     broadcast(dhb, z)
-    wide.give_out(4, wide.pieces)
+    wide.give_out(2, wide.pieces)
     chain_steps(C + 4, C + 7)
-    for d in range(1, S):
-
+    def next_planes(d):
         @pl.when(z - d >= 0)
         def _():
             at = z - d
@@ -1576,13 +1575,6 @@
                 ).start()
 
             broadcast(dh_ref.at[at, s], at)
-
-        if d == 2:
-            for j in range(1, C):
-                await_recv(gq_o.at[block_of(j)], gx_rs.at[j], peer(j))
-            inner.give_out(0, inner.pieces)
-        pass_on(d - 1)
-        chain_steps(C + 3 + 4 * d, C + 7 + 4 * d)
 
     def relay(at):
         for j in range(1, C):
@@ -1592,21 +1584,17 @@
                 dh_ref.at[at, src], dh_ref.at[at, src], pf_ss.at[at, j], pf_rs.at[at, j], partner
             ).start()
 
-    pass_on(S - 1)
-    seen = C + 3 + 4 * S
-
-    def plane_sum(t, carry):
+    def plane_sum(t, step):
         at = flip(z, t, S)
-        chain_step(seen + 6 * t)
+        chain_step(step)
         relay(at)
-        chain_step(seen + 6 * t + 1)
+        chain_step(step + 1)
 
         for j in range(C):
             src = 2 * flip(chip, j, C) + other
             await_recv(dh_ref.at[at, src], pf_rs.at[at, j], partner)
 
-        @pl.when(t == 0)
-        def _():
+        if t == 0:
             keep.wait()
 
         load = pltpu.make_async_copy(dh_ref.at[at], plane, loc.at[1])
@@ -1614,7 +1602,7 @@
         load.wait()
 
         def rows_tile(r, carry):
-            chain_step(seen + 6 * t + 2 + r)
+            chain_step(step + 2 + r)
             start = pl.multiple_of(r * rt, rt)
             ids = lax.broadcasted_iota(jnp.int32, (rt, L), 0) + (start + s * R)
             hot = jnp.concatenate(
@@ -1624,9 +1612,23 @@
             return carry
 
         lax.fori_loop(0, R // rt, rows_tile, 0)
-        return carry
-
-    lax.fori_loop(0, S, plane_sum, 0)
+
+    next_planes(1)
+    pass_on(0)
+    chain_steps(C + 7, C + 11)
+    step = C + 11
+    for t in range(S):
+        if t + 2 < S:
+            next_planes(t + 2)
+        if t + 1 < S:
+            pass_on(t + 1)
+        if t == 0:
+            for j in range(1, C):
+                await_recv(gq_o.at[block_of(j)], gx_rs.at[j], peer(j))
+            inner.give_out(0, inner.pieces)
+        chain_steps(step, step + 2)
+        plane_sum(t, step + 2)
+        step += 4 + R // rt
 
     def add_tile(r, carry):
         at = pl.ds(pl.multiple_of(r * rt, rt), rt)
@@ -1638,7 +1640,7 @@
 
     lax.fori_loop(0, R // rt, add_tile, 0)
 
-    chain_steps(seen + 6 * S, last_step)
+    chain_steps(step, last_step)
     for d in range(1, S):
         src = lax.rem(z + S - d, S)
         await_recv(zst.at[src], zs_rs.at[d, 0], (src, s))

time: 279 us -> 267 us (0.957)
  Pallas kernels: 272 us -> 263 us
  local copies, waits for them, and re-layouts: 5.14 us -> 1.27 us
    pallas_call x1, Pallas kernels: 117 us -> 105 us  [exit_call(): pl.pallas_call(functools.partial(exit_kernel, dims), out_shape=(sds((L, D...]
    unnamed x14 -> x6, local copies, waits for them, and re-layouts: 3.88 us -> 0.01 us
    pallas_call x1, Pallas kernels: 11.7 us -> 15.3 us  [attend_back_call(): pl.pallas_call(functools.partial(attend_back_kernel, (P_, hc, hh, bq, bk)...]
where the time goes in v5:
time: 267 us; the launch traced here: 265 us
  Pallas kernels  263 us (99%)
    pallas_call x1, Pallas kernels, exit_call(): pl.pallas_call(functools.partial(exit_kernel, dims), out_shape=(sds((L, D...  105 us
    pallas_call x1, Pallas kernels, middle_call(): pl.pallas_call(functools.partial(middle_kernel, dims), out_shape=(sds((L,...  76.1 us
    pallas_call x1, Pallas kernels, entry_call(): pl.pallas_call(functools.partial(entry_kernel, dims), out_shape=(sds((C,...  52.3 us
    pallas_call x1, Pallas kernels, attend_back_call(): pl.pallas_call(functools.partial(attend_back_kernel, (P_, hc, hh, bq, bk)...  15.3 us
    pallas_call x1, Pallas kernels, attend_call(): pl.pallas_call(functools.partial(attend_kernel, (P_, hc, hh, bq, bk)), ou...  9.08 us

profile of v5, /device:TPU:0, one launch (start us, length us, event | category | flops | bytes accessed | tf_op | source)
XLA Modules:
  0.0 265.2 jit_solution(2258812300314403313)
XLA Ops:
  0.6 1.3 reshape.94.bup_in_hbm
  1.9 0.0 copy-start.1
  1.9 0.0 copy-start.2
  1.9 52.3 %entry_stage.1 = (bf16[4,2,128,128]{3,2,1,0:T(8,128)(2,1)S(1)}, bf16[3,4,2,128,256]{4,3,2,1,0:T(8,128)(2,1)S(1)}, bf16[4,128,1024]{2,1,0:T(8,128)(2,1)S(1)}, f32...) custom-call(s32[1,128]{1,0:T(1,128)} %bitcast.40, ...), custom_call_target="tpu_custom_call" | custom-call | tf_op jit(solution)/shard_map/entry_stage/pallas_call | solution.py:656
  54.2 0.0 copy-start
  54.2 9.1 %attend_stage.1 = (bf16[1024,128]{1,0:T(8,128)(2,1)S(1)}, f32[2,1024]{1,0:T(2,128)S(1)}) custom-call(bf16[1024,128]{1,0:T(8,128)(2,1)S(1)} %bitcast.32, bf16[3072,256]{1,0:T(8,128)(2,1)S(1)} %bitcast.28, f32[2,1024]{1,0:T(2,128)S(1)} %get-tuple-element.67.lohi_ref), custom_call_target="tpu_custom_call" | custom-call | tf_op jit(solution)/shard_map/attend_stage/pallas_call | solution.py:795
  63.3 0.0 copy-done.1
  63.3 0.0 copy-done.2
  63.3 0.0 copy-done
  63.3 76.1 %middle_stage.1 = (bf16[128,1024]{1,0:T(8,128)(2,1)S(1)}, f32[128,1024]{1,0:T(8,128)S(1)}, bf16[4,2,128,128]{3,2,1,0:T(8,128)(2,1)S(1)}, bf16[8,32,1024]{2,1,0:T...) custom-call(bf16[4,2,128,128]{3,2,1,0:T(8,128)(2,1)S(1)} %bitcast.34, ...), custom_call_target="tpu_custom_call" | custom-call | tf_op jit(solution)/shard_map/middle_stage/pallas_call | solution.py:1220
  139.4 15.3 %attend_back_stage.1 = (bf16[1024,128]{1,0:T(8,128)(2,1)S(1)}, bf16[3072,256]{1,0:T(8,128)(2,1)S(1)}) custom-call(bf16[1024,128]{1,0:T(8,128)(2,1)S(1)} %bitcast.33, bf16[3072,256]{1,0:T(8,128)(2,1)S(1)} %bitcast.29, f32[2,1024]{1,0:T(2,128)S(1)} %get-tuple-element.67.lohi_ref, bf16[1024,128]{1,0:T(8,128)(2,1)S(1)} %get-tuple-element.68.att_ref, ...), custom_call_target="tpu_custom_call" | custom-call | tf_op jit(solution)/shard_map/attend_back_stage/pallas_call | solution.py:876
  154.7 105.1 %exit_stage.1 = (bf16[128,1024]{1,0:T(8,128)(2,1)S(1)}, bf16[4,8,128,1024]{3,2,1,0:T(8,128)(2,1)}, bf16[16,32,768]{2,1,0:T(8,128)(2,1)S(1)}, bf16[16,32,1024]{2,...) custom-call(bf16[4,2,128,128]{3,2,1,0:T(8,128)(2,1)S(1)} %bitcast.37, ...), custom_call_target="tpu_custom_call" | custom-call | tf_op jit(solution)/shard_map/exit_stage/pallas_call | solution.py:1712
  259.9 5.2 %finish_stage.1 = (f32[1024,1024]{1,0:T(8,128)}, f32[128,3072]{1,0:T(8,128)}, f32[128,4096]{1,0:T(8,128)}, f32[128,1024]{1,0:T(8,128)}, f32[512,1024]{1,0:T(8,12...) custom-call(bf16[1024,1024]{1,0:T(8,128)(2,1)S(1)} %get-tuple-elemen, ...), custom_call_target="tpu_custom_call" | custom-call | tf_op jit(solution)/shard_map/finish_stage/pallas_call | solution.py:1849
Async XLA Ops:
  1.9 61.4 %copy-start.1 = (bf16[128,1024]{1,0:T(8,128)(2,1)S(1)}, bf16[128,1024]{1,0:T(8,128)(2,1)}, u32[]{:S(2)}) copy-start(bf16[128,1024]{1,0:T(8,128)(2,1)} %wout_ref.3) | copy-start | bytes 786436
  1.9 61.4 %copy-start.2 = (bf16[128,1024]{1,0:T(8,128)(2,1)S(1)}, bf16[128,1024]{1,0:T(8,128)(2,1)}, u32[]{:S(2)}) copy-start(bf16[128,1024]{1,0:T(8,128)(2,1)} %cot_ref.1) | copy-start | bytes 786436
  54.2 9.1 %copy-start = (bf16[512,1024]{1,0:T(8,128)(2,1)S(1)}, bf16[512,1024]{1,0:T(8,128)(2,1)}, u32[]{:S(2)}) copy-start(bf16[512,1024]{1,0:T(8,128)(2,1)} %wdn_ref.3) | copy-start | bytes 3145732
